TPU v7x, 128 devices: a whole 4x4x4 slice. The times are simulated.
128 devices in a mesh: lat: 8 (over y, core), lon: 4 (over x), lev: 4 (over z).
Axes of the slice: x: 4, y: 4, z: 4, core: 2. Of those that a mesh axis runs over, the one named last changes fastest.
Arguments:
- tracer: float32 [32, 512, 128, 128], P('lat', 'lon', 'lev'), may hold values from 0.5 to 2
- conductance: float32 [32, 512, 128, 128], P('lat', 'lon', 'lev'), may hold values from 0.03 to 0.15
- source: float32 [32, 512, 128, 128], P('lat', 'lon', 'lev'), may hold values from -0.2 to 0.2
Outputs:
- standardized: float32 [32, 512, 128, 128], P('lat', 'lon', 'lev')
- tracer_end: float32 [32, 512, 128, 128], P('lat', 'lon', 'lev')
All inputs are finite; a program needn't handle non-finite values.
Results may differ from a plain program's by a relative error of at most 0.00002.
Values sent between devices are 32-bit elements; how exact they have to be, the bound alone decides.
No kernel may reach another device: no remote copies, remote signals or barrier semaphores. Data moves between devices by JAX's collectives and lax.ppermute only.
A program may use at most 128 MiB of HBM per device.

v0:
```python
import jax
import jax.numpy as jnp
from jax import lax
from jax.experimental import pallas as pl
from jax.experimental.pallas import tpu as pltpu
from jax.sharding import PartitionSpec as P


STEPS = 3
F32 = jnp.float32
VMEM = pltpu.MemorySpace.VMEM
HBM = pltpu.MemorySpace.HBM
NJ, NI, NK, NM = 4, 128, 32, 128
HALF = NI // 2
PLANE = (NI, NK, NM)
HALF_PLANE = (HALF, NK, NM)
FACES = ((NJ, NK, NM),) * 2 + ((NJ, NI, NM),) * 2
UNROLL = 8


def call(kernel, args, outs, scratch=(), aliases=None, limit=4 << 20):
    arrays, in_specs = [], []
    for array, space in args:
        in_specs.append(pl.BlockSpec(memory_space=pl.ANY if space is HBM else space))
        arrays.append(pltpu.with_memory_space_constraint(array, space))
    return pl.pallas_call(
        kernel,
        out_shape=tuple(space(shape, F32) for shape, space in outs),
        in_specs=in_specs,
        out_specs=tuple(pl.BlockSpec(memory_space=pl.ANY if space is HBM else space) for _, space in outs),
        scratch_shapes=list(scratch),
        input_output_aliases=aliases or {},
        compiler_params=pltpu.CompilerParams(vmem_limit_bytes=limit),
    )(*arrays)


def row_of(p):
    odd = lax.rem(lax.axis_index("lat"), 2)
    return odd * p + (1 - odd) * (NJ - 1 - p)


def start(src, dst, sem):
    copy = pltpu.make_async_copy(src, dst, sem)
    copy.start()
    return copy


def messages(tracer, x3a, x3b, x0, lon_low, lon_high, lev_low, lev_high, sems):
    pairs = [
        (tracer.at[row_of(3), pl.ds(0, HALF)], x3a),
        (tracer.at[row_of(3), pl.ds(HALF, HALF)], x3b),
        (tracer.at[row_of(0)], x0),
    ]
    for p in range(NJ):
        j = row_of(p)
        pairs += [
            (tracer.at[j, :, 0, :], lev_low.at[p]),
            (tracer.at[j, :, NK - 1, :], lev_high.at[p]),
            (tracer.at[j, 0], lon_low.at[p]),
            (tracer.at[j, NI - 1], lon_high.at[p]),
        ]
    copies = [start(src, dst, sems.at[n]) for n, (src, dst) in enumerate(pairs)]
    for copy in copies:
        copy.wait()


def load_edge(tracer, c, s, x2, c3, s3, sems):
    pairs = [(tracer.at[row_of(2)], x2), (c.at[row_of(3)], c3), (s.at[row_of(3)], s3)]
    copies = [start(src, dst, sems.at[n]) for n, (src, dst) in enumerate(pairs)]
    for copy in copies:
        copy.wait()


def advance(x, before, after, below, above, lev_low, lev_high, c, s, out, lev_outs=None, sums=None):
    def at(view, i, size=None):
        ref, first = view
        return ref[first + i] if size is None else ref[pl.ds(pl.multiple_of(first + i, UNROLL), size), :]

    def block(b, carry):
        i0 = b * UNROLL
        low, high = (at(lev_low, i0, UNROLL), at(lev_high, i0, UNROLL))
        prev = jnp.where(b == 0, before, at(x, jnp.maximum(i0 - 1, 0)))
        here = at(x, i0)
        for r in range(UNROLL):
            if r < UNROLL - 1:
                nxt = at(x, i0 + r + 1)
            else:
                nxt = jnp.where(b == HALF // UNROLL - 1, after, at(x, jnp.minimum(i0 + UNROLL, HALF - 1)))
            down = jnp.concatenate([low[r : r + 1], here[: NK - 1]], axis=0)
            up = jnp.concatenate([here[1:], high[r : r + 1]], axis=0)
            spread = (prev + nxt) + (at(below, i0 + r) + at(above, i0 + r)) + (down + up) - 6.0 * here
            new = here + at(c, i0 + r) * spread + at(s, i0 + r)
            out[0][out[1] + i0 + r] = new
            if lev_outs is not None:
                for (ref, first), k in zip(lev_outs, (0, NK - 1)):
                    ref[pl.ds(first + i0 + r, 1), :] = new[k : k + 1]
            if sums is not None:
                shift, total, squares = carry
                if r == 0 and sums[0] is None:
                    shift = jnp.where(b == 0, new, shift)
                moved = new - shift
                carry = (shift, total + moved, squares + moved * moved)
            prev, here = here, nxt
        return carry

    if sums is None:
        first = 0
    else:
        first = (jnp.zeros((NK, NM), F32) if sums[0] is None else sums[0], *sums[1:])
    return lax.fori_loop(0, HALF // UNROLL, block, first)


def put_stats(stats, p, sums):
    shift, total, squares = sums
    mean, square = (shift + total * (1.0 / NI), squares - total * (total * (1.0 / NI)))
    for d in range(stats.shape[0]):
        stats[d, 0, p] = mean
        stats[d, 1, p] = square


def no_sums():
    zero = jnp.zeros((NK, NM), F32)
    return (None, zero, zero)


def inner_planes(xs, on, halo, cs, outs, faces=None, stats=None, ready=lambda p: None, done=lambda p: None):
    lon_low, lon_high, lev_low, lev_high = halo
    for p in (2, 1, 0):
        ready(p)
        x, out = xs[p], outs[p]
        sums = no_sums() if stats is not None else None
        for h in (0, 1):
            first = h * HALF
            below = (on, first) if p == 0 else (xs[p - 1], first)
            above = (xs[3 + h], 0) if p == 2 else (xs[p + 1], first)
            before = x[HALF - 1] if h else lon_low[p]
            after = lon_high[p] if h else x[HALF]
            sums = advance(
                (x, first), before, after, below, above, (lev_low.at[p], first), (lev_high.at[p], first),
                (cs[p][0], first), (cs[p][1], first), (out, first),
                None if faces is None else ((faces[2].at[p], first), (faces[3].at[p], first)),
                sums if stats is not None else None,
            )
        if faces is not None:
            faces[0][p] = out[0]
            faces[1][p] = out[NI - 1]
        if stats is not None:
            put_stats(stats, p, sums)
        done(p)


def edge_half(h, x2, x3, cross, halo, c3, s3, out, faces=None, sums=None):
    lon_low, lon_high, lev_low, lev_high = halo
    p, first = 3, h * HALF
    sums = advance(
        (x3[h], 0), x3[0][HALF - 1] if h else lon_low[p], lon_high[p] if h else x3[1][0],
        (x2, first), (cross, 0), (lev_low.at[p], first), (lev_high.at[p], first), (c3, first), (s3, first), (out, 0),
        None if faces is None else ((faces[2].at[p], first), (faces[3].at[p], first)), sums,
    )
    if faces is not None:
        if h:
            faces[1][p] = out[HALF - 1]
        else:
            faces[0][p] = out[0]
    return sums


def edge_a(x2, x3a, x3b, cross, ll, lh, vl, vh, c3, s3, out, *faces):
    edge_half(0, x2, (x3a, x3b), cross, (ll, lh, vl, vh), c3, s3, out, faces)


def edge_b(x2, x3a, x3b, cross, ll, lh, vl, vh, c3, s3, a0, a1, a2, a3, out, *faces):
    edge_half(1, x2, (x3a, x3b), cross, (ll, lh, vl, vh), c3, s3, out, faces)


def edge_a_last(x2, x3a, x3b, cross, ll, lh, vl, vh, c3, s3, out, raw):
    sums = edge_half(0, x2, (x3a, x3b), cross, (ll, lh, vl, vh), c3, s3, out, None, no_sums())
    for n in range(3):
        raw[n] = sums[n]


def edge_b_last(x2, x3a, x3b, cross, ll, lh, vl, vh, c3, s3, raw, a0, out, stats):
    sums = (raw[0], raw[1], raw[2])
    put_stats(stats, 3, edge_half(1, x2, (x3a, x3b), cross, (ll, lh, vl, vh), c3, s3, out, None, sums))


def inner_first(
    tracer, c, s, x0, x2, x3a, x3b, on, ll, lh, vl, vh, a0, a1, a2, a3, q0, q1, q2, f0, f1, f2, f3, cc, ss, x1, sems
):
    loads = [[start(tracer.at[row_of(1)], x1, sems.at[6])], [], []]
    for p in (2, 1, 0):
        loads[p] += [start(c.at[row_of(p)], cc.at[p], sems.at[p]), start(s.at[row_of(p)], ss.at[p], sems.at[3 + p])]
    loads[2] += loads[0][:1]
    loads[0] = loads[0][1:]

    def ready(p):
        for copy in loads[p]:
            copy.wait()

    inner_planes(
        (x0, x1, x2, x3a, x3b), on, (ll, lh, vl, vh), [(cc.at[p], ss.at[p]) for p in range(3)], (q0, q1, q2),
        (f0, f1, f2, f3), ready=ready,
    )


def inner(x0, x1, x2, x3a, x3b, on, ll, lh, vl, vh, cc, ss, a0, a1, a2, a3, q0, q1, q2, *faces):
    inner_planes(
        (x0, x1, x2, x3a, x3b), on, (ll, lh, vl, vh), [(cc.at[p], ss.at[p]) for p in range(3)], (q0, q1, q2), faces
    )


def inner_last(x0, x1, x2, x3a, x3b, on, ll, lh, vl, vh, cc, ss, raw, q0, q1, q2, stats, end, sems):
    outs, copies = ((q0, q1, q2), [])
    inner_planes(
        (x0, x1, x2, x3a, x3b), on, (ll, lh, vl, vh), [(cc.at[p], ss.at[p]) for p in range(3)], outs, None, stats,
        done=lambda p: copies.append(start(outs[p], end.at[row_of(p)], sems.at[p])),
    )
    for copy in copies:
        copy.wait()


def scaled(q0, q1, q2, q3a, q3b, stats, a0, out, end, buffers, sems):
    parts = stats.shape[0]
    last = [start(q, end.at[row_of(3), pl.ds(h * HALF, HALF)], sems.at[NJ + h]) for h, q in enumerate((q3a, q3b))]
    copies = []
    for p in range(NJ):
        means = [stats[d, 0, p] for d in range(parts)]
        mean = sum(means[1:], means[0]) * (1.0 / parts)
        square = sum([stats[d, 1, p] for d in range(1, parts)], stats[0, 1, p])
        for m in means:
            square = square + NI * ((m - mean) * (m - mean))
        scale = lax.rsqrt(square * (1.0 / (parts * NI)) + 0.0001)
        slot = p % 2
        if p >= 2:
            copies[p - 2].wait()
        for first, q in ((0, (q0, q1, q2)[p]),) if p < 3 else ((0, q3a), (HALF, q3b)):

            def block(b, _, first=first, q=q):
                i0 = b * UNROLL
                for r in range(UNROLL):
                    buffers[slot, first + i0 + r] = (q[i0 + r] - mean) * scale
                return 0

            lax.fori_loop(0, q.shape[0] // UNROLL, block, 0)
        copies.append(start(buffers.at[slot], out.at[row_of(p)], sems.at[p]))
    for copy in (*copies[2:], *last):
        copy.wait()


def shards(tracer, c, s):
    lats, lons = (lax.axis_size(a) for a in ("lat", "lon"))
    on_pairs = [(i, i ^ 1) for i in range(lats)]
    cross_pairs = [(i, ((i + 1) ^ 1) - 1) for i in range(lats) if 0 <= ((i + 1) ^ 1) - 1 < lats]

    def to_next(array, axis):
        return lax.ppermute(array, axis, [(i, i + 1) for i in range(lax.axis_size(axis) - 1)])

    def to_previous(array, axis):
        return lax.ppermute(array, axis, [(i + 1, i) for i in range(lax.axis_size(axis) - 1)])

    def exchanged(faces):
        lon_low, lon_high, lev_low, lev_high = faces
        lev = (to_next(lev_high, "lev"), to_previous(lev_low, "lev"))
        return [to_next(lon_high, "lon"), to_previous(lon_low, "lon"), *lev]

    def swapped(q, pairs):
        return lax.ppermute(q, "lat", pairs)

    vm = lambda *arrays: [(a, VMEM) for a in arrays]
    dma = pltpu.SemaphoreType.DMA
    half, plane, face_outs = ((HALF_PLANE, VMEM), (PLANE, VMEM), [(f, VMEM) for f in FACES])
    inner_fields = ((3, *PLANE), VMEM)

    x3a, x3b, x0, *faces = call(
        messages, [(tracer, HBM)], [half, half, plane] + face_outs, scratch=[dma((3 + 4 * NJ,))]
    )
    cross = [swapped(x3a, cross_pairs), swapped(x3b, cross_pairs)]
    on = swapped(x0, on_pairs)
    halo = exchanged(faces)
    x2, c3, s3 = call(load_edge, [(a, HBM) for a in (tracer, c, s)], [plane] * 3, scratch=[dma((3,))])

    for step in range(STEPS):
        edge = vm(x2, x3a, x3b)
        rest = vm(*halo, c3, s3)
        if step < STEPS - 1:
            qa, *faces = call(edge_a, edge + vm(cross[0]) + rest, [half] + face_outs)
            cross[0] = swapped(qa, cross_pairs)
            outs = [plane] * 3 + face_outs
            if step == 0:
                q0, q1, q2, *faces, cc, ss = call(
                    inner_first,
                    [(a, HBM) for a in (tracer, c, s)] + vm(x0, x2, x3a, x3b, on, *halo, *faces),
                    outs + [inner_fields] * 2, scratch=[pltpu.VMEM(PLANE, F32), dma((7,))],
                    aliases={12 + n: 3 + n for n in range(4)}, limit=6 << 20,
                )
            else:
                q0, q1, q2, *faces = call(
                    inner, vm(x0, x1, x2, x3a, x3b, on, *halo, cc, ss, *faces), outs,
                    aliases={12 + n: 3 + n for n in range(4)},
                )
            on = swapped(q0, on_pairs)
            qb, *faces = call(
                edge_b, edge + vm(cross[1]) + rest + vm(*faces), [half] + face_outs,
                aliases={10 + n: 1 + n for n in range(4)},
            )
            cross[1] = swapped(qb, cross_pairs)
            halo = exchanged(faces)
        else:
            qa, raw = call(edge_a_last, edge + vm(cross[0]) + rest, [half, ((3, NK, NM), VMEM)])
            all_stats = ((lons, 2, NJ, NK, NM), VMEM)
            q0, q1, q2, stats, end = call(
                inner_last, vm(x0, x1, x2, x3a, x3b, on, *halo, cc, ss, raw),
                [plane] * 3 + [all_stats, ((NJ, *PLANE), HBM)], scratch=[dma((3,))],
            )
            qb, stats = call(
                edge_b_last, edge + vm(cross[1]) + rest + vm(raw, stats), [half, all_stats],
                aliases={11: 1},
            )
        x0, x1, x2, x3a, x3b = q0, q1, q2, qa, qb

    everyone = lax.all_to_all(stats, "lon", 0, 0, tiled=True)
    out, end = call(
        scaled, vm(x0, x1, x2, x3a, x3b, everyone) + [(end, HBM)], [((NJ, *PLANE), HBM)] * 2,
        scratch=[pltpu.VMEM((2, *PLANE), F32), dma((NJ + 2,))], aliases={6: 1}, limit=8 << 20,
    )
    return out, end


def solution(mesh):
    placed = P("lat", "lon", "lev", None)

    return jax.shard_map(
        shards, mesh=mesh, in_specs=(placed, placed, placed), out_specs=(placed, placed), check_vma=False
    )
```

profile of v0, /device:TPU:40, one launch (start us, length us, event | category | flops | bytes accessed | tf_op | source)
XLA Modules:
  0.0 125.6 jit_solution(9442556013878725599)
XLA Ops:
  0.6 2.5 %shard_map.50 = (f32[64,32,128]{2,1,0:T(8,128)S(1)}, f32[64,32,128]{2,1,0:T(8,128)S(1)}, f32[128,32,128]{2,1,0:T(8,128)S(1)}, f32[4,32,128]{2,1,0:T(8,128)S(1)},...) custom-call(f32[4,128,32,128]{3,2,1,0:T(8,128)} %tracer.5), custom_call_target="tpu_custom_call" | custom-call | tf_op jit(solution)/shard_map/pallas_call | solution.py:26
  3.2 0.1 collective-permute-start
  3.3 2.4 %collective-permute-start.5 = (f32[64,32,128]{2,1,0:T(8,128)S(1)}, f32[64,32,128]{2,1,0:T(8,128)S(1)}, u32[]{:S(2)}, u32[]{:S(2)}) collective-permute-start(f32[64,32,128]{2,1,0:T(8,128)S(1)} %get-tuple-element.59.x3a), channel_id=1, source_target_pairs={{16,32},{32,16},{48,64},{64,48},{80,96},{96,80},{17,33},{33,17},{4... | collective-permute-start | bytes 3145736 | tf_op jit(solution)/shard_map/ppermute | solution.py:267
  5.7 3.8 %collective-permute-start.3 = (f32[4,128,128]{2,1,0:T(8,128)S(1)}, f32[4,128,128]{2,1,0:T(8,128)S(1)}, u32[]{:S(2)}, u32[]{:S(2)}) collective-permute-start(f32[4,128,128]{2,1,0:T(8,128)S(1)} %get-tuple-element.63), channel_id=1, source_target_pairs={{0,1},{1,2},{2,3},{4,5},{5,6},{6,7},{8,9},{9,10},{10,11},{12,13},{... | collective-permute-start | bytes 786440 | tf_op jit(solution)/shard_map/ppermute | solution.py:256
  9.6 2.0 %collective-permute-start.4 = (f32[4,128,128]{2,1,0:T(8,128)S(1)}, f32[4,128,128]{2,1,0:T(8,128)S(1)}, u32[]{:S(2)}, u32[]{:S(2)}) collective-permute-start(f32[4,128,128]{2,1,0:T(8,128)S(1)} %get-tuple-element.64), channel_id=1, source_target_pairs={{1,0},{2,1},{3,2},{5,4},{6,5},{7,6},{9,8},{10,9},{11,10},{13,12},{... | collective-permute-start | bytes 786440 | tf_op jit(solution)/shard_map/ppermute | solution.py:259
  11.6 3.4 %collective-permute-start.1 = (f32[4,32,128]{2,1,0:T(8,128)S(1)}, f32[4,32,128]{2,1,0:T(8,128)S(1)}, u32[]{:S(2)}, u32[]{:S(2)}) collective-permute-start(f32[4,32,128]{2,1,0:T(8,128)S(1)} %get-tuple-element.61), channel_id=1, source_target_pairs={{0,4},{4,8},{8,12},{1,5},{5,9},{9,13},{2,6},{6,10},{10,14},{3,7},{... | collective-permute-start | bytes 196616 | tf_op jit(solution)/shard_map/ppermute | solution.py:256
  15.0 2.3 %collective-permute-done.1.ll = f32[4,32,128]{2,1,0:T(8,128)S(1)} collective-permute-done((f32[4,32,128]{2,1,0:T(8,128)S(1)}, f32[4,32,128]{2,1,0:T(8,128)S(1)}, u32[]{:S(2)}, u32[]{:S(2)}) %collective-permute-start.1) | collective-permute-done | bytes 65568 | tf_op jit(solution)/shard_map/ppermute | solution.py:256
  17.3 1.3 %collective-permute-start.2 = (f32[4,32,128]{2,1,0:T(8,128)S(1)}, f32[4,32,128]{2,1,0:T(8,128)S(1)}, u32[]{:S(2)}, u32[]{:S(2)}) collective-permute-start(f32[4,32,128]{2,1,0:T(8,128)S(1)} %get-tuple-element.62), channel_id=1, source_target_pairs={{4,0},{8,4},{12,8},{5,1},{9,5},{13,9},{6,2},{10,6},{14,10},{7,3},{... | collective-permute-start | bytes 196616 | tf_op jit(solution)/shard_map/ppermute | solution.py:259
  18.5 2.9 %shard_map.51 = (f32[128,32,128]{2,1,0:T(8,128)S(1)}, f32[128,32,128]{2,1,0:T(8,128)S(1)}, f32[128,32,128]{2,1,0:T(8,128)S(1)}) custom-call(f32[4,128,32,128]{3,2,1,0:T(8,128)} %tracer.5, f32[4,128,32,128]{3,2,1,0:T(8,128)} %c.3, f32[4,128,32,128]{3,2,1,0:T(8,128)} %s.3), custom_call_target="tpu_custom_call" | custom-call | tf_op jit(solution)/shard_map/pallas_call | solution.py:26
  21.5 2.4 %collective-permute-done.2.lh = f32[4,32,128]{2,1,0:T(8,128)S(1)} collective-permute-done((f32[4,32,128]{2,1,0:T(8,128)S(1)}, f32[4,32,128]{2,1,0:T(8,128)S(1)}, u32[]{:S(2)}, u32[]{:S(2)}) %collective-permute-start.2) | collective-permute-done | bytes 65568 | tf_op jit(solution)/shard_map/ppermute | solution.py:259
  23.9 0.0 collective-permute-done.3.vl
  23.9 0.0 collective-permute-done.4.vh
  23.9 0.0 collective-permute-done.5.cross
  23.9 0.6 shard_map.52
  24.5 0.0 collective-permute-done.on
  24.5 6.5 %shard_map.53 = (f32[128,32,128]{2,1,0:T(8,128)S(1)}, f32[128,32,128]{2,1,0:T(8,128)S(1)}, f32[128,32,128]{2,1,0:T(8,128)S(1)}, f32[4,32,128]{2,1,0:T(8,128)S(1)...) custom-call(f32[4,128,32,128]{3,2,1,0:T(8,128)} %tracer.5, ...), custom_call_target="tpu_custom_call", output_to_operand_aliasing={{3}: (12, {}), {4}: (13, {}), {5}: (14, {}), {6}: (15, {})} | custom-call | tf_op jit(solution)/shard_map/pallas_call | solution.py:26
  31.0 0.1 collective-permute-start.7
  31.1 1.9 %collective-permute-start.6 = (f32[64,32,128]{2,1,0:T(8,128)S(1)}, f32[64,32,128]{2,1,0:T(8,128)S(1)}, u32[]{:S(2)}, u32[]{:S(2)}) collective-permute-start(f32[64,32,128]{2,1,0:T(8,128)S(1)} %get-tuple-element.60.x3b), channel_id=1, source_target_pairs={{16,32},{32,16},{48,64},{64,48},{80,96},{96,80},{17,33},{33,17},{4... | collective-permute-start | bytes 3145736 | tf_op jit(solution)/shard_map/ppermute | solution.py:267
  33.0 3.6 %collective-permute-start.12 = (f32[64,32,128]{2,1,0:T(8,128)S(1)}, f32[64,32,128]{2,1,0:T(8,128)S(1)}, u32[]{:S(2)}, u32[]{:S(2)}) collective-permute-start(f32[64,32,128]{2,1,0:T(8,128)S(1)} %get-tuple-element.74.x3a), channel_id=1, source_target_pairs={{16,32},{32,16},{48,64},{64,48},{80,96},{96,80},{17,33},{33,17},{4... | collective-permute-start | bytes 3145736 | tf_op jit(solution)/shard_map/ppermute | solution.py:267
  36.6 10.5 %collective-permute-done.6.cross = f32[64,32,128]{2,1,0:T(8,128)S(1)} collective-permute-done((f32[64,32,128]{2,1,0:T(8,128)S(1)}, f32[64,32,128]{2,1,0:T(8,128)S(1)}, u32[]{:S(2)}, u32[]{:S(2)}) %collective-permute-start.6) | collective-permute-done | bytes 1048608 | tf_op jit(solution)/shard_map/ppermute | solution.py:267
  47.2 0.6 shard_map.54
  47.8 3.6 %collective-permute-start.10 = (f32[4,128,128]{2,1,0:T(8,128)S(1)}, f32[4,128,128]{2,1,0:T(8,128)S(1)}, u32[]{:S(2)}, u32[]{:S(2)}) collective-permute-start(f32[4,128,128]{2,1,0:T(8,128)S(1)} %get-tuple-element.82), channel_id=1, source_target_pairs={{0,1},{1,2},{2,3},{4,5},{5,6},{6,7},{8,9},{9,10},{10,11},{12,13},{... | collective-permute-start | bytes 786440 | tf_op jit(solution)/shard_map/ppermute | solution.py:256
  51.4 2.2 %collective-permute-start.11 = (f32[4,128,128]{2,1,0:T(8,128)S(1)}, f32[4,128,128]{2,1,0:T(8,128)S(1)}, u32[]{:S(2)}, u32[]{:S(2)}) collective-permute-start(f32[4,128,128]{2,1,0:T(8,128)S(1)} %get-tuple-element.83), channel_id=1, source_target_pairs={{1,0},{2,1},{3,2},{5,4},{6,5},{7,6},{9,8},{10,9},{11,10},{13,12},{... | collective-permute-start | bytes 786440 | tf_op jit(solution)/shard_map/ppermute | solution.py:259
  53.6 3.9 %collective-permute-start.8 = (f32[4,32,128]{2,1,0:T(8,128)S(1)}, f32[4,32,128]{2,1,0:T(8,128)S(1)}, u32[]{:S(2)}, u32[]{:S(2)}) collective-permute-start(f32[4,32,128]{2,1,0:T(8,128)S(1)} %get-tuple-element.80), channel_id=1, source_target_pairs={{0,4},{4,8},{8,12},{1,5},{5,9},{9,13},{2,6},{6,10},{10,14},{3,7},{... | collective-permute-start | bytes 196616 | tf_op jit(solution)/shard_map/ppermute | solution.py:256
  57.6 0.9 collective-permute-done.12.cross
  58.4 1.3 %collective-permute-start.9 = (f32[4,32,128]{2,1,0:T(8,128)S(1)}, f32[4,32,128]{2,1,0:T(8,128)S(1)}, u32[]{:S(2)}, u32[]{:S(2)}) collective-permute-start(f32[4,32,128]{2,1,0:T(8,128)S(1)} %get-tuple-element.81), channel_id=1, source_target_pairs={{4,0},{8,4},{12,8},{5,1},{9,5},{13,9},{6,2},{10,6},{14,10},{7,3},{... | collective-permute-start | bytes 196616 | tf_op jit(solution)/shard_map/ppermute | solution.py:259
  59.7 1.9 %collective-permute-start.13 = (f32[64,32,128]{2,1,0:T(8,128)S(1)}, f32[64,32,128]{2,1,0:T(8,128)S(1)}, u32[]{:S(2)}, u32[]{:S(2)}) collective-permute-start(f32[64,32,128]{2,1,0:T(8,128)S(1)} %get-tuple-element.79.x3b), channel_id=1, source_target_pairs={{16,32},{32,16},{48,64},{64,48},{80,96},{96,80},{17,33},{33,17},{4... | collective-permute-start | bytes 3145736 | tf_op jit(solution)/shard_map/ppermute | solution.py:267
  61.7 3.5 %collective-permute-done.9.lh = f32[4,32,128]{2,1,0:T(8,128)S(1)} collective-permute-done((f32[4,32,128]{2,1,0:T(8,128)S(1)}, f32[4,32,128]{2,1,0:T(8,128)S(1)}, u32[]{:S(2)}, u32[]{:S(2)}) %collective-permute-start.9) | collective-permute-done | bytes 65568 | tf_op jit(solution)/shard_map/ppermute | solution.py:259
  65.2 0.0 collective-permute-done.10.vl
  65.2 0.6 shard_map.55
  65.8 3.5 %shard_map.56 = (f32[128,32,128]{2,1,0:T(8,128)S(1)}, f32[128,32,128]{2,1,0:T(8,128)S(1)}, f32[128,32,128]{2,1,0:T(8,128)S(1)}, f32[4,32,128]{2,1,0:T(8,128)S(1)...) custom-call(f32[128,32,128]{2,1,0:T(8,128)S(1)} %get-tuple-element.7, ...), custom_call_target="tpu_custom_call", output_to_operand_aliasing={{3}: (12, {}), {4}: (13, {}), {5}: (14, {}), {6}: (15, {})} | custom-call | tf_op jit(solution)/shard_map/pallas_call | solution.py:26
  69.3 0.3 collective-permute-start.14
  69.6 1.9 %collective-permute-start.19 = (f32[64,32,128]{2,1,0:T(8,128)S(1)}, f32[64,32,128]{2,1,0:T(8,128)S(1)}, u32[]{:S(2)}, u32[]{:S(2)}) collective-permute-start(f32[64,32,128]{2,1,0:T(8,128)S(1)} %get-tuple-element.93.x3a), channel_id=1, source_target_pairs={{16,32},{32,16},{48,64},{64,48},{80,96},{96,80},{17,33},{33,17},{4... | collective-permute-start | bytes 3145736 | tf_op jit(solution)/shard_map/ppermute | solution.py:267
  71.5 4.4 %collective-permute-done.13.cross = f32[64,32,128]{2,1,0:T(8,128)S(1)} collective-permute-done((f32[64,32,128]{2,1,0:T(8,128)S(1)}, f32[64,32,128]{2,1,0:T(8,128)S(1)}, u32[]{:S(2)}, u32[]{:S(2)}) %collective-permute-start.13) | collective-permute-done | bytes 1048608 | tf_op jit(solution)/shard_map/ppermute | solution.py:267
  75.8 0.6 shard_map.57
  76.4 2.2 %collective-permute-start.20 = (f32[64,32,128]{2,1,0:T(8,128)S(1)}, f32[64,32,128]{2,1,0:T(8,128)S(1)}, u32[]{:S(2)}, u32[]{:S(2)}) collective-permute-start(f32[64,32,128]{2,1,0:T(8,128)S(1)} %get-tuple-element.98.x3b), channel_id=1, source_target_pairs={{16,32},{32,16},{48,64},{64,48},{80,96},{96,80},{17,33},{33,17},{4... | collective-permute-start | bytes 3145736 | tf_op jit(solution)/shard_map/ppermute | solution.py:267
  78.6 3.6 %collective-permute-start.17 = (f32[4,128,128]{2,1,0:T(8,128)S(1)}, f32[4,128,128]{2,1,0:T(8,128)S(1)}, u32[]{:S(2)}, u32[]{:S(2)}) collective-permute-start(f32[4,128,128]{2,1,0:T(8,128)S(1)} %get-tuple-element.101), channel_id=1, source_target_pairs={{0,1},{1,2},{2,3},{4,5},{5,6},{6,7},{8,9},{9,10},{10,11},{12,13},{... | collective-permute-start | bytes 786440 | tf_op jit(solution)/shard_map/ppermute | solution.py:256
  82.3 2.2 %collective-permute-start.18 = (f32[4,128,128]{2,1,0:T(8,128)S(1)}, f32[4,128,128]{2,1,0:T(8,128)S(1)}, u32[]{:S(2)}, u32[]{:S(2)}) collective-permute-start(f32[4,128,128]{2,1,0:T(8,128)S(1)} %get-tuple-element.102), channel_id=1, source_target_pairs={{1,0},{2,1},{3,2},{5,4},{6,5},{7,6},{9,8},{10,9},{11,10},{13,12},{... | collective-permute-start | bytes 786440 | tf_op jit(solution)/shard_map/ppermute | solution.py:259
  84.5 2.6 %collective-permute-done.19.cross = f32[64,32,128]{2,1,0:T(8,128)S(1)} collective-permute-done((f32[64,32,128]{2,1,0:T(8,128)S(1)}, f32[64,32,128]{2,1,0:T(8,128)S(1)}, u32[]{:S(2)}, u32[]{:S(2)}) %collective-permute-start.19) | collective-permute-done | bytes 1048608 | tf_op jit(solution)/shard_map/ppermute | solution.py:267
  87.1 4.5 %collective-permute-start.15 = (f32[4,32,128]{2,1,0:T(8,128)S(1)}, f32[4,32,128]{2,1,0:T(8,128)S(1)}, u32[]{:S(2)}, u32[]{:S(2)}) collective-permute-start(f32[4,32,128]{2,1,0:T(8,128)S(1)} %get-tuple-element.99), channel_id=1, source_target_pairs={{0,4},{4,8},{8,12},{1,5},{5,9},{9,13},{2,6},{6,10},{10,14},{3,7},{... | collective-permute-start | bytes 196616 | tf_op jit(solution)/shard_map/ppermute | solution.py:256
  91.6 2.4 %collective-permute-done.15.ll = f32[4,32,128]{2,1,0:T(8,128)S(1)} collective-permute-done((f32[4,32,128]{2,1,0:T(8,128)S(1)}, f32[4,32,128]{2,1,0:T(8,128)S(1)}, u32[]{:S(2)}, u32[]{:S(2)}) %collective-permute-start.15) | collective-permute-done | bytes 65568 | tf_op jit(solution)/shard_map/ppermute | solution.py:256
  94.0 1.3 %collective-permute-start.16 = (f32[4,32,128]{2,1,0:T(8,128)S(1)}, f32[4,32,128]{2,1,0:T(8,128)S(1)}, u32[]{:S(2)}, u32[]{:S(2)}) collective-permute-start(f32[4,32,128]{2,1,0:T(8,128)S(1)} %get-tuple-element.100), channel_id=1, source_target_pairs={{4,0},{8,4},{12,8},{5,1},{9,5},{13,9},{6,2},{10,6},{14,10},{7,3},{... | collective-permute-start | bytes 196616 | tf_op jit(solution)/shard_map/ppermute | solution.py:259
  95.3 5.6 %collective-permute-done.16.lh = f32[4,32,128]{2,1,0:T(8,128)S(1)} collective-permute-done((f32[4,32,128]{2,1,0:T(8,128)S(1)}, f32[4,32,128]{2,1,0:T(8,128)S(1)}, u32[]{:S(2)}, u32[]{:S(2)}) %collective-permute-start.16) | collective-permute-done | bytes 65568 | tf_op jit(solution)/shard_map/ppermute | solution.py:259
  100.8 0.7 shard_map.58
  101.6 5.7 %shard_map.59 = (f32[128,32,128]{2,1,0:T(8,128)S(1)}, f32[128,32,128]{2,1,0:T(8,128)S(1)}, f32[128,32,128]{2,1,0:T(8,128)S(1)}, f32[4,2,4,32,128]{4,3,2,1,0:T(8,128)S(1)}, f32[4,128,32,128]{3,2,1,0:T(8,128)}) custom-call(f32[128,32,128]{2,1,0:T(8,128)S(1)} %get-tuple-element.90.x0, f32[128,32,128]{2,1,0:T(8,128)S(1)} %get-tuple-element.91.x1, ...), custom_call_target="tpu_custom_call" | custom-call | tf_op jit(solution)/shard_map/pallas_call | solution.py:26
  107.3 0.7 shard_map.60
  108.0 13.3 %all_to_all.5.stats = f32[4,2,4,32,128]{4,3,2,1,0:T(8,128)S(1)} all-to-all(f32[4,2,4,32,128]{4,3,2,1,0:T(8,128)S(1)} %get-tuple-element.110), channel_id=1, replica_groups=mesh['lat'=8,'lon'=4,'lev'=4] {'lon'}, dimensions={0} | all-to-all | bytes 1048576 | tf_op jit(solution)/shard_map/all_to_all | solution.py:321
  121.3 4.3 %shard_map.61 = (f32[4,128,32,128]{3,2,1,0:T(8,128)}, f32[4,128,32,128]{3,2,1,0:T(8,128)}) custom-call(f32[128,32,128]{2,1,0:T(8,128)S(1)} %get-tuple-element.104.q0, f32[128,32,128]{2,1,0:T(8,128)S(1)} %get-tuple-element.105.q1, f32[128,32,128]{2,1,0:T(8,128)S(1)} %get-tuple-element.106.q2, ...), custom_call_target="tpu_custom_call", output_to_operand_aliasing={{1}: (6, {})} | custom-call | tf_op jit(solution)/shard_map/pallas_call | solution.py:26
  (7 shorter events, 0.0 us)
Async XLA Ops:
  3.2 21.3 %collective-permute-start = (f32[128,32,128]{2,1,0:T(8,128)S(1)}, f32[128,32,128]{2,1,0:T(8,128)S(1)}, u32[]{:S(2)}, u32[]{:S(2)}) collective-permute-start(f32[128,32,128]{2,1,0:T(8,128)S(1)} %get-tuple-element.57.x0), channel_id=1, source_target_pairs={{0,16},{16,0},{32,48},{48,32},{64,80},{80,64},{96,112},{112,96},{1... | collective-permute-start | bytes 6291464 | tf_op jit(solution)/shard_map/ppermute | solution.py:267
  3.3 20.6 %collective-permute-start.5 = (f32[64,32,128]{2,1,0:T(8,128)S(1)}, f32[64,32,128]{2,1,0:T(8,128)S(1)}, u32[]{:S(2)}, u32[]{:S(2)}) collective-permute-start(f32[64,32,128]{2,1,0:T(8,128)S(1)} %get-tuple-element.59.x3a), channel_id=1, source_target_pairs={{16,32},{32,16},{48,64},{64,48},{80,96},{96,80},{17,33},{33,17},{4... | collective-permute-start | bytes 3145736 | tf_op jit(solution)/shard_map/ppermute | solution.py:267
  5.7 18.2 %collective-permute-start.3 = (f32[4,128,128]{2,1,0:T(8,128)S(1)}, f32[4,128,128]{2,1,0:T(8,128)S(1)}, u32[]{:S(2)}, u32[]{:S(2)}) collective-permute-start(f32[4,128,128]{2,1,0:T(8,128)S(1)} %get-tuple-element.63), channel_id=1, source_target_pairs={{0,1},{1,2},{2,3},{4,5},{5,6},{6,7},{8,9},{9,10},{10,11},{12,13},{... | collective-permute-start | bytes 786440 | tf_op jit(solution)/shard_map/ppermute | solution.py:256
  9.6 14.3 %collective-permute-start.4 = (f32[4,128,128]{2,1,0:T(8,128)S(1)}, f32[4,128,128]{2,1,0:T(8,128)S(1)}, u32[]{:S(2)}, u32[]{:S(2)}) collective-permute-start(f32[4,128,128]{2,1,0:T(8,128)S(1)} %get-tuple-element.64), channel_id=1, source_target_pairs={{1,0},{2,1},{3,2},{5,4},{6,5},{7,6},{9,8},{10,9},{11,10},{13,12},{... | collective-permute-start | bytes 786440 | tf_op jit(solution)/shard_map/ppermute | solution.py:259
  11.6 5.7 %collective-permute-start.1 = (f32[4,32,128]{2,1,0:T(8,128)S(1)}, f32[4,32,128]{2,1,0:T(8,128)S(1)}, u32[]{:S(2)}, u32[]{:S(2)}) collective-permute-start(f32[4,32,128]{2,1,0:T(8,128)S(1)} %get-tuple-element.61), channel_id=1, source_target_pairs={{0,4},{4,8},{8,12},{1,5},{5,9},{9,13},{2,6},{6,10},{10,14},{3,7},{... | collective-permute-start | bytes 196616 | tf_op jit(solution)/shard_map/ppermute | solution.py:256
  17.3 6.6 %collective-permute-start.2 = (f32[4,32,128]{2,1,0:T(8,128)S(1)}, f32[4,32,128]{2,1,0:T(8,128)S(1)}, u32[]{:S(2)}, u32[]{:S(2)}) collective-permute-start(f32[4,32,128]{2,1,0:T(8,128)S(1)} %get-tuple-element.62), channel_id=1, source_target_pairs={{4,0},{8,4},{12,8},{5,1},{9,5},{13,9},{6,2},{10,6},{14,10},{7,3},{... | collective-permute-start | bytes 196616 | tf_op jit(solution)/shard_map/ppermute | solution.py:259
  31.0 34.8 %collective-permute-start.7 = (f32[128,32,128]{2,1,0:T(8,128)S(1)}, f32[128,32,128]{2,1,0:T(8,128)S(1)}, u32[]{:S(2)}, u32[]{:S(2)}) collective-permute-start(f32[128,32,128]{2,1,0:T(8,128)S(1)} %get-tuple-element.71.x0), channel_id=1, source_target_pairs={{0,16},{16,0},{32,48},{48,32},{64,80},{80,64},{96,112},{112,96},{1... | collective-permute-start | bytes 6291464 | tf_op jit(solution)/shard_map/ppermute | solution.py:267
  31.1 16.1 %collective-permute-start.6 = (f32[64,32,128]{2,1,0:T(8,128)S(1)}, f32[64,32,128]{2,1,0:T(8,128)S(1)}, u32[]{:S(2)}, u32[]{:S(2)}) collective-permute-start(f32[64,32,128]{2,1,0:T(8,128)S(1)} %get-tuple-element.60.x3b), channel_id=1, source_target_pairs={{16,32},{32,16},{48,64},{64,48},{80,96},{96,80},{17,33},{33,17},{4... | collective-permute-start | bytes 3145736 | tf_op jit(solution)/shard_map/ppermute | solution.py:267
  33.0 25.4 %collective-permute-start.12 = (f32[64,32,128]{2,1,0:T(8,128)S(1)}, f32[64,32,128]{2,1,0:T(8,128)S(1)}, u32[]{:S(2)}, u32[]{:S(2)}) collective-permute-start(f32[64,32,128]{2,1,0:T(8,128)S(1)} %get-tuple-element.74.x3a), channel_id=1, source_target_pairs={{16,32},{32,16},{48,64},{64,48},{80,96},{96,80},{17,33},{33,17},{4... | collective-permute-start | bytes 3145736 | tf_op jit(solution)/shard_map/ppermute | solution.py:267
  47.8 17.4 %collective-permute-start.10 = (f32[4,128,128]{2,1,0:T(8,128)S(1)}, f32[4,128,128]{2,1,0:T(8,128)S(1)}, u32[]{:S(2)}, u32[]{:S(2)}) collective-permute-start(f32[4,128,128]{2,1,0:T(8,128)S(1)} %get-tuple-element.82), channel_id=1, source_target_pairs={{0,1},{1,2},{2,3},{4,5},{5,6},{6,7},{8,9},{9,10},{10,11},{12,13},{... | collective-permute-start | bytes 786440 | tf_op jit(solution)/shard_map/ppermute | solution.py:256
  51.4 13.8 %collective-permute-start.11 = (f32[4,128,128]{2,1,0:T(8,128)S(1)}, f32[4,128,128]{2,1,0:T(8,128)S(1)}, u32[]{:S(2)}, u32[]{:S(2)}) collective-permute-start(f32[4,128,128]{2,1,0:T(8,128)S(1)} %get-tuple-element.83), channel_id=1, source_target_pairs={{1,0},{2,1},{3,2},{5,4},{6,5},{7,6},{9,8},{10,9},{11,10},{13,12},{... | collective-permute-start | bytes 786440 | tf_op jit(solution)/shard_map/ppermute | solution.py:259
  53.6 6.1 %collective-permute-start.8 = (f32[4,32,128]{2,1,0:T(8,128)S(1)}, f32[4,32,128]{2,1,0:T(8,128)S(1)}, u32[]{:S(2)}, u32[]{:S(2)}) collective-permute-start(f32[4,32,128]{2,1,0:T(8,128)S(1)} %get-tuple-element.80), channel_id=1, source_target_pairs={{0,4},{4,8},{8,12},{1,5},{5,9},{9,13},{2,6},{6,10},{10,14},{3,7},{... | collective-permute-start | bytes 196616 | tf_op jit(solution)/shard_map/ppermute | solution.py:256
  58.4 6.8 %collective-permute-start.9 = (f32[4,32,128]{2,1,0:T(8,128)S(1)}, f32[4,32,128]{2,1,0:T(8,128)S(1)}, u32[]{:S(2)}, u32[]{:S(2)}) collective-permute-start(f32[4,32,128]{2,1,0:T(8,128)S(1)} %get-tuple-element.81), channel_id=1, source_target_pairs={{4,0},{8,4},{12,8},{5,1},{9,5},{13,9},{6,2},{10,6},{14,10},{7,3},{... | collective-permute-start | bytes 196616 | tf_op jit(solution)/shard_map/ppermute | solution.py:259
  59.7 16.1 %collective-permute-start.13 = (f32[64,32,128]{2,1,0:T(8,128)S(1)}, f32[64,32,128]{2,1,0:T(8,128)S(1)}, u32[]{:S(2)}, u32[]{:S(2)}) collective-permute-start(f32[64,32,128]{2,1,0:T(8,128)S(1)} %get-tuple-element.79.x3b), channel_id=1, source_target_pairs={{16,32},{32,16},{48,64},{64,48},{80,96},{96,80},{17,33},{33,17},{4... | collective-permute-start | bytes 3145736 | tf_op jit(solution)/shard_map/ppermute | solution.py:267
  69.3 32.3 %collective-permute-start.14 = (f32[128,32,128]{2,1,0:T(8,128)S(1)}, f32[128,32,128]{2,1,0:T(8,128)S(1)}, u32[]{:S(2)}, u32[]{:S(2)}) collective-permute-start(f32[128,32,128]{2,1,0:T(8,128)S(1)} %get-tuple-element.90.x0), channel_id=1, source_target_pairs={{0,16},{16,0},{32,48},{48,32},{64,80},{80,64},{96,112},{112,96},{1... | collective-permute-start | bytes 6291464 | tf_op jit(solution)/shard_map/ppermute | solution.py:267
  69.6 17.5 %collective-permute-start.19 = (f32[64,32,128]{2,1,0:T(8,128)S(1)}, f32[64,32,128]{2,1,0:T(8,128)S(1)}, u32[]{:S(2)}, u32[]{:S(2)}) collective-permute-start(f32[64,32,128]{2,1,0:T(8,128)S(1)} %get-tuple-element.93.x3a), channel_id=1, source_target_pairs={{16,32},{32,16},{48,64},{64,48},{80,96},{96,80},{17,33},{33,17},{4... | collective-permute-start | bytes 3145736 | tf_op jit(solution)/shard_map/ppermute | solution.py:267
  76.4 30.9 %collective-permute-start.20 = (f32[64,32,128]{2,1,0:T(8,128)S(1)}, f32[64,32,128]{2,1,0:T(8,128)S(1)}, u32[]{:S(2)}, u32[]{:S(2)}) collective-permute-start(f32[64,32,128]{2,1,0:T(8,128)S(1)} %get-tuple-element.98.x3b), channel_id=1, source_target_pairs={{16,32},{32,16},{48,64},{64,48},{80,96},{96,80},{17,33},{33,17},{4... | collective-permute-start | bytes 3145736 | tf_op jit(solution)/shard_map/ppermute | solution.py:267
  78.6 22.2 %collective-permute-start.17 = (f32[4,128,128]{2,1,0:T(8,128)S(1)}, f32[4,128,128]{2,1,0:T(8,128)S(1)}, u32[]{:S(2)}, u32[]{:S(2)}) collective-permute-start(f32[4,128,128]{2,1,0:T(8,128)S(1)} %get-tuple-element.101), channel_id=1, source_target_pairs={{0,1},{1,2},{2,3},{4,5},{5,6},{6,7},{8,9},{9,10},{10,11},{12,13},{... | collective-permute-start | bytes 786440 | tf_op jit(solution)/shard_map/ppermute | solution.py:256
  82.3 18.5 %collective-permute-start.18 = (f32[4,128,128]{2,1,0:T(8,128)S(1)}, f32[4,128,128]{2,1,0:T(8,128)S(1)}, u32[]{:S(2)}, u32[]{:S(2)}) collective-permute-start(f32[4,128,128]{2,1,0:T(8,128)S(1)} %get-tuple-element.102), channel_id=1, source_target_pairs={{1,0},{2,1},{3,2},{5,4},{6,5},{7,6},{9,8},{10,9},{11,10},{13,12},{... | collective-permute-start | bytes 786440 | tf_op jit(solution)/shard_map/ppermute | solution.py:259
  87.1 6.9 %collective-permute-start.15 = (f32[4,32,128]{2,1,0:T(8,128)S(1)}, f32[4,32,128]{2,1,0:T(8,128)S(1)}, u32[]{:S(2)}, u32[]{:S(2)}) collective-permute-start(f32[4,32,128]{2,1,0:T(8,128)S(1)} %get-tuple-element.99), channel_id=1, source_target_pairs={{0,4},{4,8},{8,12},{1,5},{5,9},{9,13},{2,6},{6,10},{10,14},{3,7},{... | collective-permute-start | bytes 196616 | tf_op jit(solution)/shard_map/ppermute | solution.py:256
  94.0 6.8 %collective-permute-start.16 = (f32[4,32,128]{2,1,0:T(8,128)S(1)}, f32[4,32,128]{2,1,0:T(8,128)S(1)}, u32[]{:S(2)}, u32[]{:S(2)}) collective-permute-start(f32[4,32,128]{2,1,0:T(8,128)S(1)} %get-tuple-element.100), channel_id=1, source_target_pairs={{4,0},{8,4},{12,8},{5,1},{9,5},{13,9},{6,2},{10,6},{14,10},{7,3},{... | collective-permute-start | bytes 196616 | tf_op jit(solution)/shard_map/ppermute | solution.py:259
where the time goes:
time: 126 us
  starting transfers between devices  47.8 us (38%)
  waiting for transfers between devices  34.5 us (27%)
  Pallas kernels  29.2 us (23%)
  blocking collectives  13.3 us (11%)
    pallas_call x12, Pallas kernels, call(): pl.pallas_call(kernel, out_shape=tuple((space(shape, F32) for shape, spac...  29.2 us
    ppermute x6, starting transfers between devices, to_next(): lax.ppermute(array, axis, [(i, i + 1) for i in range(lax.axis_size(axis)...  23 us
    ppermute x9, waiting for transfers between devices, swapped(): return lax.ppermute(q, 'lat', pairs)  18.3 us
    ppermute x9, starting transfers between devices, swapped(): return lax.ppermute(q, 'lat', pairs)  14.5 us
    all_to_all x1, blocking collectives, shards(): everyone = lax.all_to_all(stats, 'lon', 0, 0, tiled=True)  13.3 us
    ppermute x6, waiting for transfers between devices, to_previous(): lax.ppermute(array, axis, [(i + 1, i) for i in range(lax.axis_size(axis)...  11.5 us
    ppermute x6, starting transfers between devices, to_previous(): lax.ppermute(array, axis, [(i + 1, i) for i in range(lax.axis_size(axis)...  10.3 us
    ppermute x6, waiting for transfers between devices, to_next(): lax.ppermute(array, axis, [(i, i + 1) for i in range(lax.axis_size(axis)...  4.63 us
  transfers between devices with their start and end apart: 21, of which 9 were waited for; matrix products, arithmetic and copies ran while one was open for 0% of the time, Pallas kernels for 12%

commit v1 on v0

--- a/solution.py
+++ b/solution.py
@@ -39,15 +39,26 @@
     return odd * p + (1 - odd) * (NJ - 1 - p)
 
 
+def at_end(axis, high):
+    return lax.axis_index(axis) == (lax.axis_size(axis) - 1 if high else 0)
+
+
+def unless(outside, values):
+    return jnp.where(outside, jnp.zeros_like(values), values)
+
+
 def start(src, dst, sem):
     copy = pltpu.make_async_copy(src, dst, sem)
     copy.start()
     return copy
 
 
-def messages(tracer, x3a, x3b, x0, lon_low, lon_high, lev_low, lev_high, sems):
+def first(tracer, x3a, sem):
+    start(tracer.at[row_of(3), pl.ds(0, HALF)], x3a, sem).wait()
+
+
+def messages(tracer, x3b, x0, lon_low, lon_high, lev_low, lev_high, sems):
     pairs = [
-        (tracer.at[row_of(3), pl.ds(0, HALF)], x3a),
         (tracer.at[row_of(3), pl.ds(HALF, HALF)], x3b),
         (tracer.at[row_of(0)], x0),
     ]
@@ -71,14 +82,15 @@
         copy.wait()
 
 
-def advance(x, before, after, below, above, lev_low, lev_high, c, s, out, lev_outs=None, sums=None):
+def advance(x, before, after, below, above, lev_low, lev_high, c, s, out, lev_outs=None, sums=None, top=False):
     def at(view, i, size=None):
         ref, first = view
         return ref[first + i] if size is None else ref[pl.ds(pl.multiple_of(first + i, UNROLL), size), :]
 
     def block(b, carry):
         i0 = b * UNROLL
-        low, high = (at(lev_low, i0, UNROLL), at(lev_high, i0, UNROLL))
+        low = unless(at_end("lev", False), at(lev_low, i0, UNROLL))
+        high = unless(at_end("lev", True), at(lev_high, i0, UNROLL))
         prev = jnp.where(b == 0, before, at(x, jnp.maximum(i0 - 1, 0)))
         here = at(x, i0)
         for r in range(UNROLL):
@@ -88,7 +100,8 @@
                 nxt = jnp.where(b == HALF // UNROLL - 1, after, at(x, jnp.minimum(i0 + UNROLL, HALF - 1)))
             down = jnp.concatenate([low[r : r + 1], here[: NK - 1]], axis=0)
             up = jnp.concatenate([here[1:], high[r : r + 1]], axis=0)
-            spread = (prev + nxt) + (at(below, i0 + r) + at(above, i0 + r)) + (down + up) - 6.0 * here
+            over = at(above, i0 + r) if top is False else unless(top, at(above, i0 + r))
+            spread = (prev + nxt) + (at(below, i0 + r) + over) + (down + up) - 6.0 * here
             new = here + at(c, i0 + r) * spread + at(s, i0 + r)
             out[0][out[1] + i0 + r] = new
             if lev_outs is not None:
@@ -112,10 +125,8 @@
 
 def put_stats(stats, p, sums):
     shift, total, squares = sums
-    mean, square = (shift + total * (1.0 / NI), squares - total * (total * (1.0 / NI)))
-    for d in range(stats.shape[0]):
-        stats[d, 0, p] = mean
-        stats[d, 1, p] = square
+    stats[0, p] = shift + total * (1.0 / NI)
+    stats[1, p] = squares - total * (total * (1.0 / NI))
 
 
 def no_sums():
@@ -133,8 +144,8 @@
             first = h * HALF
             below = (on, first) if p == 0 else (xs[p - 1], first)
             above = (xs[3 + h], 0) if p == 2 else (xs[p + 1], first)
-            before = x[HALF - 1] if h else lon_low[p]
-            after = lon_high[p] if h else x[HALF]
+            before = x[HALF - 1] if h else unless(at_end("lon", False), lon_low[p])
+            after = unless(at_end("lon", True), lon_high[p]) if h else x[HALF]
             sums = advance(
                 (x, first), before, after, below, above, (lev_low.at[p], first), (lev_high.at[p], first),
                 (cs[p][0], first), (cs[p][1], first), (out, first),
@@ -152,10 +163,13 @@
 def edge_half(h, x2, x3, cross, halo, c3, s3, out, faces=None, sums=None):
     lon_low, lon_high, lev_low, lev_high = halo
     p, first = 3, h * HALF
+    before = x3[0][HALF - 1] if h else unless(at_end("lon", False), lon_low[p])
+    after = unless(at_end("lon", True), lon_high[p]) if h else x3[1][0]
     sums = advance(
-        (x3[h], 0), x3[0][HALF - 1] if h else lon_low[p], lon_high[p] if h else x3[1][0],
+        (x3[h], 0), before, after,
         (x2, first), (cross, 0), (lev_low.at[p], first), (lev_high.at[p], first), (c3, first), (s3, first), (out, 0),
         None if faces is None else ((faces[2].at[p], first), (faces[3].at[p], first)), sums,
+        jnp.logical_or(at_end("lat", False), at_end("lat", True)),
     )
     if faces is not None:
         if h:
@@ -179,9 +193,9 @@
         raw[n] = sums[n]
 
 
-def edge_b_last(x2, x3a, x3b, cross, ll, lh, vl, vh, c3, s3, raw, a0, out, stats):
+def edge_b_last(x2, x3a, x3b, cross, ll, lh, vl, vh, c3, s3, raw, out, stats):
     sums = (raw[0], raw[1], raw[2])
-    put_stats(stats, 3, edge_half(1, x2, (x3a, x3b), cross, (ll, lh, vl, vh), c3, s3, out, None, sums))
+    put_stats(stats, 0, edge_half(1, x2, (x3a, x3b), cross, (ll, lh, vl, vh), c3, s3, out, None, sums))
 
 
 def inner_first(
@@ -219,49 +233,68 @@
         copy.wait()
 
 
-def scaled(q0, q1, q2, q3a, q3b, stats, a0, out, end, buffers, sems):
-    parts = stats.shape[0]
-    last = [start(q, end.at[row_of(3), pl.ds(h * HALF, HALF)], sems.at[NJ + h]) for h, q in enumerate((q3a, q3b))]
-    copies = []
-    for p in range(NJ):
-        means = [stats[d, 0, p] for d in range(parts)]
-        mean = sum(means[1:], means[0]) * (1.0 / parts)
-        square = sum([stats[d, 1, p] for d in range(1, parts)], stats[0, 1, p])
-        for m in means:
-            square = square + NI * ((m - mean) * (m - mean))
-        scale = lax.rsqrt(square * (1.0 / (parts * NI)) + 0.0001)
-        slot = p % 2
-        if p >= 2:
-            copies[p - 2].wait()
-        for first, q in ((0, (q0, q1, q2)[p]),) if p < 3 else ((0, q3a), (HALF, q3b)):
-
-            def block(b, _, first=first, q=q):
-                i0 = b * UNROLL
-                for r in range(UNROLL):
-                    buffers[slot, first + i0 + r] = (q[i0 + r] - mean) * scale
-                return 0
-
-            lax.fori_loop(0, q.shape[0] // UNROLL, block, 0)
-        copies.append(start(buffers.at[slot], out.at[row_of(p)], sems.at[p]))
-    for copy in (*copies[2:], *last):
-        copy.wait()
+def scaled(parts, p, stats):
+    means = [part[0, p] for part in stats]
+    mean = sum(means[1:], means[0]) * (1.0 / parts)
+    square = sum([part[1, p] for part in stats[1:]], stats[0][1, p])
+    for m in means:
+        square = square + NI * ((m - mean) * (m - mean))
+    return mean, lax.rsqrt(square * (1.0 / (parts * NI)) + 0.0001)
+
+
+def scale_rows(q, mean, scale, out):
+    def block(b, _):
+        i0 = b * UNROLL
+        for r in range(UNROLL):
+            out[i0 + r] = (q[i0 + r] - mean) * scale
+        return 0
+
+    lax.fori_loop(0, q.shape[0] // UNROLL, block, 0)
+
+
+def scale_inner(parts):
+    def kernel(q0, q1, q2, q3a, q3b, *rest):
+        stats, (_, out, end, buffers, sems) = rest[:parts], rest[parts:]
+        copies = [start(q, end.at[row_of(3), pl.ds(h * HALF, HALF)], sems.at[3 + h]) for h, q in enumerate((q3a, q3b))]
+        for p, q in enumerate((q0, q1, q2)):
+            scale_rows(q, *scaled(parts, p, stats), buffers.at[p])
+            copies.append(start(buffers.at[p], out.at[row_of(p)], sems.at[p]))
+        for copy in copies:
+            copy.wait()
+
+    return kernel
+
+
+def scale_edge(parts):
+    def kernel(q3a, q3b, *rest):
+        stats, (_, out, buffers, sems) = rest[:parts], rest[parts:]
+        mean, scale = scaled(parts, 0, stats)
+        copies = []
+        for h, q in enumerate((q3a, q3b)):
+            scale_rows(q, mean, scale, buffers.at[h])
+            copies.append(start(buffers.at[h], out.at[row_of(3), pl.ds(h * HALF, HALF)], sems.at[h]))
+        for copy in copies:
+            copy.wait()
+
+    return kernel
 
 
 def shards(tracer, c, s):
     lats, lons = (lax.axis_size(a) for a in ("lat", "lon"))
     on_pairs = [(i, i ^ 1) for i in range(lats)]
-    cross_pairs = [(i, ((i + 1) ^ 1) - 1) for i in range(lats) if 0 <= ((i + 1) ^ 1) - 1 < lats]
-
-    def to_next(array, axis):
-        return lax.ppermute(array, axis, [(i, i + 1) for i in range(lax.axis_size(axis) - 1)])
-
-    def to_previous(array, axis):
-        return lax.ppermute(array, axis, [(i + 1, i) for i in range(lax.axis_size(axis) - 1)])
+    cross_pairs = [(i, (((i + 1) ^ 1) - 1) % lats) for i in range(lats)]
+
+    def rotated(array, axis, by):
+        n = lax.axis_size(axis)
+        return lax.ppermute(array, axis, [(i, (i + by) % n) for i in range(n)])
+
+    def of_everyone(array):
+        return [array] + [rotated(array, "lon", by) for by in range(1, lons)]
 
     def exchanged(faces):
         lon_low, lon_high, lev_low, lev_high = faces
-        lev = (to_next(lev_high, "lev"), to_previous(lev_low, "lev"))
-        return [to_next(lon_high, "lon"), to_previous(lon_low, "lon"), *lev]
+        lev = (rotated(lev_high, "lev", 1), rotated(lev_low, "lev", -1))
+        return [rotated(lon_high, "lon", 1), rotated(lon_low, "lon", -1), *lev]
 
     def swapped(q, pairs):
         return lax.ppermute(q, "lat", pairs)
@@ -271,9 +304,8 @@
     half, plane, face_outs = ((HALF_PLANE, VMEM), (PLANE, VMEM), [(f, VMEM) for f in FACES])
     inner_fields = ((3, *PLANE), VMEM)
 
-    x3a, x3b, x0, *faces = call(
-        messages, [(tracer, HBM)], [half, half, plane] + face_outs, scratch=[dma((3 + 4 * NJ,))]
-    )
+    (x3a,) = call(first, [(tracer, HBM)], [half], scratch=[dma(())])
+    x3b, x0, *faces = call(messages, [(tracer, HBM)], [half, plane] + face_outs, scratch=[dma((2 + 4 * NJ,))])
     cross = [swapped(x3a, cross_pairs), swapped(x3b, cross_pairs)]
     on = swapped(x0, on_pairs)
     halo = exchanged(faces)
@@ -307,21 +339,23 @@
             halo = exchanged(faces)
         else:
             qa, raw = call(edge_a_last, edge + vm(cross[0]) + rest, [half, ((3, NK, NM), VMEM)])
-            all_stats = ((lons, 2, NJ, NK, NM), VMEM)
             q0, q1, q2, stats, end = call(
                 inner_last, vm(x0, x1, x2, x3a, x3b, on, *halo, cc, ss, raw),
-                [plane] * 3 + [all_stats, ((NJ, *PLANE), HBM)], scratch=[dma((3,))],
+                [plane] * 3 + [((2, 3, NK, NM), VMEM), ((NJ, *PLANE), HBM)], scratch=[dma((3,))],
             )
-            qb, stats = call(
-                edge_b_last, edge + vm(cross[1]) + rest + vm(raw, stats), [half, all_stats],
-                aliases={11: 1},
-            )
+            inner_stats = of_everyone(stats)
+            qb, stats = call(edge_b_last, edge + vm(cross[1]) + rest + vm(raw), [half, ((2, 1, NK, NM), VMEM)])
+            edge_stats = of_everyone(stats)
         x0, x1, x2, x3a, x3b = q0, q1, q2, qa, qb
 
-    everyone = lax.all_to_all(stats, "lon", 0, 0, tiled=True)
     out, end = call(
-        scaled, vm(x0, x1, x2, x3a, x3b, everyone) + [(end, HBM)], [((NJ, *PLANE), HBM)] * 2,
-        scratch=[pltpu.VMEM((2, *PLANE), F32), dma((NJ + 2,))], aliases={6: 1}, limit=8 << 20,
+        scale_inner(lons), vm(x0, x1, x2, x3a, x3b, *inner_stats) + [(end, HBM)],
+        [((NJ, *PLANE), HBM)] * 2, scratch=[pltpu.VMEM((3, *PLANE), F32), dma((5,))],
+        aliases={5 + lons: 1}, limit=10 << 20,
+    )
+    (out,) = call(
+        scale_edge(lons), vm(x3a, x3b, *edge_stats) + [(out, HBM)], [((NJ, *PLANE), HBM)],
+        scratch=[pltpu.VMEM((2, *HALF_PLANE), F32), dma((2,))], aliases={2 + lons: 0}, limit=6 << 20,
     )
     return out, end
 

time: 126 us -> 124 us (0.984)
  the two profiles are of different devices: /device:TPU:40 before, /device:TPU:0 now
where the time goes in v1:
time: 124 us
  waiting for transfers between devices  52.4 us (42%)
  starting transfers between devices  39.8 us (32%)
  Pallas kernels  30.8 us (25%)
    ppermute x9, waiting for transfers between devices, swapped(): return lax.ppermute(q, 'lat', pairs)  37 us
    pallas_call x14, Pallas kernels, call(): pl.pallas_call(kernel, out_shape=tuple((space(shape, F32) for shape, spac...  30.8 us
    ppermute x18, starting transfers between devices, rotated(): return lax.ppermute(array, axis, [(i, (i + by) % n) for i in range(n)])  29.1 us
    ppermute x18, waiting for transfers between devices, rotated(): return lax.ppermute(array, axis, [(i, (i + by) % n) for i in range(n)])  15.4 us
    ppermute x9, starting transfers between devices, swapped(): return lax.ppermute(q, 'lat', pairs)  10.7 us
  transfers between devices with their start and end apart: 27, of which 11 were waited for; matrix products, arithmetic and copies ran while one was open for 0% of the time, Pallas kernels for 14%

profile of v1, /device:TPU:0, one launch (start us, length us, event | category | flops | bytes accessed | tf_op | source)
XLA Modules:
  0.0 123.8 jit_solution(9643417898466671887)
XLA Ops:
  0.6 2.2 %shard_map.50 = (f32[64,32,128]{2,1,0:T(8,128)S(1)}, f32[128,32,128]{2,1,0:T(8,128)S(1)}, f32[4,32,128]{2,1,0:T(8,128)S(1)}, f32[4,32,128]{2,1,0:T(8,128)S(1)}, ...) custom-call(f32[4,128,32,128]{3,2,1,0:T(8,128)} %tracer.7), custom_call_target="tpu_custom_call" | custom-call | tf_op jit(solution)/shard_map/pallas_call | solution.py:26
  2.9 1.2 %shard_map.52.x3a = f32[64,32,128]{2,1,0:T(8,128)S(1)} custom-call(f32[4,128,32,128]{3,2,1,0:T(8,128)} %tracer.7), custom_call_target="tpu_custom_call" | custom-call | tf_op jit(solution)/shard_map/pallas_call | solution.py:26
  4.2 3.3 %collective-permute-start.5 = (f32[64,32,128]{2,1,0:T(8,128)S(1)}, f32[64,32,128]{2,1,0:T(8,128)S(1)}, u32[]{:S(2)}, u32[]{:S(2)}) collective-permute-start(f32[64,32,128]{2,1,0:T(8,128)S(1)} %shard_map.52.x3a), channel_id=1, source_target_pairs={{0,112},{16,32},{32,16},{48,64},{64,48},{80,96},{96,80},{112,0},{1... | collective-permute-start | bytes 3145736 | tf_op jit(solution)/shard_map/ppermute | solution.py:300
  7.5 1.9 %collective-permute-start.3 = (f32[4,128,128]{2,1,0:T(8,128)S(1)}, f32[4,128,128]{2,1,0:T(8,128)S(1)}, u32[]{:S(2)}, u32[]{:S(2)}) collective-permute-start(f32[4,128,128]{2,1,0:T(8,128)S(1)} %get-tuple-element.63), channel_id=1, source_target_pairs={{0,1},{1,2},{2,3},{3,0},{4,5},{5,6},{6,7},{7,4},{8,9},{9,10},{10,1... | collective-permute-start | bytes 786440 | tf_op jit(solution)/shard_map/ppermute | solution.py:289
  9.4 2.1 %collective-permute-start.4 = (f32[4,128,128]{2,1,0:T(8,128)S(1)}, f32[4,128,128]{2,1,0:T(8,128)S(1)}, u32[]{:S(2)}, u32[]{:S(2)}) collective-permute-start(f32[4,128,128]{2,1,0:T(8,128)S(1)} %get-tuple-element.64), channel_id=1, source_target_pairs={{0,3},{1,0},{2,1},{3,2},{4,7},{5,4},{6,5},{7,6},{8,11},{9,8},{10,9... | collective-permute-start | bytes 786440 | tf_op jit(solution)/shard_map/ppermute | solution.py:289
  11.5 1.5 %collective-permute-start.1 = (f32[4,32,128]{2,1,0:T(8,128)S(1)}, f32[4,32,128]{2,1,0:T(8,128)S(1)}, u32[]{:S(2)}, u32[]{:S(2)}) collective-permute-start(f32[4,32,128]{2,1,0:T(8,128)S(1)} %get-tuple-element.61), channel_id=1, source_target_pairs={{0,4},{4,8},{8,12},{12,0},{1,5},{5,9},{9,13},{13,1},{2,6},{6,10},{... | collective-permute-start | bytes 196616 | tf_op jit(solution)/shard_map/ppermute | solution.py:289
  13.0 4.0 %collective-permute-done.1.ll = f32[4,32,128]{2,1,0:T(8,128)S(1)} collective-permute-done((f32[4,32,128]{2,1,0:T(8,128)S(1)}, f32[4,32,128]{2,1,0:T(8,128)S(1)}, u32[]{:S(2)}, u32[]{:S(2)}) %collective-permute-start.1) | collective-permute-done | bytes 65568 | tf_op jit(solution)/shard_map/ppermute | solution.py:289
  17.0 1.5 %collective-permute-start.2 = (f32[4,32,128]{2,1,0:T(8,128)S(1)}, f32[4,32,128]{2,1,0:T(8,128)S(1)}, u32[]{:S(2)}, u32[]{:S(2)}) collective-permute-start(f32[4,32,128]{2,1,0:T(8,128)S(1)} %get-tuple-element.62), channel_id=1, source_target_pairs={{0,12},{4,0},{8,4},{12,8},{1,13},{5,1},{9,5},{13,9},{2,14},{6,2},{... | collective-permute-start | bytes 196616 | tf_op jit(solution)/shard_map/ppermute | solution.py:289
  18.6 2.9 %shard_map.51 = (f32[128,32,128]{2,1,0:T(8,128)S(1)}, f32[128,32,128]{2,1,0:T(8,128)S(1)}, f32[128,32,128]{2,1,0:T(8,128)S(1)}) custom-call(f32[4,128,32,128]{3,2,1,0:T(8,128)} %tracer.7, f32[4,128,32,128]{3,2,1,0:T(8,128)} %c.3, f32[4,128,32,128]{3,2,1,0:T(8,128)} %s.3), custom_call_target="tpu_custom_call" | custom-call | tf_op jit(solution)/shard_map/pallas_call | solution.py:26
  21.5 0.6 shard_map.53
  22.1 6.5 %shard_map.54 = (f32[128,32,128]{2,1,0:T(8,128)S(1)}, f32[128,32,128]{2,1,0:T(8,128)S(1)}, f32[128,32,128]{2,1,0:T(8,128)S(1)}, f32[4,32,128]{2,1,0:T(8,128)S(1)...) custom-call(f32[4,128,32,128]{3,2,1,0:T(8,128)} %tracer.7, ...), custom_call_target="tpu_custom_call", output_to_operand_aliasing={{3}: (12, {}), {4}: (13, {}), {5}: (14, {}), {6}: (15, {})} | custom-call | tf_op jit(solution)/shard_map/pallas_call | solution.py:26
  28.7 1.5 %collective-permute-start.6 = (f32[64,32,128]{2,1,0:T(8,128)S(1)}, f32[64,32,128]{2,1,0:T(8,128)S(1)}, u32[]{:S(2)}, u32[]{:S(2)}) collective-permute-start(f32[64,32,128]{2,1,0:T(8,128)S(1)} %get-tuple-element.60.x3b), channel_id=1, source_target_pairs={{0,112},{16,32},{32,16},{48,64},{64,48},{80,96},{96,80},{112,0},{1... | collective-permute-start | bytes 3145736 | tf_op jit(solution)/shard_map/ppermute | solution.py:300
  30.2 1.5 %collective-permute-start.12 = (f32[64,32,128]{2,1,0:T(8,128)S(1)}, f32[64,32,128]{2,1,0:T(8,128)S(1)}, u32[]{:S(2)}, u32[]{:S(2)}) collective-permute-start(f32[64,32,128]{2,1,0:T(8,128)S(1)} %get-tuple-element.74.x3a), channel_id=1, source_target_pairs={{0,112},{16,32},{32,16},{48,64},{64,48},{80,96},{96,80},{112,0},{1... | collective-permute-start | bytes 3145736 | tf_op jit(solution)/shard_map/ppermute | solution.py:300
  31.7 12.5 %collective-permute-done.6.cross = f32[64,32,128]{2,1,0:T(8,128)S(1)} collective-permute-done((f32[64,32,128]{2,1,0:T(8,128)S(1)}, f32[64,32,128]{2,1,0:T(8,128)S(1)}, u32[]{:S(2)}, u32[]{:S(2)}) %collective-permute-start.6) | collective-permute-done | bytes 1048608 | tf_op jit(solution)/shard_map/ppermute | solution.py:300
  44.2 0.6 shard_map.55
  44.8 0.4 collective-permute-start.10
  45.3 2.9 %collective-permute-start.11 = (f32[4,128,128]{2,1,0:T(8,128)S(1)}, f32[4,128,128]{2,1,0:T(8,128)S(1)}, u32[]{:S(2)}, u32[]{:S(2)}) collective-permute-start(f32[4,128,128]{2,1,0:T(8,128)S(1)} %get-tuple-element.83), channel_id=1, source_target_pairs={{0,3},{1,0},{2,1},{3,2},{4,7},{5,4},{6,5},{7,6},{8,11},{9,8},{10,9... | collective-permute-start | bytes 786440 | tf_op jit(solution)/shard_map/ppermute | solution.py:289
  48.1 0.8 collective-permute-start.8
  49.0 6.5 %collective-permute-done.12.cross = f32[64,32,128]{2,1,0:T(8,128)S(1)} collective-permute-done((f32[64,32,128]{2,1,0:T(8,128)S(1)}, f32[64,32,128]{2,1,0:T(8,128)S(1)}, u32[]{:S(2)}, u32[]{:S(2)}) %collective-permute-start.12) | collective-permute-done | bytes 1048608 | tf_op jit(solution)/shard_map/ppermute | solution.py:300
  55.5 2.6 %collective-permute-start.9 = (f32[4,32,128]{2,1,0:T(8,128)S(1)}, f32[4,32,128]{2,1,0:T(8,128)S(1)}, u32[]{:S(2)}, u32[]{:S(2)}) collective-permute-start(f32[4,32,128]{2,1,0:T(8,128)S(1)} %get-tuple-element.81), channel_id=1, source_target_pairs={{0,12},{4,0},{8,4},{12,8},{1,13},{5,1},{9,5},{13,9},{2,14},{6,2},{... | collective-permute-start | bytes 196616 | tf_op jit(solution)/shard_map/ppermute | solution.py:289
  58.0 1.9 %collective-permute-done.9.lh = f32[4,32,128]{2,1,0:T(8,128)S(1)} collective-permute-done((f32[4,32,128]{2,1,0:T(8,128)S(1)}, f32[4,32,128]{2,1,0:T(8,128)S(1)}, u32[]{:S(2)}, u32[]{:S(2)}) %collective-permute-start.9) | collective-permute-done | bytes 65568 | tf_op jit(solution)/shard_map/ppermute | solution.py:289
  59.9 0.6 shard_map.56
  60.5 3.5 %shard_map.57 = (f32[128,32,128]{2,1,0:T(8,128)S(1)}, f32[128,32,128]{2,1,0:T(8,128)S(1)}, f32[128,32,128]{2,1,0:T(8,128)S(1)}, f32[4,32,128]{2,1,0:T(8,128)S(1)...) custom-call(f32[128,32,128]{2,1,0:T(8,128)S(1)} %get-tuple-element.7, ...), custom_call_target="tpu_custom_call", output_to_operand_aliasing={{3}: (12, {}), {4}: (13, {}), {5}: (14, {}), {6}: (15, {})} | custom-call | tf_op jit(solution)/shard_map/pallas_call | solution.py:26
  64.0 0.1 collective-permute-start.23
  64.1 1.1 collective-permute-start.13
  65.2 1.9 %collective-permute-start.14 = (f32[64,32,128]{2,1,0:T(8,128)S(1)}, f32[64,32,128]{2,1,0:T(8,128)S(1)}, u32[]{:S(2)}, u32[]{:S(2)}) collective-permute-start(f32[64,32,128]{2,1,0:T(8,128)S(1)} %get-tuple-element.91.x3a), channel_id=1, source_target_pairs={{0,112},{16,32},{32,16},{48,64},{64,48},{80,96},{96,80},{112,0},{1... | collective-permute-start | bytes 3145736 | tf_op jit(solution)/shard_map/ppermute | solution.py:300
  67.2 12.5 %collective-permute-done.13.cross = f32[64,32,128]{2,1,0:T(8,128)S(1)} collective-permute-done((f32[64,32,128]{2,1,0:T(8,128)S(1)}, f32[64,32,128]{2,1,0:T(8,128)S(1)}, u32[]{:S(2)}, u32[]{:S(2)}) %collective-permute-start.13) | collective-permute-done | bytes 1048608 | tf_op jit(solution)/shard_map/ppermute | solution.py:300
  79.6 0.6 shard_map.58
  80.2 1.1 collective-permute-start.19
  81.3 1.9 %collective-permute-start.17 = (f32[4,128,128]{2,1,0:T(8,128)S(1)}, f32[4,128,128]{2,1,0:T(8,128)S(1)}, u32[]{:S(2)}, u32[]{:S(2)}) collective-permute-start(f32[4,128,128]{2,1,0:T(8,128)S(1)} %get-tuple-element.99), channel_id=1, source_target_pairs={{0,1},{1,2},{2,3},{3,0},{4,5},{5,6},{6,7},{7,4},{8,9},{9,10},{10,1... | collective-permute-start | bytes 786440 | tf_op jit(solution)/shard_map/ppermute | solution.py:289
  83.2 2.1 %collective-permute-start.18 = (f32[4,128,128]{2,1,0:T(8,128)S(1)}, f32[4,128,128]{2,1,0:T(8,128)S(1)}, u32[]{:S(2)}, u32[]{:S(2)}) collective-permute-start(f32[4,128,128]{2,1,0:T(8,128)S(1)} %get-tuple-element.100), channel_id=1, source_target_pairs={{0,3},{1,0},{2,1},{3,2},{4,7},{5,4},{6,5},{7,6},{8,11},{9,8},{10,9... | collective-permute-start | bytes 786440 | tf_op jit(solution)/shard_map/ppermute | solution.py:289
  85.4 5.5 %collective-permute-done.14.cross = f32[64,32,128]{2,1,0:T(8,128)S(1)} collective-permute-done((f32[64,32,128]{2,1,0:T(8,128)S(1)}, f32[64,32,128]{2,1,0:T(8,128)S(1)}, u32[]{:S(2)}, u32[]{:S(2)}) %collective-permute-start.14) | collective-permute-done | bytes 1048608 | tf_op jit(solution)/shard_map/ppermute | solution.py:300
  90.9 0.3 collective-permute-start.15
  91.2 5.5 %collective-permute-done.15.ll = f32[4,32,128]{2,1,0:T(8,128)S(1)} collective-permute-done((f32[4,32,128]{2,1,0:T(8,128)S(1)}, f32[4,32,128]{2,1,0:T(8,128)S(1)}, u32[]{:S(2)}, u32[]{:S(2)}) %collective-permute-start.15) | collective-permute-done | bytes 65568 | tf_op jit(solution)/shard_map/ppermute | solution.py:289
  96.7 2.0 %collective-permute-start.16 = (f32[4,32,128]{2,1,0:T(8,128)S(1)}, f32[4,32,128]{2,1,0:T(8,128)S(1)}, u32[]{:S(2)}, u32[]{:S(2)}) collective-permute-start(f32[4,32,128]{2,1,0:T(8,128)S(1)} %get-tuple-element.98), channel_id=1, source_target_pairs={{0,12},{4,0},{8,4},{12,8},{1,13},{5,1},{9,5},{13,9},{2,14},{6,2},{... | collective-permute-start | bytes 196616 | tf_op jit(solution)/shard_map/ppermute | solution.py:289
  98.7 2.2 %collective-permute-done.16.lh = f32[4,32,128]{2,1,0:T(8,128)S(1)} collective-permute-done((f32[4,32,128]{2,1,0:T(8,128)S(1)}, f32[4,32,128]{2,1,0:T(8,128)S(1)}, u32[]{:S(2)}, u32[]{:S(2)}) %collective-permute-start.16) | collective-permute-done | bytes 65568 | tf_op jit(solution)/shard_map/ppermute | solution.py:289
  101.0 0.7 shard_map.59
  101.7 5.8 %shard_map.61 = (f32[128,32,128]{2,1,0:T(8,128)S(1)}, f32[128,32,128]{2,1,0:T(8,128)S(1)}, f32[128,32,128]{2,1,0:T(8,128)S(1)}, f32[2,3,32,128]{3,2,1,0:T(8,128)S(1)}, f32[4,128,32,128]{3,2,1,0:T(8,128)}) custom-call(f32[128,32,128]{2,1,0:T(8,128)S(1)} %get-tuple-element.105.x0, f32[128,32,128]{2,1,0:T(8,128)S(1)} %get-tuple-element.106.x1, ...), custom_call_target="tpu_custom_call" | custom-call | tf_op jit(solution)/shard_map/pallas_call | solution.py:26
  107.5 3.3 %collective-permute-start.26 = (f32[2,3,32,128]{3,2,1,0:T(8,128)S(1)}, f32[2,3,32,128]{3,2,1,0:T(8,128)S(1)}, u32[]{:S(2)}, u32[]{:S(2)}) collective-permute-start(f32[2,3,32,128]{3,2,1,0:T(8,128)S(1)} %get-tuple-element.110.rest_0_), channel_id=1, source_target_pairs={{0,12},{4,0},{8,4},{12,8},{1,13},{5,1},{9,5},{13,9},{2,14},{6,2},{... | collective-permute-start | bytes 294920 | tf_op jit(solution)/shard_map/ppermute | solution.py:289
  110.8 0.9 collective-permute-start.24
  111.7 0.7 shard_map.60
  112.5 2.4 %collective-permute-start.22 = (f32[2,1,32,128]{3,2,1,0:T(8,128)S(1)}, f32[2,1,32,128]{3,2,1,0:T(8,128)S(1)}, u32[]{:S(2)}, u32[]{:S(2)}) collective-permute-start(f32[2,1,32,128]{3,2,1,0:T(8,128)S(1)} %get-tuple-element.104.rest_0_), channel_id=1, source_target_pairs={{0,12},{4,0},{8,4},{12,8},{1,13},{5,1},{9,5},{13,9},{2,14},{6,2},{... | collective-permute-start | bytes 98312 | tf_op jit(solution)/shard_map/ppermute | solution.py:289
  114.8 2.3 %collective-permute-start.21 = (f32[2,1,32,128]{3,2,1,0:T(8,128)S(1)}, f32[2,1,32,128]{3,2,1,0:T(8,128)S(1)}, u32[]{:S(2)}, u32[]{:S(2)}) collective-permute-start(f32[2,1,32,128]{3,2,1,0:T(8,128)S(1)} %get-tuple-element.104.rest_0_), channel_id=1, source_target_pairs={{0,8},{4,12},{8,0},{12,4},{1,9},{5,13},{9,1},{13,5},{2,10},{6,14},... | collective-permute-start | bytes 98312 | tf_op jit(solution)/shard_map/ppermute | solution.py:289
  117.2 0.5 collective-permute-done.25.rest_2_
  117.6 0.8 collective-permute-done.24.rest_1_
  118.4 3.4 %shard_map.62 = (f32[4,128,32,128]{3,2,1,0:T(8,128)}, f32[4,128,32,128]{3,2,1,0:T(8,128)}) custom-call(f32[128,32,128]{2,1,0:T(8,128)S(1)} %get-tuple-element.107.q0, f32[128,32,128]{2,1,0:T(8,128)S(1)} %get-tuple-element.108.q1, f32[128,32,128]{2,1,0:T(8,128)S(1)} %get-tuple-element.109.q2, ...), custom_call_target="tpu_custom_call", output_to_operand_aliasing={{1}: (9, {})} | custom-call | tf_op jit(solution)/shard_map/pallas_call | solution.py:26
  121.8 0.5 collective-permute-done.20.rest_1_
  122.3 1.5 %shard_map.63 = f32[4,128,32,128]{3,2,1,0:T(8,128)} custom-call(f32[64,32,128]{2,1,0:T(8,128)S(1)} %get-tuple-element.101.q3a, f32[64,32,128]{2,1,0:T(8,128)S(1)} %get-tuple-element.103.q3b, f32[2,1,32,128]{3,2,1,0:T(8,128)S(1)} %get-tuple-element.104.rest_0_, f32[2,1,32,128]{3,2,1,0:T(8,128)S(1)} %collective-permute-done.20.rest_1_, ...), custom_call_target="tpu_custom_call", output_to_operand_aliasing={{}: (6, {})} | custom-call | tf_op jit(solution)/shard_map/pallas_call | solution.py:26
  (20 shorter events, 0.2 us)
Async XLA Ops:
  2.8 19.2 %collective-permute-start = (f32[128,32,128]{2,1,0:T(8,128)S(1)}, f32[128,32,128]{2,1,0:T(8,128)S(1)}, u32[]{:S(2)}, u32[]{:S(2)}) collective-permute-start(f32[128,32,128]{2,1,0:T(8,128)S(1)} %get-tuple-element.58.x0), channel_id=1, source_target_pairs={{0,16},{16,0},{32,48},{48,32},{64,80},{80,64},{96,112},{112,96},{1... | collective-permute-start | bytes 6291464 | tf_op jit(solution)/shard_map/ppermute | solution.py:300
  4.2 17.3 %collective-permute-start.5 = (f32[64,32,128]{2,1,0:T(8,128)S(1)}, f32[64,32,128]{2,1,0:T(8,128)S(1)}, u32[]{:S(2)}, u32[]{:S(2)}) collective-permute-start(f32[64,32,128]{2,1,0:T(8,128)S(1)} %shard_map.52.x3a), channel_id=1, source_target_pairs={{0,112},{16,32},{32,16},{48,64},{64,48},{80,96},{96,80},{112,0},{1... | collective-permute-start | bytes 3145736 | tf_op jit(solution)/shard_map/ppermute | solution.py:300
  7.5 14.0 %collective-permute-start.3 = (f32[4,128,128]{2,1,0:T(8,128)S(1)}, f32[4,128,128]{2,1,0:T(8,128)S(1)}, u32[]{:S(2)}, u32[]{:S(2)}) collective-permute-start(f32[4,128,128]{2,1,0:T(8,128)S(1)} %get-tuple-element.63), channel_id=1, source_target_pairs={{0,1},{1,2},{2,3},{3,0},{4,5},{5,6},{6,7},{7,4},{8,9},{9,10},{10,1... | collective-permute-start | bytes 786440 | tf_op jit(solution)/shard_map/ppermute | solution.py:289
  9.4 12.1 %collective-permute-start.4 = (f32[4,128,128]{2,1,0:T(8,128)S(1)}, f32[4,128,128]{2,1,0:T(8,128)S(1)}, u32[]{:S(2)}, u32[]{:S(2)}) collective-permute-start(f32[4,128,128]{2,1,0:T(8,128)S(1)} %get-tuple-element.64), channel_id=1, source_target_pairs={{0,3},{1,0},{2,1},{3,2},{4,7},{5,4},{6,5},{7,6},{8,11},{9,8},{10,9... | collective-permute-start | bytes 786440 | tf_op jit(solution)/shard_map/ppermute | solution.py:289
  11.5 5.5 %collective-permute-start.1 = (f32[4,32,128]{2,1,0:T(8,128)S(1)}, f32[4,32,128]{2,1,0:T(8,128)S(1)}, u32[]{:S(2)}, u32[]{:S(2)}) collective-permute-start(f32[4,32,128]{2,1,0:T(8,128)S(1)} %get-tuple-element.61), channel_id=1, source_target_pairs={{0,4},{4,8},{8,12},{12,0},{1,5},{5,9},{9,13},{13,1},{2,6},{6,10},{... | collective-permute-start | bytes 196616 | tf_op jit(solution)/shard_map/ppermute | solution.py:289
  17.0 4.4 %collective-permute-start.2 = (f32[4,32,128]{2,1,0:T(8,128)S(1)}, f32[4,32,128]{2,1,0:T(8,128)S(1)}, u32[]{:S(2)}, u32[]{:S(2)}) collective-permute-start(f32[4,32,128]{2,1,0:T(8,128)S(1)} %get-tuple-element.62), channel_id=1, source_target_pairs={{0,12},{4,0},{8,4},{12,8},{1,13},{5,1},{9,5},{13,9},{2,14},{6,2},{... | collective-permute-start | bytes 196616 | tf_op jit(solution)/shard_map/ppermute | solution.py:289
  28.6 31.9 %collective-permute-start.7 = (f32[128,32,128]{2,1,0:T(8,128)S(1)}, f32[128,32,128]{2,1,0:T(8,128)S(1)}, u32[]{:S(2)}, u32[]{:S(2)}) collective-permute-start(f32[128,32,128]{2,1,0:T(8,128)S(1)} %get-tuple-element.71.x0), channel_id=1, source_target_pairs={{0,16},{16,0},{32,48},{48,32},{64,80},{80,64},{96,112},{112,96},{1... | collective-permute-start | bytes 6291464 | tf_op jit(solution)/shard_map/ppermute | solution.py:300
  28.7 15.5 %collective-permute-start.6 = (f32[64,32,128]{2,1,0:T(8,128)S(1)}, f32[64,32,128]{2,1,0:T(8,128)S(1)}, u32[]{:S(2)}, u32[]{:S(2)}) collective-permute-start(f32[64,32,128]{2,1,0:T(8,128)S(1)} %get-tuple-element.60.x3b), channel_id=1, source_target_pairs={{0,112},{16,32},{32,16},{48,64},{64,48},{80,96},{96,80},{112,0},{1... | collective-permute-start | bytes 3145736 | tf_op jit(solution)/shard_map/ppermute | solution.py:300
  30.2 25.3 %collective-permute-start.12 = (f32[64,32,128]{2,1,0:T(8,128)S(1)}, f32[64,32,128]{2,1,0:T(8,128)S(1)}, u32[]{:S(2)}, u32[]{:S(2)}) collective-permute-start(f32[64,32,128]{2,1,0:T(8,128)S(1)} %get-tuple-element.74.x3a), channel_id=1, source_target_pairs={{0,112},{16,32},{32,16},{48,64},{64,48},{80,96},{96,80},{112,0},{1... | collective-permute-start | bytes 3145736 | tf_op jit(solution)/shard_map/ppermute | solution.py:300
  44.8 15.1 %collective-permute-start.10 = (f32[4,128,128]{2,1,0:T(8,128)S(1)}, f32[4,128,128]{2,1,0:T(8,128)S(1)}, u32[]{:S(2)}, u32[]{:S(2)}) collective-permute-start(f32[4,128,128]{2,1,0:T(8,128)S(1)} %get-tuple-element.82), channel_id=1, source_target_pairs={{0,1},{1,2},{2,3},{3,0},{4,5},{5,6},{6,7},{7,4},{8,9},{9,10},{10,1... | collective-permute-start | bytes 786440 | tf_op jit(solution)/shard_map/ppermute | solution.py:289
  45.3 14.7 %collective-permute-start.11 = (f32[4,128,128]{2,1,0:T(8,128)S(1)}, f32[4,128,128]{2,1,0:T(8,128)S(1)}, u32[]{:S(2)}, u32[]{:S(2)}) collective-permute-start(f32[4,128,128]{2,1,0:T(8,128)S(1)} %get-tuple-element.83), channel_id=1, source_target_pairs={{0,3},{1,0},{2,1},{3,2},{4,7},{5,4},{6,5},{7,6},{8,11},{9,8},{10,9... | collective-permute-start | bytes 786440 | tf_op jit(solution)/shard_map/ppermute | solution.py:289
  48.1 9.9 %collective-permute-start.8 = (f32[4,32,128]{2,1,0:T(8,128)S(1)}, f32[4,32,128]{2,1,0:T(8,128)S(1)}, u32[]{:S(2)}, u32[]{:S(2)}) collective-permute-start(f32[4,32,128]{2,1,0:T(8,128)S(1)} %get-tuple-element.80), channel_id=1, source_target_pairs={{0,4},{4,8},{8,12},{12,0},{1,5},{5,9},{9,13},{13,1},{2,6},{6,10},{... | collective-permute-start | bytes 196616 | tf_op jit(solution)/shard_map/ppermute | solution.py:289
  55.5 4.5 %collective-permute-start.9 = (f32[4,32,128]{2,1,0:T(8,128)S(1)}, f32[4,32,128]{2,1,0:T(8,128)S(1)}, u32[]{:S(2)}, u32[]{:S(2)}) collective-permute-start(f32[4,32,128]{2,1,0:T(8,128)S(1)} %get-tuple-element.81), channel_id=1, source_target_pairs={{0,12},{4,0},{8,4},{12,8},{1,13},{5,1},{9,5},{13,9},{2,14},{6,2},{... | collective-permute-start | bytes 196616 | tf_op jit(solution)/shard_map/ppermute | solution.py:289
  64.0 37.7 %collective-permute-start.23 = (f32[128,32,128]{2,1,0:T(8,128)S(1)}, f32[128,32,128]{2,1,0:T(8,128)S(1)}, u32[]{:S(2)}, u32[]{:S(2)}) collective-permute-start(f32[128,32,128]{2,1,0:T(8,128)S(1)} %get-tuple-element.105.x0), channel_id=1, source_target_pairs={{0,16},{16,0},{32,48},{48,32},{64,80},{80,64},{96,112},{112,96},{1... | collective-permute-start | bytes 6291464 | tf_op jit(solution)/shard_map/ppermute | solution.py:300
  64.1 15.5 %collective-permute-start.13 = (f32[64,32,128]{2,1,0:T(8,128)S(1)}, f32[64,32,128]{2,1,0:T(8,128)S(1)}, u32[]{:S(2)}, u32[]{:S(2)}) collective-permute-start(f32[64,32,128]{2,1,0:T(8,128)S(1)} %get-tuple-element.79.x3b), channel_id=1, source_target_pairs={{0,112},{16,32},{32,16},{48,64},{64,48},{80,96},{96,80},{112,0},{1... | collective-permute-start | bytes 3145736 | tf_op jit(solution)/shard_map/ppermute | solution.py:300
  65.2 25.7 %collective-permute-start.14 = (f32[64,32,128]{2,1,0:T(8,128)S(1)}, f32[64,32,128]{2,1,0:T(8,128)S(1)}, u32[]{:S(2)}, u32[]{:S(2)}) collective-permute-start(f32[64,32,128]{2,1,0:T(8,128)S(1)} %get-tuple-element.91.x3a), channel_id=1, source_target_pairs={{0,112},{16,32},{32,16},{48,64},{64,48},{80,96},{96,80},{112,0},{1... | collective-permute-start | bytes 3145736 | tf_op jit(solution)/shard_map/ppermute | solution.py:300
  80.2 31.5 %collective-permute-start.19 = (f32[64,32,128]{2,1,0:T(8,128)S(1)}, f32[64,32,128]{2,1,0:T(8,128)S(1)}, u32[]{:S(2)}, u32[]{:S(2)}) collective-permute-start(f32[64,32,128]{2,1,0:T(8,128)S(1)} %get-tuple-element.96.x3b), channel_id=1, source_target_pairs={{0,112},{16,32},{32,16},{48,64},{64,48},{80,96},{96,80},{112,0},{1... | collective-permute-start | bytes 3145736 | tf_op jit(solution)/shard_map/ppermute | solution.py:300
  81.3 19.6 %collective-permute-start.17 = (f32[4,128,128]{2,1,0:T(8,128)S(1)}, f32[4,128,128]{2,1,0:T(8,128)S(1)}, u32[]{:S(2)}, u32[]{:S(2)}) collective-permute-start(f32[4,128,128]{2,1,0:T(8,128)S(1)} %get-tuple-element.99), channel_id=1, source_target_pairs={{0,1},{1,2},{2,3},{3,0},{4,5},{5,6},{6,7},{7,4},{8,9},{9,10},{10,1... | collective-permute-start | bytes 786440 | tf_op jit(solution)/shard_map/ppermute | solution.py:289
  83.2 17.7 %collective-permute-start.18 = (f32[4,128,128]{2,1,0:T(8,128)S(1)}, f32[4,128,128]{2,1,0:T(8,128)S(1)}, u32[]{:S(2)}, u32[]{:S(2)}) collective-permute-start(f32[4,128,128]{2,1,0:T(8,128)S(1)} %get-tuple-element.100), channel_id=1, source_target_pairs={{0,3},{1,0},{2,1},{3,2},{4,7},{5,4},{6,5},{7,6},{8,11},{9,8},{10,9... | collective-permute-start | bytes 786440 | tf_op jit(solution)/shard_map/ppermute | solution.py:289
  90.9 5.8 %collective-permute-start.15 = (f32[4,32,128]{2,1,0:T(8,128)S(1)}, f32[4,32,128]{2,1,0:T(8,128)S(1)}, u32[]{:S(2)}, u32[]{:S(2)}) collective-permute-start(f32[4,32,128]{2,1,0:T(8,128)S(1)} %get-tuple-element.97), channel_id=1, source_target_pairs={{0,4},{4,8},{8,12},{12,0},{1,5},{5,9},{9,13},{13,1},{2,6},{6,10},{... | collective-permute-start | bytes 196616 | tf_op jit(solution)/shard_map/ppermute | solution.py:289
  96.7 4.3 %collective-permute-start.16 = (f32[4,32,128]{2,1,0:T(8,128)S(1)}, f32[4,32,128]{2,1,0:T(8,128)S(1)}, u32[]{:S(2)}, u32[]{:S(2)}) collective-permute-start(f32[4,32,128]{2,1,0:T(8,128)S(1)} %get-tuple-element.98), channel_id=1, source_target_pairs={{0,12},{4,0},{8,4},{12,8},{1,13},{5,1},{9,5},{13,9},{2,14},{6,2},{... | collective-permute-start | bytes 196616 | tf_op jit(solution)/shard_map/ppermute | solution.py:289
  107.5 9.7 %collective-permute-start.26 = (f32[2,3,32,128]{3,2,1,0:T(8,128)S(1)}, f32[2,3,32,128]{3,2,1,0:T(8,128)S(1)}, u32[]{:S(2)}, u32[]{:S(2)}) collective-permute-start(f32[2,3,32,128]{3,2,1,0:T(8,128)S(1)} %get-tuple-element.110.rest_0_), channel_id=1, source_target_pairs={{0,12},{4,0},{8,4},{12,8},{1,13},{5,1},{9,5},{13,9},{2,14},{6,2},{... | collective-permute-start | bytes 294920 | tf_op jit(solution)/shard_map/ppermute | solution.py:289
  110.8 6.8 %collective-permute-start.25 = (f32[2,3,32,128]{3,2,1,0:T(8,128)S(1)}, f32[2,3,32,128]{3,2,1,0:T(8,128)S(1)}, u32[]{:S(2)}, u32[]{:S(2)}) collective-permute-start(f32[2,3,32,128]{3,2,1,0:T(8,128)S(1)} %get-tuple-element.110.rest_0_), channel_id=1, source_target_pairs={{0,8},{4,12},{8,0},{12,4},{1,9},{5,13},{9,1},{13,5},{2,10},{6,14},... | collective-permute-start | bytes 294920 | tf_op jit(solution)/shard_map/ppermute | solution.py:289
  110.8 7.6 %collective-permute-start.24 = (f32[2,3,32,128]{3,2,1,0:T(8,128)S(1)}, f32[2,3,32,128]{3,2,1,0:T(8,128)S(1)}, u32[]{:S(2)}, u32[]{:S(2)}) collective-permute-start(f32[2,3,32,128]{3,2,1,0:T(8,128)S(1)} %get-tuple-element.110.rest_0_), channel_id=1, source_target_pairs={{0,4},{4,8},{8,12},{12,0},{1,5},{5,9},{9,13},{13,1},{2,6},{6,10},{... | collective-permute-start | bytes 294920 | tf_op jit(solution)/shard_map/ppermute | solution.py:289
  112.5 9.3 %collective-permute-start.22 = (f32[2,1,32,128]{3,2,1,0:T(8,128)S(1)}, f32[2,1,32,128]{3,2,1,0:T(8,128)S(1)}, u32[]{:S(2)}, u32[]{:S(2)}) collective-permute-start(f32[2,1,32,128]{3,2,1,0:T(8,128)S(1)} %get-tuple-element.104.rest_0_), channel_id=1, source_target_pairs={{0,12},{4,0},{8,4},{12,8},{1,13},{5,1},{9,5},{13,9},{2,14},{6,2},{... | collective-permute-start | bytes 98312 | tf_op jit(solution)/shard_map/ppermute | solution.py:289
  114.8 6.9 %collective-permute-start.21 = (f32[2,1,32,128]{3,2,1,0:T(8,128)S(1)}, f32[2,1,32,128]{3,2,1,0:T(8,128)S(1)}, u32[]{:S(2)}, u32[]{:S(2)}) collective-permute-start(f32[2,1,32,128]{3,2,1,0:T(8,128)S(1)} %get-tuple-element.104.rest_0_), channel_id=1, source_target_pairs={{0,8},{4,12},{8,0},{12,4},{1,9},{5,13},{9,1},{13,5},{2,10},{6,14},... | collective-permute-start | bytes 98312 | tf_op jit(solution)/shard_map/ppermute | solution.py:289
  117.2 5.1 %collective-permute-start.20 = (f32[2,1,32,128]{3,2,1,0:T(8,128)S(1)}, f32[2,1,32,128]{3,2,1,0:T(8,128)S(1)}, u32[]{:S(2)}, u32[]{:S(2)}) collective-permute-start(f32[2,1,32,128]{3,2,1,0:T(8,128)S(1)} %get-tuple-element.104.rest_0_), channel_id=1, source_target_pairs={{0,4},{4,8},{8,12},{12,0},{1,5},{5,9},{9,13},{13,1},{2,6},{6,10},{... | collective-permute-start | bytes 98312 | tf_op jit(solution)/shard_map/ppermute | solution.py:289

commit v2 on v1

--- a/solution.py
+++ b/solution.py
@@ -16,6 +16,7 @@
 HALF_PLANE = (HALF, NK, NM)
 FACES = ((NJ, NK, NM),) * 2 + ((NJ, NI, NM),) * 2
 UNROLL = 8
+PIECE = 16
 
 
 def call(kernel, args, outs, scratch=(), aliases=None, limit=4 << 20):
@@ -53,8 +54,11 @@
     return copy
 
 
-def first(tracer, x3a, sem):
-    start(tracer.at[row_of(3), pl.ds(0, HALF)], x3a, sem).wait()
+def first(tracer, x3a, sems):
+    rows = [pl.ds(n, HALF // 4) for n in range(0, HALF, HALF // 4)]
+    copies = [start(tracer.at[row_of(3), r], x3a.at[r], sems.at[n]) for n, r in enumerate(rows)]
+    for copy in copies:
+        copy.wait()
 
 
 def messages(tracer, x3b, x0, lon_low, lon_high, lev_low, lev_high, sems):
@@ -134,7 +138,7 @@
     return (None, zero, zero)
 
 
-def inner_planes(xs, on, halo, cs, outs, faces=None, stats=None, ready=lambda p: None, done=lambda p: None):
+def inner_planes(xs, on, halo, cs, outs, faces=None, stats=None, ready=lambda p: None, done=lambda p, h: None):
     lon_low, lon_high, lev_low, lev_high = halo
     for p in (2, 1, 0):
         ready(p)
@@ -152,12 +156,12 @@
                 None if faces is None else ((faces[2].at[p], first), (faces[3].at[p], first)),
                 sums if stats is not None else None,
             )
+            done(p, h)
         if faces is not None:
             faces[0][p] = out[0]
             faces[1][p] = out[NI - 1]
         if stats is not None:
             put_stats(stats, p, sums)
-        done(p)
 
 
 def edge_half(h, x2, x3, cross, halo, c3, s3, out, faces=None, sums=None):
@@ -223,11 +227,16 @@
     )
 
 
-def inner_last(x0, x1, x2, x3a, x3b, on, ll, lh, vl, vh, cc, ss, raw, q0, q1, q2, stats, end, sems):
+def inner_last(x0, x1, x2, x3a, x3b, on, ll, lh, vl, vh, cc, ss, q0, q1, q2, stats, end, sems):
     outs, copies = ((q0, q1, q2), [])
+
+    def done(p, h):
+        rows = pl.ds(h * HALF, HALF)
+        copies.append(start(outs[p].at[rows], end.at[row_of(p), rows], sems.at[2 * p + h]))
+
     inner_planes(
         (x0, x1, x2, x3a, x3b), on, (ll, lh, vl, vh), [(cc.at[p], ss.at[p]) for p in range(3)], outs, None, stats,
-        done=lambda p: copies.append(start(outs[p], end.at[row_of(p)], sems.at[p])),
+        done=done,
     )
     for copy in copies:
         copy.wait()
@@ -267,29 +276,36 @@
 
 def scale_edge(parts):
     def kernel(q3a, q3b, *rest):
-        stats, (_, out, buffers, sems) = rest[:parts], rest[parts:]
+        stats, (_, out, buffer, sems) = rest[:parts], rest[parts:]
         mean, scale = scaled(parts, 0, stats)
         copies = []
         for h, q in enumerate((q3a, q3b)):
-            scale_rows(q, mean, scale, buffers.at[h])
-            copies.append(start(buffers.at[h], out.at[row_of(3), pl.ds(h * HALF, HALF)], sems.at[h]))
+            for first in range(0, HALF, PIECE):
+                rows = pl.ds(h * HALF + first, PIECE)
+                scale_rows(q.at[pl.ds(first, PIECE)], mean, scale, buffer.at[rows])
+                copies.append(start(buffer.at[rows], out.at[row_of(3), rows], sems.at[len(copies)]))
         for copy in copies:
             copy.wait()
 
     return kernel
+
+
+def turns(n):
+    return range(n - 1, 0, -1)
 
 
 def shards(tracer, c, s):
     lats, lons = (lax.axis_size(a) for a in ("lat", "lon"))
     on_pairs = [(i, i ^ 1) for i in range(lats)]
     cross_pairs = [(i, (((i + 1) ^ 1) - 1) % lats) for i in range(lats)]
+    inside_pairs = cross_pairs[1:-1]
 
     def rotated(array, axis, by):
         n = lax.axis_size(axis)
         return lax.ppermute(array, axis, [(i, (i + by) % n) for i in range(n)])
 
     def of_everyone(array):
-        return [array] + [rotated(array, "lon", by) for by in range(1, lons)]
+        return [array] + [rotated(array, "lon", by) for by in turns(lons)]
 
     def exchanged(faces):
         lon_low, lon_high, lev_low, lev_high = faces
@@ -304,7 +320,7 @@
     half, plane, face_outs = ((HALF_PLANE, VMEM), (PLANE, VMEM), [(f, VMEM) for f in FACES])
     inner_fields = ((3, *PLANE), VMEM)
 
-    (x3a,) = call(first, [(tracer, HBM)], [half], scratch=[dma(())])
+    (x3a,) = call(first, [(tracer, HBM)], [half], scratch=[dma((4,))])
     x3b, x0, *faces = call(messages, [(tracer, HBM)], [half, plane] + face_outs, scratch=[dma((2 + 4 * NJ,))])
     cross = [swapped(x3a, cross_pairs), swapped(x3b, cross_pairs)]
     on = swapped(x0, on_pairs)
@@ -335,15 +351,15 @@
                 edge_b, edge + vm(cross[1]) + rest + vm(*faces), [half] + face_outs,
                 aliases={10 + n: 1 + n for n in range(4)},
             )
-            cross[1] = swapped(qb, cross_pairs)
+            cross[1] = swapped(qb, inside_pairs)
             halo = exchanged(faces)
         else:
-            qa, raw = call(edge_a_last, edge + vm(cross[0]) + rest, [half, ((3, NK, NM), VMEM)])
             q0, q1, q2, stats, end = call(
-                inner_last, vm(x0, x1, x2, x3a, x3b, on, *halo, cc, ss, raw),
-                [plane] * 3 + [((2, 3, NK, NM), VMEM), ((NJ, *PLANE), HBM)], scratch=[dma((3,))],
+                inner_last, vm(x0, x1, x2, x3a, x3b, on, *halo, cc, ss),
+                [plane] * 3 + [((2, 3, NK, NM), VMEM), ((NJ, *PLANE), HBM)], scratch=[dma((6,))],
             )
             inner_stats = of_everyone(stats)
+            qa, raw = call(edge_a_last, edge + vm(cross[0]) + rest, [half, ((3, NK, NM), VMEM)])
             qb, stats = call(edge_b_last, edge + vm(cross[1]) + rest + vm(raw), [half, ((2, 1, NK, NM), VMEM)])
             edge_stats = of_everyone(stats)
         x0, x1, x2, x3a, x3b = q0, q1, q2, qa, qb
@@ -355,7 +371,7 @@
     )
     (out,) = call(
         scale_edge(lons), vm(x3a, x3b, *edge_stats) + [(out, HBM)], [((NJ, *PLANE), HBM)],
-        scratch=[pltpu.VMEM((2, *HALF_PLANE), F32), dma((2,))], aliases={2 + lons: 0}, limit=6 << 20,
+        scratch=[pltpu.VMEM(PLANE, F32), dma((NI // PIECE,))], aliases={2 + lons: 0}, limit=6 << 20,
     )
     return out, end
 

time: 124 us -> 118 us (0.952)
  the two profiles are of different devices: /device:TPU:0 before, /device:TPU:40 now
where the time goes in v2:
time: 118 us; the launch traced here: 117 us
  waiting for transfers between devices  48 us (41%)
  starting transfers between devices  37.8 us (32%)
  Pallas kernels  30.4 us (26%)
    ppermute x9, waiting for transfers between devices, swapped(): return lax.ppermute(q, 'lat', pairs)  33.1 us
    pallas_call x14, Pallas kernels, call(): pl.pallas_call(kernel, out_shape=tuple((space(shape, F32) for shape, spac...  30.4 us
    ppermute x18, starting transfers between devices, rotated(): return lax.ppermute(array, axis, [(i, (i + by) % n) for i in range(n)])  26.1 us
    ppermute x18, waiting for transfers between devices, rotated(): return lax.ppermute(array, axis, [(i, (i + by) % n) for i in range(n)])  14.9 us
    ppermute x9, starting transfers between devices, swapped(): return lax.ppermute(q, 'lat', pairs)  11.8 us
  transfers between devices with their start and end apart: 27, of which 9 were waited for; matrix products, arithmetic and copies ran while one was open for 0% of the time, Pallas kernels for 14%

profile of v2, /device:TPU:40, one launch (start us, length us, event | category | flops | bytes accessed | tf_op | source)
XLA Modules:
  0.0 117.0 jit_solution(16826492669301855211)
XLA Ops:
  0.6 2.2 %shard_map.50 = (f32[64,32,128]{2,1,0:T(8,128)S(1)}, f32[128,32,128]{2,1,0:T(8,128)S(1)}, f32[4,32,128]{2,1,0:T(8,128)S(1)}, f32[4,32,128]{2,1,0:T(8,128)S(1)}, ...) custom-call(f32[4,128,32,128]{3,2,1,0:T(8,128)} %tracer.7), custom_call_target="tpu_custom_call" | custom-call | tf_op jit(solution)/shard_map/pallas_call | solution.py:27
  2.8 0.1 collective-permute-start
  2.9 1.2 %shard_map.52.x3a = f32[64,32,128]{2,1,0:T(8,128)S(1)} custom-call(f32[4,128,32,128]{3,2,1,0:T(8,128)} %tracer.7), custom_call_target="tpu_custom_call" | custom-call | tf_op jit(solution)/shard_map/pallas_call | solution.py:27
  4.2 0.6 collective-permute-start.5
  4.8 1.9 %collective-permute-start.3 = (f32[4,128,128]{2,1,0:T(8,128)S(1)}, f32[4,128,128]{2,1,0:T(8,128)S(1)}, u32[]{:S(2)}, u32[]{:S(2)}) collective-permute-start(f32[4,128,128]{2,1,0:T(8,128)S(1)} %get-tuple-element.63), channel_id=1, source_target_pairs={{0,1},{1,2},{2,3},{3,0},{4,5},{5,6},{6,7},{7,4},{8,9},{9,10},{10,1... | collective-permute-start | bytes 786440 | tf_op jit(solution)/shard_map/ppermute | solution.py:305
  6.7 0.1 collective-permute-start.4
  6.8 1.5 %collective-permute-start.1 = (f32[4,32,128]{2,1,0:T(8,128)S(1)}, f32[4,32,128]{2,1,0:T(8,128)S(1)}, u32[]{:S(2)}, u32[]{:S(2)}) collective-permute-start(f32[4,32,128]{2,1,0:T(8,128)S(1)} %get-tuple-element.61), channel_id=1, source_target_pairs={{0,4},{4,8},{8,12},{12,0},{1,5},{5,9},{9,13},{13,1},{2,6},{6,10},{... | collective-permute-start | bytes 196616 | tf_op jit(solution)/shard_map/ppermute | solution.py:305
  8.3 4.5 %collective-permute-done.1.ll = f32[4,32,128]{2,1,0:T(8,128)S(1)} collective-permute-done((f32[4,32,128]{2,1,0:T(8,128)S(1)}, f32[4,32,128]{2,1,0:T(8,128)S(1)}, u32[]{:S(2)}, u32[]{:S(2)}) %collective-permute-start.1) | collective-permute-done | bytes 65568 | tf_op jit(solution)/shard_map/ppermute | solution.py:305
  12.8 1.5 %collective-permute-start.2 = (f32[4,32,128]{2,1,0:T(8,128)S(1)}, f32[4,32,128]{2,1,0:T(8,128)S(1)}, u32[]{:S(2)}, u32[]{:S(2)}) collective-permute-start(f32[4,32,128]{2,1,0:T(8,128)S(1)} %get-tuple-element.62), channel_id=1, source_target_pairs={{0,12},{4,0},{8,4},{12,8},{1,13},{5,1},{9,5},{13,9},{2,14},{6,2},{... | collective-permute-start | bytes 196616 | tf_op jit(solution)/shard_map/ppermute | solution.py:305
  14.4 2.9 %shard_map.51 = (f32[128,32,128]{2,1,0:T(8,128)S(1)}, f32[128,32,128]{2,1,0:T(8,128)S(1)}, f32[128,32,128]{2,1,0:T(8,128)S(1)}) custom-call(f32[4,128,32,128]{3,2,1,0:T(8,128)} %tracer.7, f32[4,128,32,128]{3,2,1,0:T(8,128)} %c.3, f32[4,128,32,128]{3,2,1,0:T(8,128)} %s.3), custom_call_target="tpu_custom_call" | custom-call | tf_op jit(solution)/shard_map/pallas_call | solution.py:27
  17.3 1.2 %collective-permute-done.5.cross = f32[64,32,128]{2,1,0:T(8,128)S(1)} collective-permute-done((f32[64,32,128]{2,1,0:T(8,128)S(1)}, f32[64,32,128]{2,1,0:T(8,128)S(1)}, u32[]{:S(2)}, u32[]{:S(2)}) %collective-permute-start.5) | collective-permute-done | bytes 1048608 | tf_op jit(solution)/shard_map/ppermute | solution.py:316
  18.5 0.6 shard_map.53
  19.1 6.5 %shard_map.54 = (f32[128,32,128]{2,1,0:T(8,128)S(1)}, f32[128,32,128]{2,1,0:T(8,128)S(1)}, f32[128,32,128]{2,1,0:T(8,128)S(1)}, f32[4,32,128]{2,1,0:T(8,128)S(1)...) custom-call(f32[4,128,32,128]{3,2,1,0:T(8,128)} %tracer.7, ...), custom_call_target="tpu_custom_call", output_to_operand_aliasing={{3}: (12, {}), {4}: (13, {}), {5}: (14, {}), {6}: (15, {})} | custom-call | tf_op jit(solution)/shard_map/pallas_call | solution.py:27
  25.6 0.6 collective-permute-start.7
  26.1 1.4 %collective-permute-start.6 = (f32[64,32,128]{2,1,0:T(8,128)S(1)}, f32[64,32,128]{2,1,0:T(8,128)S(1)}, u32[]{:S(2)}, u32[]{:S(2)}) collective-permute-start(f32[64,32,128]{2,1,0:T(8,128)S(1)} %get-tuple-element.60.x3b), channel_id=1, source_target_pairs={{0,112},{16,32},{32,16},{48,64},{64,48},{80,96},{96,80},{112,0},{1... | collective-permute-start | bytes 3145736 | tf_op jit(solution)/shard_map/ppermute | solution.py:316
  27.6 0.3 collective-permute-start.12
  27.9 12.5 %collective-permute-done.6.cross = f32[64,32,128]{2,1,0:T(8,128)S(1)} collective-permute-done((f32[64,32,128]{2,1,0:T(8,128)S(1)}, f32[64,32,128]{2,1,0:T(8,128)S(1)}, u32[]{:S(2)}, u32[]{:S(2)}) %collective-permute-start.6) | collective-permute-done | bytes 1048608 | tf_op jit(solution)/shard_map/ppermute | solution.py:316
  40.4 0.6 shard_map.55
  41.0 2.0 %collective-permute-start.10 = (f32[4,128,128]{2,1,0:T(8,128)S(1)}, f32[4,128,128]{2,1,0:T(8,128)S(1)}, u32[]{:S(2)}, u32[]{:S(2)}) collective-permute-start(f32[4,128,128]{2,1,0:T(8,128)S(1)} %get-tuple-element.82), channel_id=1, source_target_pairs={{0,1},{1,2},{2,3},{3,0},{4,5},{5,6},{6,7},{7,4},{8,9},{9,10},{10,1... | collective-permute-start | bytes 786440 | tf_op jit(solution)/shard_map/ppermute | solution.py:305
  43.0 0.1 collective-permute-start.11
  43.1 1.5 %collective-permute-start.8 = (f32[4,32,128]{2,1,0:T(8,128)S(1)}, f32[4,32,128]{2,1,0:T(8,128)S(1)}, u32[]{:S(2)}, u32[]{:S(2)}) collective-permute-start(f32[4,32,128]{2,1,0:T(8,128)S(1)} %get-tuple-element.80), channel_id=1, source_target_pairs={{0,4},{4,8},{8,12},{12,0},{1,5},{5,9},{9,13},{13,1},{2,6},{6,10},{... | collective-permute-start | bytes 196616 | tf_op jit(solution)/shard_map/ppermute | solution.py:305
  44.6 7.1 %collective-permute-done.12.cross = f32[64,32,128]{2,1,0:T(8,128)S(1)} collective-permute-done((f32[64,32,128]{2,1,0:T(8,128)S(1)}, f32[64,32,128]{2,1,0:T(8,128)S(1)}, u32[]{:S(2)}, u32[]{:S(2)}) %collective-permute-start.12) | collective-permute-done | bytes 1048608 | tf_op jit(solution)/shard_map/ppermute | solution.py:316
  51.6 2.8 %collective-permute-start.9 = (f32[4,32,128]{2,1,0:T(8,128)S(1)}, f32[4,32,128]{2,1,0:T(8,128)S(1)}, u32[]{:S(2)}, u32[]{:S(2)}) collective-permute-start(f32[4,32,128]{2,1,0:T(8,128)S(1)} %get-tuple-element.81), channel_id=1, source_target_pairs={{0,12},{4,0},{8,4},{12,8},{1,13},{5,1},{9,5},{13,9},{2,14},{6,2},{... | collective-permute-start | bytes 196616 | tf_op jit(solution)/shard_map/ppermute | solution.py:305
  54.4 1.9 %collective-permute-done.9.lh = f32[4,32,128]{2,1,0:T(8,128)S(1)} collective-permute-done((f32[4,32,128]{2,1,0:T(8,128)S(1)}, f32[4,32,128]{2,1,0:T(8,128)S(1)}, u32[]{:S(2)}, u32[]{:S(2)}) %collective-permute-start.9) | collective-permute-done | bytes 65568 | tf_op jit(solution)/shard_map/ppermute | solution.py:305
  56.3 0.6 shard_map.56
  56.9 3.5 %shard_map.57 = (f32[128,32,128]{2,1,0:T(8,128)S(1)}, f32[128,32,128]{2,1,0:T(8,128)S(1)}, f32[128,32,128]{2,1,0:T(8,128)S(1)}, f32[4,32,128]{2,1,0:T(8,128)S(1)...) custom-call(f32[128,32,128]{2,1,0:T(8,128)S(1)} %get-tuple-element.7, ...), custom_call_target="tpu_custom_call", output_to_operand_aliasing={{3}: (12, {}), {4}: (13, {}), {5}: (14, {}), {6}: (15, {})} | custom-call | tf_op jit(solution)/shard_map/pallas_call | solution.py:27
  60.5 4.6 %collective-permute-start.13 = (f32[64,32,128]{2,1,0:T(8,128)S(1)}, f32[64,32,128]{2,1,0:T(8,128)S(1)}, u32[]{:S(2)}, u32[]{:S(2)}) collective-permute-start(f32[64,32,128]{2,1,0:T(8,128)S(1)} %get-tuple-element.79.x3b), channel_id=1, source_target_pairs={{16,32},{32,16},{48,64},{64,48},{80,96},{96,80},{17,33},{33,17},{4... | collective-permute-start | bytes 3145736 | tf_op jit(solution)/shard_map/ppermute | solution.py:316
  65.1 0.1 collective-permute-start.14
  65.2 12.4 %collective-permute-done.13.cross = f32[64,32,128]{2,1,0:T(8,128)S(1)} collective-permute-done((f32[64,32,128]{2,1,0:T(8,128)S(1)}, f32[64,32,128]{2,1,0:T(8,128)S(1)}, u32[]{:S(2)}, u32[]{:S(2)}) %collective-permute-start.13) | collective-permute-done | bytes 1048608 | tf_op jit(solution)/shard_map/ppermute | solution.py:316
  77.6 0.6 shard_map.58
  78.2 3.9 %collective-permute-start.19 = (f32[64,32,128]{2,1,0:T(8,128)S(1)}, f32[64,32,128]{2,1,0:T(8,128)S(1)}, u32[]{:S(2)}, u32[]{:S(2)}) collective-permute-start(f32[64,32,128]{2,1,0:T(8,128)S(1)} %get-tuple-element.96.x3b), channel_id=1, source_target_pairs={{16,32},{32,16},{48,64},{64,48},{80,96},{96,80},{17,33},{33,17},{4... | collective-permute-start | bytes 3145736 | tf_op jit(solution)/shard_map/ppermute | solution.py:316
  82.1 1.2 collective-permute-start.15
  83.3 2.6 %collective-permute-start.16 = (f32[4,32,128]{2,1,0:T(8,128)S(1)}, f32[4,32,128]{2,1,0:T(8,128)S(1)}, u32[]{:S(2)}, u32[]{:S(2)}) collective-permute-start(f32[4,32,128]{2,1,0:T(8,128)S(1)} %get-tuple-element.98), channel_id=1, source_target_pairs={{0,12},{4,0},{8,4},{12,8},{1,13},{5,1},{9,5},{13,9},{2,14},{6,2},{... | collective-permute-start | bytes 196616 | tf_op jit(solution)/shard_map/ppermute | solution.py:305
  85.9 2.2 %collective-permute-done.15.ll = f32[4,32,128]{2,1,0:T(8,128)S(1)} collective-permute-done((f32[4,32,128]{2,1,0:T(8,128)S(1)}, f32[4,32,128]{2,1,0:T(8,128)S(1)}, u32[]{:S(2)}, u32[]{:S(2)}) %collective-permute-start.15) | collective-permute-done | bytes 65568 | tf_op jit(solution)/shard_map/ppermute | solution.py:305
  88.0 1.9 %collective-permute-start.17 = (f32[4,128,128]{2,1,0:T(8,128)S(1)}, f32[4,128,128]{2,1,0:T(8,128)S(1)}, u32[]{:S(2)}, u32[]{:S(2)}) collective-permute-start(f32[4,128,128]{2,1,0:T(8,128)S(1)} %get-tuple-element.99), channel_id=1, source_target_pairs={{0,1},{1,2},{2,3},{3,0},{4,5},{5,6},{6,7},{7,4},{8,9},{9,10},{10,1... | collective-permute-start | bytes 786440 | tf_op jit(solution)/shard_map/ppermute | solution.py:305
  89.9 0.1 collective-permute-start.18
  90.1 4.6 %collective-permute-done.17.vl = f32[4,128,128]{2,1,0:T(8,128)S(1)} collective-permute-done((f32[4,128,128]{2,1,0:T(8,128)S(1)}, f32[4,128,128]{2,1,0:T(8,128)S(1)}, u32[]{:S(2)}, u32[]{:S(2)}) %collective-permute-start.17) | collective-permute-done | bytes 262176 | tf_op jit(solution)/shard_map/ppermute | solution.py:305
  94.6 1.7 %collective-permute-done.18.vh = f32[4,128,128]{2,1,0:T(8,128)S(1)} collective-permute-done((f32[4,128,128]{2,1,0:T(8,128)S(1)}, f32[4,128,128]{2,1,0:T(8,128)S(1)}, u32[]{:S(2)}, u32[]{:S(2)}) %collective-permute-start.18) | collective-permute-done | bytes 262176 | tf_op jit(solution)/shard_map/ppermute | solution.py:305
  96.3 5.4 %shard_map.61 = (f32[128,32,128]{2,1,0:T(8,128)S(1)}, f32[128,32,128]{2,1,0:T(8,128)S(1)}, f32[128,32,128]{2,1,0:T(8,128)S(1)}, f32[2,3,32,128]{3,2,1,0:T(8,128)S(1)}, f32[4,128,32,128]{3,2,1,0:T(8,128)}) custom-call(f32[128,32,128]{2,1,0:T(8,128)S(1)} %get-tuple-element.105.x0, f32[128,32,128]{2,1,0:T(8,128)S(1)} %get-tuple-element.106.x1, ...), custom_call_target="tpu_custom_call" | custom-call | tf_op jit(solution)/shard_map/pallas_call | solution.py:27
  101.8 3.5 %collective-permute-start.25 = (f32[2,3,32,128]{3,2,1,0:T(8,128)S(1)}, f32[2,3,32,128]{3,2,1,0:T(8,128)S(1)}, u32[]{:S(2)}, u32[]{:S(2)}) collective-permute-start(f32[2,3,32,128]{3,2,1,0:T(8,128)S(1)} %get-tuple-element.110.rest_0_), channel_id=1, source_target_pairs={{0,8},{4,12},{8,0},{12,4},{1,9},{5,13},{9,1},{13,5},{2,10},{6,14},... | collective-permute-start | bytes 294920 | tf_op jit(solution)/shard_map/ppermute | solution.py:305
  105.3 0.9 collective-permute-start.24
  106.1 0.7 shard_map.59
  106.9 0.7 shard_map.60
  107.6 1.2 %collective-permute-start.22 = (f32[2,1,32,128]{3,2,1,0:T(8,128)S(1)}, f32[2,1,32,128]{3,2,1,0:T(8,128)S(1)}, u32[]{:S(2)}, u32[]{:S(2)}) collective-permute-start(f32[2,1,32,128]{3,2,1,0:T(8,128)S(1)} %get-tuple-element.104.rest_0_), channel_id=1, source_target_pairs={{0,4},{4,8},{8,12},{12,0},{1,5},{5,9},{9,13},{13,1},{2,6},{6,10},{... | collective-permute-start | bytes 98312 | tf_op jit(solution)/shard_map/ppermute | solution.py:305
  108.9 0.7 collective-permute-start.21
  109.6 2.5 %collective-permute-start.20 = (f32[2,1,32,128]{3,2,1,0:T(8,128)S(1)}, f32[2,1,32,128]{3,2,1,0:T(8,128)S(1)}, u32[]{:S(2)}, u32[]{:S(2)}) collective-permute-start(f32[2,1,32,128]{3,2,1,0:T(8,128)S(1)} %get-tuple-element.104.rest_0_), channel_id=1, source_target_pairs={{0,12},{4,0},{8,4},{12,8},{1,13},{5,1},{9,5},{13,9},{2,14},{6,2},{... | collective-permute-start | bytes 98312 | tf_op jit(solution)/shard_map/ppermute | solution.py:305
  112.2 3.4 %shard_map.62 = (f32[4,128,32,128]{3,2,1,0:T(8,128)}, f32[4,128,32,128]{3,2,1,0:T(8,128)}) custom-call(f32[128,32,128]{2,1,0:T(8,128)S(1)} %get-tuple-element.107.q0, f32[128,32,128]{2,1,0:T(8,128)S(1)} %get-tuple-element.108.q1, f32[128,32,128]{2,1,0:T(8,128)S(1)} %get-tuple-element.109.q2, ...), custom_call_target="tpu_custom_call", output_to_operand_aliasing={{1}: (9, {})} | custom-call | tf_op jit(solution)/shard_map/pallas_call | solution.py:27
  115.6 1.4 %shard_map.63 = f32[4,128,32,128]{3,2,1,0:T(8,128)} custom-call(f32[64,32,128]{2,1,0:T(8,128)S(1)} %get-tuple-element.101.q3a, f32[64,32,128]{2,1,0:T(8,128)S(1)} %get-tuple-element.103.q3b, f32[2,1,32,128]{3,2,1,0:T(8,128)S(1)} %get-tuple-element.104.rest_0_, f32[2,1,32,128]{3,2,1,0:T(8,128)S(1)} %collective-permute-done.20.rest_1_, ...), custom_call_target="tpu_custom_call", output_to_operand_aliasing={{}: (6, {})} | custom-call | tf_op jit(solution)/shard_map/pallas_call | solution.py:27
  (20 shorter events, 0.2 us)
Async XLA Ops:
  2.8 16.2 %collective-permute-start = (f32[128,32,128]{2,1,0:T(8,128)S(1)}, f32[128,32,128]{2,1,0:T(8,128)S(1)}, u32[]{:S(2)}, u32[]{:S(2)}) collective-permute-start(f32[128,32,128]{2,1,0:T(8,128)S(1)} %get-tuple-element.58.x0), channel_id=1, source_target_pairs={{0,16},{16,0},{32,48},{48,32},{64,80},{80,64},{96,112},{112,96},{1... | collective-permute-start | bytes 6291464 | tf_op jit(solution)/shard_map/ppermute | solution.py:316
  4.2 14.3 %collective-permute-start.5 = (f32[64,32,128]{2,1,0:T(8,128)S(1)}, f32[64,32,128]{2,1,0:T(8,128)S(1)}, u32[]{:S(2)}, u32[]{:S(2)}) collective-permute-start(f32[64,32,128]{2,1,0:T(8,128)S(1)} %shard_map.52.x3a), channel_id=1, source_target_pairs={{0,112},{16,32},{32,16},{48,64},{64,48},{80,96},{96,80},{112,0},{1... | collective-permute-start | bytes 3145736 | tf_op jit(solution)/shard_map/ppermute | solution.py:316
  4.8 12.5 %collective-permute-start.3 = (f32[4,128,128]{2,1,0:T(8,128)S(1)}, f32[4,128,128]{2,1,0:T(8,128)S(1)}, u32[]{:S(2)}, u32[]{:S(2)}) collective-permute-start(f32[4,128,128]{2,1,0:T(8,128)S(1)} %get-tuple-element.63), channel_id=1, source_target_pairs={{0,1},{1,2},{2,3},{3,0},{4,5},{5,6},{6,7},{7,4},{8,9},{9,10},{10,1... | collective-permute-start | bytes 786440 | tf_op jit(solution)/shard_map/ppermute | solution.py:305
  6.7 10.6 %collective-permute-start.4 = (f32[4,128,128]{2,1,0:T(8,128)S(1)}, f32[4,128,128]{2,1,0:T(8,128)S(1)}, u32[]{:S(2)}, u32[]{:S(2)}) collective-permute-start(f32[4,128,128]{2,1,0:T(8,128)S(1)} %get-tuple-element.64), channel_id=1, source_target_pairs={{0,3},{1,0},{2,1},{3,2},{4,7},{5,4},{6,5},{7,6},{8,11},{9,8},{10,9... | collective-permute-start | bytes 786440 | tf_op jit(solution)/shard_map/ppermute | solution.py:305
  6.8 6.0 %collective-permute-start.1 = (f32[4,32,128]{2,1,0:T(8,128)S(1)}, f32[4,32,128]{2,1,0:T(8,128)S(1)}, u32[]{:S(2)}, u32[]{:S(2)}) collective-permute-start(f32[4,32,128]{2,1,0:T(8,128)S(1)} %get-tuple-element.61), channel_id=1, source_target_pairs={{0,4},{4,8},{8,12},{12,0},{1,5},{5,9},{9,13},{13,1},{2,6},{6,10},{... | collective-permute-start | bytes 196616 | tf_op jit(solution)/shard_map/ppermute | solution.py:305
  12.8 4.4 %collective-permute-start.2 = (f32[4,32,128]{2,1,0:T(8,128)S(1)}, f32[4,32,128]{2,1,0:T(8,128)S(1)}, u32[]{:S(2)}, u32[]{:S(2)}) collective-permute-start(f32[4,32,128]{2,1,0:T(8,128)S(1)} %get-tuple-element.62), channel_id=1, source_target_pairs={{0,12},{4,0},{8,4},{12,8},{1,13},{5,1},{9,5},{13,9},{2,14},{6,2},{... | collective-permute-start | bytes 196616 | tf_op jit(solution)/shard_map/ppermute | solution.py:305
  25.6 31.3 %collective-permute-start.7 = (f32[128,32,128]{2,1,0:T(8,128)S(1)}, f32[128,32,128]{2,1,0:T(8,128)S(1)}, u32[]{:S(2)}, u32[]{:S(2)}) collective-permute-start(f32[128,32,128]{2,1,0:T(8,128)S(1)} %get-tuple-element.71.x0), channel_id=1, source_target_pairs={{0,16},{16,0},{32,48},{48,32},{64,80},{80,64},{96,112},{112,96},{1... | collective-permute-start | bytes 6291464 | tf_op jit(solution)/shard_map/ppermute | solution.py:316
  26.1 14.2 %collective-permute-start.6 = (f32[64,32,128]{2,1,0:T(8,128)S(1)}, f32[64,32,128]{2,1,0:T(8,128)S(1)}, u32[]{:S(2)}, u32[]{:S(2)}) collective-permute-start(f32[64,32,128]{2,1,0:T(8,128)S(1)} %get-tuple-element.60.x3b), channel_id=1, source_target_pairs={{0,112},{16,32},{32,16},{48,64},{64,48},{80,96},{96,80},{112,0},{1... | collective-permute-start | bytes 3145736 | tf_op jit(solution)/shard_map/ppermute | solution.py:316
  27.6 24.0 %collective-permute-start.12 = (f32[64,32,128]{2,1,0:T(8,128)S(1)}, f32[64,32,128]{2,1,0:T(8,128)S(1)}, u32[]{:S(2)}, u32[]{:S(2)}) collective-permute-start(f32[64,32,128]{2,1,0:T(8,128)S(1)} %get-tuple-element.74.x3a), channel_id=1, source_target_pairs={{0,112},{16,32},{32,16},{48,64},{64,48},{80,96},{96,80},{112,0},{1... | collective-permute-start | bytes 3145736 | tf_op jit(solution)/shard_map/ppermute | solution.py:316
  41.0 15.3 %collective-permute-start.10 = (f32[4,128,128]{2,1,0:T(8,128)S(1)}, f32[4,128,128]{2,1,0:T(8,128)S(1)}, u32[]{:S(2)}, u32[]{:S(2)}) collective-permute-start(f32[4,128,128]{2,1,0:T(8,128)S(1)} %get-tuple-element.82), channel_id=1, source_target_pairs={{0,1},{1,2},{2,3},{3,0},{4,5},{5,6},{6,7},{7,4},{8,9},{9,10},{10,1... | collective-permute-start | bytes 786440 | tf_op jit(solution)/shard_map/ppermute | solution.py:305
  43.0 13.3 %collective-permute-start.11 = (f32[4,128,128]{2,1,0:T(8,128)S(1)}, f32[4,128,128]{2,1,0:T(8,128)S(1)}, u32[]{:S(2)}, u32[]{:S(2)}) collective-permute-start(f32[4,128,128]{2,1,0:T(8,128)S(1)} %get-tuple-element.83), channel_id=1, source_target_pairs={{0,3},{1,0},{2,1},{3,2},{4,7},{5,4},{6,5},{7,6},{8,11},{9,8},{10,9... | collective-permute-start | bytes 786440 | tf_op jit(solution)/shard_map/ppermute | solution.py:305
  43.1 11.3 %collective-permute-start.8 = (f32[4,32,128]{2,1,0:T(8,128)S(1)}, f32[4,32,128]{2,1,0:T(8,128)S(1)}, u32[]{:S(2)}, u32[]{:S(2)}) collective-permute-start(f32[4,32,128]{2,1,0:T(8,128)S(1)} %get-tuple-element.80), channel_id=1, source_target_pairs={{0,4},{4,8},{8,12},{12,0},{1,5},{5,9},{9,13},{13,1},{2,6},{6,10},{... | collective-permute-start | bytes 196616 | tf_op jit(solution)/shard_map/ppermute | solution.py:305
  51.6 4.7 %collective-permute-start.9 = (f32[4,32,128]{2,1,0:T(8,128)S(1)}, f32[4,32,128]{2,1,0:T(8,128)S(1)}, u32[]{:S(2)}, u32[]{:S(2)}) collective-permute-start(f32[4,32,128]{2,1,0:T(8,128)S(1)} %get-tuple-element.81), channel_id=1, source_target_pairs={{0,12},{4,0},{8,4},{12,8},{1,13},{5,1},{9,5},{13,9},{2,14},{6,2},{... | collective-permute-start | bytes 196616 | tf_op jit(solution)/shard_map/ppermute | solution.py:305
  60.4 35.9 %collective-permute-start.23 = (f32[128,32,128]{2,1,0:T(8,128)S(1)}, f32[128,32,128]{2,1,0:T(8,128)S(1)}, u32[]{:S(2)}, u32[]{:S(2)}) collective-permute-start(f32[128,32,128]{2,1,0:T(8,128)S(1)} %get-tuple-element.105.x0), channel_id=1, source_target_pairs={{0,16},{16,0},{32,48},{48,32},{64,80},{80,64},{96,112},{112,96},{1... | collective-permute-start | bytes 6291464 | tf_op jit(solution)/shard_map/ppermute | solution.py:316
  60.5 17.1 %collective-permute-start.13 = (f32[64,32,128]{2,1,0:T(8,128)S(1)}, f32[64,32,128]{2,1,0:T(8,128)S(1)}, u32[]{:S(2)}, u32[]{:S(2)}) collective-permute-start(f32[64,32,128]{2,1,0:T(8,128)S(1)} %get-tuple-element.79.x3b), channel_id=1, source_target_pairs={{16,32},{32,16},{48,64},{64,48},{80,96},{96,80},{17,33},{33,17},{4... | collective-permute-start | bytes 3145736 | tf_op jit(solution)/shard_map/ppermute | solution.py:316
  65.1 41.0 %collective-permute-start.14 = (f32[64,32,128]{2,1,0:T(8,128)S(1)}, f32[64,32,128]{2,1,0:T(8,128)S(1)}, u32[]{:S(2)}, u32[]{:S(2)}) collective-permute-start(f32[64,32,128]{2,1,0:T(8,128)S(1)} %get-tuple-element.91.x3a), channel_id=1, source_target_pairs={{0,112},{16,32},{32,16},{48,64},{64,48},{80,96},{96,80},{112,0},{1... | collective-permute-start | bytes 3145736 | tf_op jit(solution)/shard_map/ppermute | solution.py:316
  78.2 28.7 %collective-permute-start.19 = (f32[64,32,128]{2,1,0:T(8,128)S(1)}, f32[64,32,128]{2,1,0:T(8,128)S(1)}, u32[]{:S(2)}, u32[]{:S(2)}) collective-permute-start(f32[64,32,128]{2,1,0:T(8,128)S(1)} %get-tuple-element.96.x3b), channel_id=1, source_target_pairs={{16,32},{32,16},{48,64},{64,48},{80,96},{96,80},{17,33},{33,17},{4... | collective-permute-start | bytes 3145736 | tf_op jit(solution)/shard_map/ppermute | solution.py:316
  82.1 5.9 %collective-permute-start.15 = (f32[4,32,128]{2,1,0:T(8,128)S(1)}, f32[4,32,128]{2,1,0:T(8,128)S(1)}, u32[]{:S(2)}, u32[]{:S(2)}) collective-permute-start(f32[4,32,128]{2,1,0:T(8,128)S(1)} %get-tuple-element.97), channel_id=1, source_target_pairs={{0,4},{4,8},{8,12},{12,0},{1,5},{5,9},{9,13},{13,1},{2,6},{6,10},{... | collective-permute-start | bytes 196616 | tf_op jit(solution)/shard_map/ppermute | solution.py:305
  83.3 6.6 %collective-permute-start.16 = (f32[4,32,128]{2,1,0:T(8,128)S(1)}, f32[4,32,128]{2,1,0:T(8,128)S(1)}, u32[]{:S(2)}, u32[]{:S(2)}) collective-permute-start(f32[4,32,128]{2,1,0:T(8,128)S(1)} %get-tuple-element.98), channel_id=1, source_target_pairs={{0,12},{4,0},{8,4},{12,8},{1,13},{5,1},{9,5},{13,9},{2,14},{6,2},{... | collective-permute-start | bytes 196616 | tf_op jit(solution)/shard_map/ppermute | solution.py:305
  88.0 6.6 %collective-permute-start.17 = (f32[4,128,128]{2,1,0:T(8,128)S(1)}, f32[4,128,128]{2,1,0:T(8,128)S(1)}, u32[]{:S(2)}, u32[]{:S(2)}) collective-permute-start(f32[4,128,128]{2,1,0:T(8,128)S(1)} %get-tuple-element.99), channel_id=1, source_target_pairs={{0,1},{1,2},{2,3},{3,0},{4,5},{5,6},{6,7},{7,4},{8,9},{9,10},{10,1... | collective-permute-start | bytes 786440 | tf_op jit(solution)/shard_map/ppermute | solution.py:305
  89.9 6.4 %collective-permute-start.18 = (f32[4,128,128]{2,1,0:T(8,128)S(1)}, f32[4,128,128]{2,1,0:T(8,128)S(1)}, u32[]{:S(2)}, u32[]{:S(2)}) collective-permute-start(f32[4,128,128]{2,1,0:T(8,128)S(1)} %get-tuple-element.100), channel_id=1, source_target_pairs={{0,3},{1,0},{2,1},{3,2},{4,7},{5,4},{6,5},{7,6},{8,11},{9,8},{10,9... | collective-permute-start | bytes 786440 | tf_op jit(solution)/shard_map/ppermute | solution.py:305
  101.7 7.9 %collective-permute-start.26 = (f32[2,3,32,128]{3,2,1,0:T(8,128)S(1)}, f32[2,3,32,128]{3,2,1,0:T(8,128)S(1)}, u32[]{:S(2)}, u32[]{:S(2)}) collective-permute-start(f32[2,3,32,128]{3,2,1,0:T(8,128)S(1)} %get-tuple-element.110.rest_0_), channel_id=1, source_target_pairs={{0,4},{4,8},{8,12},{12,0},{1,5},{5,9},{9,13},{13,1},{2,6},{6,10},{... | collective-permute-start | bytes 294920 | tf_op jit(solution)/shard_map/ppermute | solution.py:305
  101.8 10.4 %collective-permute-start.25 = (f32[2,3,32,128]{3,2,1,0:T(8,128)S(1)}, f32[2,3,32,128]{3,2,1,0:T(8,128)S(1)}, u32[]{:S(2)}, u32[]{:S(2)}) collective-permute-start(f32[2,3,32,128]{3,2,1,0:T(8,128)S(1)} %get-tuple-element.110.rest_0_), channel_id=1, source_target_pairs={{0,8},{4,12},{8,0},{12,4},{1,9},{5,13},{9,1},{13,5},{2,10},{6,14},... | collective-permute-start | bytes 294920 | tf_op jit(solution)/shard_map/ppermute | solution.py:305
  105.3 6.9 %collective-permute-start.24 = (f32[2,3,32,128]{3,2,1,0:T(8,128)S(1)}, f32[2,3,32,128]{3,2,1,0:T(8,128)S(1)}, u32[]{:S(2)}, u32[]{:S(2)}) collective-permute-start(f32[2,3,32,128]{3,2,1,0:T(8,128)S(1)} %get-tuple-element.110.rest_0_), channel_id=1, source_target_pairs={{0,12},{4,0},{8,4},{12,8},{1,13},{5,1},{9,5},{13,9},{2,14},{6,2},{... | collective-permute-start | bytes 294920 | tf_op jit(solution)/shard_map/ppermute | solution.py:305
  107.6 7.9 %collective-permute-start.22 = (f32[2,1,32,128]{3,2,1,0:T(8,128)S(1)}, f32[2,1,32,128]{3,2,1,0:T(8,128)S(1)}, u32[]{:S(2)}, u32[]{:S(2)}) collective-permute-start(f32[2,1,32,128]{3,2,1,0:T(8,128)S(1)} %get-tuple-element.104.rest_0_), channel_id=1, source_target_pairs={{0,4},{4,8},{8,12},{12,0},{1,5},{5,9},{9,13},{13,1},{2,6},{6,10},{... | collective-permute-start | bytes 98312 | tf_op jit(solution)/shard_map/ppermute | solution.py:305
  108.9 6.7 %collective-permute-start.21 = (f32[2,1,32,128]{3,2,1,0:T(8,128)S(1)}, f32[2,1,32,128]{3,2,1,0:T(8,128)S(1)}, u32[]{:S(2)}, u32[]{:S(2)}) collective-permute-start(f32[2,1,32,128]{3,2,1,0:T(8,128)S(1)} %get-tuple-element.104.rest_0_), channel_id=1, source_target_pairs={{0,8},{4,12},{8,0},{12,4},{1,9},{5,13},{9,1},{13,5},{2,10},{6,14},... | collective-permute-start | bytes 98312 | tf_op jit(solution)/shard_map/ppermute | solution.py:305
  109.6 6.0 %collective-permute-start.20 = (f32[2,1,32,128]{3,2,1,0:T(8,128)S(1)}, f32[2,1,32,128]{3,2,1,0:T(8,128)S(1)}, u32[]{:S(2)}, u32[]{:S(2)}) collective-permute-start(f32[2,1,32,128]{3,2,1,0:T(8,128)S(1)} %get-tuple-element.104.rest_0_), channel_id=1, source_target_pairs={{0,12},{4,0},{8,4},{12,8},{1,13},{5,1},{9,5},{13,9},{2,14},{6,2},{... | collective-permute-start | bytes 98312 | tf_op jit(solution)/shard_map/ppermute | solution.py:305

commit v3 on v2

--- a/solution.py
+++ b/solution.py
@@ -112,30 +112,36 @@
                 for (ref, first), k in zip(lev_outs, (0, NK - 1)):
                     ref[pl.ds(first + i0 + r, 1), :] = new[k : k + 1]
             if sums is not None:
-                shift, total, squares = carry
+                shift, total = carry
                 if r == 0 and sums[0] is None:
                     shift = jnp.where(b == 0, new, shift)
-                moved = new - shift
-                carry = (shift, total + moved, squares + moved * moved)
+                carry = (shift, total + (new - shift))
             prev, here = here, nxt
         return carry
 
     if sums is None:
         first = 0
     else:
-        first = (jnp.zeros((NK, NM), F32) if sums[0] is None else sums[0], *sums[1:])
+        first = (jnp.zeros((NK, NM), F32) if sums[0] is None else sums[0], sums[1])
     return lax.fori_loop(0, HALF // UNROLL, block, first)
 
 
-def put_stats(stats, p, sums):
-    shift, total, squares = sums
-    stats[0, p] = shift + total * (1.0 / NI)
-    stats[1, p] = squares - total * (total * (1.0 / NI))
+def moments(q, sums):
+    shift, total = sums
+    rows = q.shape[0]
+    mean = shift + total * (1.0 / rows)
+
+    def block(b, squares):
+        for r in range(UNROLL):
+            moved = q[b * UNROLL + r] - mean
+            squares = squares + moved * moved
+        return squares
+
+    return mean, lax.fori_loop(0, rows // UNROLL, block, jnp.zeros((NK, NM), F32))
 
 
 def no_sums():
-    zero = jnp.zeros((NK, NM), F32)
-    return (None, zero, zero)
+    return (None, jnp.zeros((NK, NM), F32))
 
 
 def inner_planes(xs, on, halo, cs, outs, faces=None, stats=None, ready=lambda p: None, done=lambda p, h: None):
@@ -161,7 +167,7 @@
             faces[0][p] = out[0]
             faces[1][p] = out[NI - 1]
         if stats is not None:
-            put_stats(stats, p, sums)
+            stats[0, p], stats[1, p] = moments(out, sums)
 
 
 def edge_half(h, x2, x3, cross, halo, c3, s3, out, faces=None, sums=None):
@@ -192,14 +198,13 @@
 
 
 def edge_a_last(x2, x3a, x3b, cross, ll, lh, vl, vh, c3, s3, out, raw):
-    sums = edge_half(0, x2, (x3a, x3b), cross, (ll, lh, vl, vh), c3, s3, out, None, no_sums())
-    for n in range(3):
-        raw[n] = sums[n]
+    raw[0], raw[1] = moments(out, edge_half(0, x2, (x3a, x3b), cross, (ll, lh, vl, vh), c3, s3, out, None, no_sums()))
 
 
 def edge_b_last(x2, x3a, x3b, cross, ll, lh, vl, vh, c3, s3, raw, out, stats):
-    sums = (raw[0], raw[1], raw[2])
-    put_stats(stats, 0, edge_half(1, x2, (x3a, x3b), cross, (ll, lh, vl, vh), c3, s3, out, None, sums))
+    mean, square = moments(out, edge_half(1, x2, (x3a, x3b), cross, (ll, lh, vl, vh), c3, s3, out, None, no_sums()))
+    stats[0, 0] = 0.5 * (raw[0] + mean)
+    stats[1, 0] = raw[1] + square + (0.5 * HALF) * ((raw[0] - mean) * (raw[0] - mean))
 
 
 def inner_first(
@@ -359,7 +364,7 @@
                 [plane] * 3 + [((2, 3, NK, NM), VMEM), ((NJ, *PLANE), HBM)], scratch=[dma((6,))],
             )
             inner_stats = of_everyone(stats)
-            qa, raw = call(edge_a_last, edge + vm(cross[0]) + rest, [half, ((3, NK, NM), VMEM)])
+            qa, raw = call(edge_a_last, edge + vm(cross[0]) + rest, [half, ((2, NK, NM), VMEM)])
             qb, stats = call(edge_b_last, edge + vm(cross[1]) + rest + vm(raw), [half, ((2, 1, NK, NM), VMEM)])
             edge_stats = of_everyone(stats)
         x0, x1, x2, x3a, x3b = q0, q1, q2, qa, qb

time: 118 us -> 119 us (level)
  no operation moved by 1% of the time
where the time goes in v3:
time: 119 us; the launch traced here: 117 us
  waiting for transfers between devices  48 us (40%)
  starting transfers between devices  37.8 us (32%)
  Pallas kernels  30.6 us (26%)
    ppermute x9, waiting for transfers between devices, swapped(): return lax.ppermute(q, 'lat', pairs)  33.1 us
    pallas_call x14, Pallas kernels, call(): pl.pallas_call(kernel, out_shape=tuple((space(shape, F32) for shape, spac...  30.6 us
    ppermute x18, starting transfers between devices, rotated(): return lax.ppermute(array, axis, [(i, (i + by) % n) for i in range(n)])  26.1 us
    ppermute x18, waiting for transfers between devices, rotated(): return lax.ppermute(array, axis, [(i, (i + by) % n) for i in range(n)])  14.9 us
    ppermute x9, starting transfers between devices, swapped(): return lax.ppermute(q, 'lat', pairs)  11.8 us
  transfers between devices with their start and end apart: 27, of which 9 were waited for; matrix products, arithmetic and copies ran while one was open for 0% of the time, Pallas kernels for 14%

profile of v3, /device:TPU:40, one launch (start us, length us, event | category | flops | bytes accessed | tf_op | source)
XLA Modules:
  0.0 117.3 jit_solution(16210006439616135017)
XLA Ops:
  0.6 2.2 %shard_map.50 = (f32[64,32,128]{2,1,0:T(8,128)S(1)}, f32[128,32,128]{2,1,0:T(8,128)S(1)}, f32[4,32,128]{2,1,0:T(8,128)S(1)}, f32[4,32,128]{2,1,0:T(8,128)S(1)}, ...) custom-call(f32[4,128,32,128]{3,2,1,0:T(8,128)} %tracer.7), custom_call_target="tpu_custom_call" | custom-call | tf_op jit(solution)/shard_map/pallas_call | solution.py:27
  2.8 0.1 collective-permute-start
  2.9 1.2 %shard_map.52.x3a = f32[64,32,128]{2,1,0:T(8,128)S(1)} custom-call(f32[4,128,32,128]{3,2,1,0:T(8,128)} %tracer.7), custom_call_target="tpu_custom_call" | custom-call | tf_op jit(solution)/shard_map/pallas_call | solution.py:27
  4.2 0.6 collective-permute-start.5
  4.8 1.9 %collective-permute-start.3 = (f32[4,128,128]{2,1,0:T(8,128)S(1)}, f32[4,128,128]{2,1,0:T(8,128)S(1)}, u32[]{:S(2)}, u32[]{:S(2)}) collective-permute-start(f32[4,128,128]{2,1,0:T(8,128)S(1)} %get-tuple-element.63), channel_id=1, source_target_pairs={{0,1},{1,2},{2,3},{3,0},{4,5},{5,6},{6,7},{7,4},{8,9},{9,10},{10,1... | collective-permute-start | bytes 786440 | tf_op jit(solution)/shard_map/ppermute | solution.py:310
  6.7 0.1 collective-permute-start.4
  6.8 1.5 %collective-permute-start.1 = (f32[4,32,128]{2,1,0:T(8,128)S(1)}, f32[4,32,128]{2,1,0:T(8,128)S(1)}, u32[]{:S(2)}, u32[]{:S(2)}) collective-permute-start(f32[4,32,128]{2,1,0:T(8,128)S(1)} %get-tuple-element.61), channel_id=1, source_target_pairs={{0,4},{4,8},{8,12},{12,0},{1,5},{5,9},{9,13},{13,1},{2,6},{6,10},{... | collective-permute-start | bytes 196616 | tf_op jit(solution)/shard_map/ppermute | solution.py:310
  8.3 4.5 %collective-permute-done.1.ll = f32[4,32,128]{2,1,0:T(8,128)S(1)} collective-permute-done((f32[4,32,128]{2,1,0:T(8,128)S(1)}, f32[4,32,128]{2,1,0:T(8,128)S(1)}, u32[]{:S(2)}, u32[]{:S(2)}) %collective-permute-start.1) | collective-permute-done | bytes 65568 | tf_op jit(solution)/shard_map/ppermute | solution.py:310
  12.8 1.5 %collective-permute-start.2 = (f32[4,32,128]{2,1,0:T(8,128)S(1)}, f32[4,32,128]{2,1,0:T(8,128)S(1)}, u32[]{:S(2)}, u32[]{:S(2)}) collective-permute-start(f32[4,32,128]{2,1,0:T(8,128)S(1)} %get-tuple-element.62), channel_id=1, source_target_pairs={{0,12},{4,0},{8,4},{12,8},{1,13},{5,1},{9,5},{13,9},{2,14},{6,2},{... | collective-permute-start | bytes 196616 | tf_op jit(solution)/shard_map/ppermute | solution.py:310
  14.4 2.9 %shard_map.51 = (f32[128,32,128]{2,1,0:T(8,128)S(1)}, f32[128,32,128]{2,1,0:T(8,128)S(1)}, f32[128,32,128]{2,1,0:T(8,128)S(1)}) custom-call(f32[4,128,32,128]{3,2,1,0:T(8,128)} %tracer.7, f32[4,128,32,128]{3,2,1,0:T(8,128)} %c.3, f32[4,128,32,128]{3,2,1,0:T(8,128)} %s.3), custom_call_target="tpu_custom_call" | custom-call | tf_op jit(solution)/shard_map/pallas_call | solution.py:27
  17.3 1.2 %collective-permute-done.5.cross = f32[64,32,128]{2,1,0:T(8,128)S(1)} collective-permute-done((f32[64,32,128]{2,1,0:T(8,128)S(1)}, f32[64,32,128]{2,1,0:T(8,128)S(1)}, u32[]{:S(2)}, u32[]{:S(2)}) %collective-permute-start.5) | collective-permute-done | bytes 1048608 | tf_op jit(solution)/shard_map/ppermute | solution.py:321
  18.5 0.6 shard_map.53
  19.1 6.5 %shard_map.54 = (f32[128,32,128]{2,1,0:T(8,128)S(1)}, f32[128,32,128]{2,1,0:T(8,128)S(1)}, f32[128,32,128]{2,1,0:T(8,128)S(1)}, f32[4,32,128]{2,1,0:T(8,128)S(1)...) custom-call(f32[4,128,32,128]{3,2,1,0:T(8,128)} %tracer.7, ...), custom_call_target="tpu_custom_call", output_to_operand_aliasing={{3}: (12, {}), {4}: (13, {}), {5}: (14, {}), {6}: (15, {})} | custom-call | tf_op jit(solution)/shard_map/pallas_call | solution.py:27
  25.6 0.6 collective-permute-start.7
  26.1 1.4 %collective-permute-start.6 = (f32[64,32,128]{2,1,0:T(8,128)S(1)}, f32[64,32,128]{2,1,0:T(8,128)S(1)}, u32[]{:S(2)}, u32[]{:S(2)}) collective-permute-start(f32[64,32,128]{2,1,0:T(8,128)S(1)} %get-tuple-element.60.x3b), channel_id=1, source_target_pairs={{0,112},{16,32},{32,16},{48,64},{64,48},{80,96},{96,80},{112,0},{1... | collective-permute-start | bytes 3145736 | tf_op jit(solution)/shard_map/ppermute | solution.py:321
  27.6 0.3 collective-permute-start.12
  27.9 12.5 %collective-permute-done.6.cross = f32[64,32,128]{2,1,0:T(8,128)S(1)} collective-permute-done((f32[64,32,128]{2,1,0:T(8,128)S(1)}, f32[64,32,128]{2,1,0:T(8,128)S(1)}, u32[]{:S(2)}, u32[]{:S(2)}) %collective-permute-start.6) | collective-permute-done | bytes 1048608 | tf_op jit(solution)/shard_map/ppermute | solution.py:321
  40.4 0.6 shard_map.55
  41.0 2.0 %collective-permute-start.10 = (f32[4,128,128]{2,1,0:T(8,128)S(1)}, f32[4,128,128]{2,1,0:T(8,128)S(1)}, u32[]{:S(2)}, u32[]{:S(2)}) collective-permute-start(f32[4,128,128]{2,1,0:T(8,128)S(1)} %get-tuple-element.82), channel_id=1, source_target_pairs={{0,1},{1,2},{2,3},{3,0},{4,5},{5,6},{6,7},{7,4},{8,9},{9,10},{10,1... | collective-permute-start | bytes 786440 | tf_op jit(solution)/shard_map/ppermute | solution.py:310
  43.0 0.1 collective-permute-start.11
  43.1 1.5 %collective-permute-start.8 = (f32[4,32,128]{2,1,0:T(8,128)S(1)}, f32[4,32,128]{2,1,0:T(8,128)S(1)}, u32[]{:S(2)}, u32[]{:S(2)}) collective-permute-start(f32[4,32,128]{2,1,0:T(8,128)S(1)} %get-tuple-element.80), channel_id=1, source_target_pairs={{0,4},{4,8},{8,12},{12,0},{1,5},{5,9},{9,13},{13,1},{2,6},{6,10},{... | collective-permute-start | bytes 196616 | tf_op jit(solution)/shard_map/ppermute | solution.py:310
  44.6 7.1 %collective-permute-done.12.cross = f32[64,32,128]{2,1,0:T(8,128)S(1)} collective-permute-done((f32[64,32,128]{2,1,0:T(8,128)S(1)}, f32[64,32,128]{2,1,0:T(8,128)S(1)}, u32[]{:S(2)}, u32[]{:S(2)}) %collective-permute-start.12) | collective-permute-done | bytes 1048608 | tf_op jit(solution)/shard_map/ppermute | solution.py:321
  51.6 2.8 %collective-permute-start.9 = (f32[4,32,128]{2,1,0:T(8,128)S(1)}, f32[4,32,128]{2,1,0:T(8,128)S(1)}, u32[]{:S(2)}, u32[]{:S(2)}) collective-permute-start(f32[4,32,128]{2,1,0:T(8,128)S(1)} %get-tuple-element.81), channel_id=1, source_target_pairs={{0,12},{4,0},{8,4},{12,8},{1,13},{5,1},{9,5},{13,9},{2,14},{6,2},{... | collective-permute-start | bytes 196616 | tf_op jit(solution)/shard_map/ppermute | solution.py:310
  54.4 1.9 %collective-permute-done.9.lh = f32[4,32,128]{2,1,0:T(8,128)S(1)} collective-permute-done((f32[4,32,128]{2,1,0:T(8,128)S(1)}, f32[4,32,128]{2,1,0:T(8,128)S(1)}, u32[]{:S(2)}, u32[]{:S(2)}) %collective-permute-start.9) | collective-permute-done | bytes 65568 | tf_op jit(solution)/shard_map/ppermute | solution.py:310
  56.3 0.6 shard_map.56
  56.9 3.5 %shard_map.57 = (f32[128,32,128]{2,1,0:T(8,128)S(1)}, f32[128,32,128]{2,1,0:T(8,128)S(1)}, f32[128,32,128]{2,1,0:T(8,128)S(1)}, f32[4,32,128]{2,1,0:T(8,128)S(1)...) custom-call(f32[128,32,128]{2,1,0:T(8,128)S(1)} %get-tuple-element.7, ...), custom_call_target="tpu_custom_call", output_to_operand_aliasing={{3}: (12, {}), {4}: (13, {}), {5}: (14, {}), {6}: (15, {})} | custom-call | tf_op jit(solution)/shard_map/pallas_call | solution.py:27
  60.5 4.6 %collective-permute-start.13 = (f32[64,32,128]{2,1,0:T(8,128)S(1)}, f32[64,32,128]{2,1,0:T(8,128)S(1)}, u32[]{:S(2)}, u32[]{:S(2)}) collective-permute-start(f32[64,32,128]{2,1,0:T(8,128)S(1)} %get-tuple-element.79.x3b), channel_id=1, source_target_pairs={{16,32},{32,16},{48,64},{64,48},{80,96},{96,80},{17,33},{33,17},{4... | collective-permute-start | bytes 3145736 | tf_op jit(solution)/shard_map/ppermute | solution.py:321
  65.1 0.1 collective-permute-start.14
  65.2 12.4 %collective-permute-done.13.cross = f32[64,32,128]{2,1,0:T(8,128)S(1)} collective-permute-done((f32[64,32,128]{2,1,0:T(8,128)S(1)}, f32[64,32,128]{2,1,0:T(8,128)S(1)}, u32[]{:S(2)}, u32[]{:S(2)}) %collective-permute-start.13) | collective-permute-done | bytes 1048608 | tf_op jit(solution)/shard_map/ppermute | solution.py:321
  77.6 0.6 shard_map.58
  78.2 3.9 %collective-permute-start.19 = (f32[64,32,128]{2,1,0:T(8,128)S(1)}, f32[64,32,128]{2,1,0:T(8,128)S(1)}, u32[]{:S(2)}, u32[]{:S(2)}) collective-permute-start(f32[64,32,128]{2,1,0:T(8,128)S(1)} %get-tuple-element.96.x3b), channel_id=1, source_target_pairs={{16,32},{32,16},{48,64},{64,48},{80,96},{96,80},{17,33},{33,17},{4... | collective-permute-start | bytes 3145736 | tf_op jit(solution)/shard_map/ppermute | solution.py:321
  82.1 1.2 collective-permute-start.15
  83.3 2.6 %collective-permute-start.16 = (f32[4,32,128]{2,1,0:T(8,128)S(1)}, f32[4,32,128]{2,1,0:T(8,128)S(1)}, u32[]{:S(2)}, u32[]{:S(2)}) collective-permute-start(f32[4,32,128]{2,1,0:T(8,128)S(1)} %get-tuple-element.98), channel_id=1, source_target_pairs={{0,12},{4,0},{8,4},{12,8},{1,13},{5,1},{9,5},{13,9},{2,14},{6,2},{... | collective-permute-start | bytes 196616 | tf_op jit(solution)/shard_map/ppermute | solution.py:310
  85.9 2.2 %collective-permute-done.15.ll = f32[4,32,128]{2,1,0:T(8,128)S(1)} collective-permute-done((f32[4,32,128]{2,1,0:T(8,128)S(1)}, f32[4,32,128]{2,1,0:T(8,128)S(1)}, u32[]{:S(2)}, u32[]{:S(2)}) %collective-permute-start.15) | collective-permute-done | bytes 65568 | tf_op jit(solution)/shard_map/ppermute | solution.py:310
  88.0 1.9 %collective-permute-start.17 = (f32[4,128,128]{2,1,0:T(8,128)S(1)}, f32[4,128,128]{2,1,0:T(8,128)S(1)}, u32[]{:S(2)}, u32[]{:S(2)}) collective-permute-start(f32[4,128,128]{2,1,0:T(8,128)S(1)} %get-tuple-element.99), channel_id=1, source_target_pairs={{0,1},{1,2},{2,3},{3,0},{4,5},{5,6},{6,7},{7,4},{8,9},{9,10},{10,1... | collective-permute-start | bytes 786440 | tf_op jit(solution)/shard_map/ppermute | solution.py:310
  89.9 0.1 collective-permute-start.18
  90.1 4.6 %collective-permute-done.17.vl = f32[4,128,128]{2,1,0:T(8,128)S(1)} collective-permute-done((f32[4,128,128]{2,1,0:T(8,128)S(1)}, f32[4,128,128]{2,1,0:T(8,128)S(1)}, u32[]{:S(2)}, u32[]{:S(2)}) %collective-permute-start.17) | collective-permute-done | bytes 262176 | tf_op jit(solution)/shard_map/ppermute | solution.py:310
  94.6 1.7 %collective-permute-done.18.vh = f32[4,128,128]{2,1,0:T(8,128)S(1)} collective-permute-done((f32[4,128,128]{2,1,0:T(8,128)S(1)}, f32[4,128,128]{2,1,0:T(8,128)S(1)}, u32[]{:S(2)}, u32[]{:S(2)}) %collective-permute-start.18) | collective-permute-done | bytes 262176 | tf_op jit(solution)/shard_map/ppermute | solution.py:310
  96.3 5.5 %shard_map.61 = (f32[128,32,128]{2,1,0:T(8,128)S(1)}, f32[128,32,128]{2,1,0:T(8,128)S(1)}, f32[128,32,128]{2,1,0:T(8,128)S(1)}, f32[2,3,32,128]{3,2,1,0:T(8,128)S(1)}, f32[4,128,32,128]{3,2,1,0:T(8,128)}) custom-call(f32[128,32,128]{2,1,0:T(8,128)S(1)} %get-tuple-element.105.x0, f32[128,32,128]{2,1,0:T(8,128)S(1)} %get-tuple-element.106.x1, ...), custom_call_target="tpu_custom_call" | custom-call | tf_op jit(solution)/shard_map/pallas_call | solution.py:27
  101.9 3.5 %collective-permute-start.25 = (f32[2,3,32,128]{3,2,1,0:T(8,128)S(1)}, f32[2,3,32,128]{3,2,1,0:T(8,128)S(1)}, u32[]{:S(2)}, u32[]{:S(2)}) collective-permute-start(f32[2,3,32,128]{3,2,1,0:T(8,128)S(1)} %get-tuple-element.110.rest_0_), channel_id=1, source_target_pairs={{0,8},{4,12},{8,0},{12,4},{1,9},{5,13},{9,1},{13,5},{2,10},{6,14},... | collective-permute-start | bytes 294920 | tf_op jit(solution)/shard_map/ppermute | solution.py:310
  105.4 0.9 collective-permute-start.24
  106.2 0.8 shard_map.59
  107.1 0.8 shard_map.60
  107.9 1.2 %collective-permute-start.22 = (f32[2,1,32,128]{3,2,1,0:T(8,128)S(1)}, f32[2,1,32,128]{3,2,1,0:T(8,128)S(1)}, u32[]{:S(2)}, u32[]{:S(2)}) collective-permute-start(f32[2,1,32,128]{3,2,1,0:T(8,128)S(1)} %get-tuple-element.104.rest_0_), channel_id=1, source_target_pairs={{0,4},{4,8},{8,12},{12,0},{1,5},{5,9},{9,13},{13,1},{2,6},{6,10},{... | collective-permute-start | bytes 98312 | tf_op jit(solution)/shard_map/ppermute | solution.py:310
  109.1 0.7 collective-permute-start.21
  109.9 2.5 %collective-permute-start.20 = (f32[2,1,32,128]{3,2,1,0:T(8,128)S(1)}, f32[2,1,32,128]{3,2,1,0:T(8,128)S(1)}, u32[]{:S(2)}, u32[]{:S(2)}) collective-permute-start(f32[2,1,32,128]{3,2,1,0:T(8,128)S(1)} %get-tuple-element.104.rest_0_), channel_id=1, source_target_pairs={{0,12},{4,0},{8,4},{12,8},{1,13},{5,1},{9,5},{13,9},{2,14},{6,2},{... | collective-permute-start | bytes 98312 | tf_op jit(solution)/shard_map/ppermute | solution.py:310
  112.4 3.4 %shard_map.62 = (f32[4,128,32,128]{3,2,1,0:T(8,128)}, f32[4,128,32,128]{3,2,1,0:T(8,128)}) custom-call(f32[128,32,128]{2,1,0:T(8,128)S(1)} %get-tuple-element.107.q0, f32[128,32,128]{2,1,0:T(8,128)S(1)} %get-tuple-element.108.q1, f32[128,32,128]{2,1,0:T(8,128)S(1)} %get-tuple-element.109.q2, ...), custom_call_target="tpu_custom_call", output_to_operand_aliasing={{1}: (9, {})} | custom-call | tf_op jit(solution)/shard_map/pallas_call | solution.py:27
  115.8 1.4 %shard_map.63 = f32[4,128,32,128]{3,2,1,0:T(8,128)} custom-call(f32[64,32,128]{2,1,0:T(8,128)S(1)} %get-tuple-element.101.q3a, f32[64,32,128]{2,1,0:T(8,128)S(1)} %get-tuple-element.103.q3b, f32[2,1,32,128]{3,2,1,0:T(8,128)S(1)} %get-tuple-element.104.rest_0_, f32[2,1,32,128]{3,2,1,0:T(8,128)S(1)} %collective-permute-done.20.rest_1_, ...), custom_call_target="tpu_custom_call", output_to_operand_aliasing={{}: (6, {})} | custom-call | tf_op jit(solution)/shard_map/pallas_call | solution.py:27
  (20 shorter events, 0.2 us)
Async XLA Ops:
  2.8 16.2 %collective-permute-start = (f32[128,32,128]{2,1,0:T(8,128)S(1)}, f32[128,32,128]{2,1,0:T(8,128)S(1)}, u32[]{:S(2)}, u32[]{:S(2)}) collective-permute-start(f32[128,32,128]{2,1,0:T(8,128)S(1)} %get-tuple-element.58.x0), channel_id=1, source_target_pairs={{0,16},{16,0},{32,48},{48,32},{64,80},{80,64},{96,112},{112,96},{1... | collective-permute-start | bytes 6291464 | tf_op jit(solution)/shard_map/ppermute | solution.py:321
  4.2 14.3 %collective-permute-start.5 = (f32[64,32,128]{2,1,0:T(8,128)S(1)}, f32[64,32,128]{2,1,0:T(8,128)S(1)}, u32[]{:S(2)}, u32[]{:S(2)}) collective-permute-start(f32[64,32,128]{2,1,0:T(8,128)S(1)} %shard_map.52.x3a), channel_id=1, source_target_pairs={{0,112},{16,32},{32,16},{48,64},{64,48},{80,96},{96,80},{112,0},{1... | collective-permute-start | bytes 3145736 | tf_op jit(solution)/shard_map/ppermute | solution.py:321
  4.8 12.5 %collective-permute-start.3 = (f32[4,128,128]{2,1,0:T(8,128)S(1)}, f32[4,128,128]{2,1,0:T(8,128)S(1)}, u32[]{:S(2)}, u32[]{:S(2)}) collective-permute-start(f32[4,128,128]{2,1,0:T(8,128)S(1)} %get-tuple-element.63), channel_id=1, source_target_pairs={{0,1},{1,2},{2,3},{3,0},{4,5},{5,6},{6,7},{7,4},{8,9},{9,10},{10,1... | collective-permute-start | bytes 786440 | tf_op jit(solution)/shard_map/ppermute | solution.py:310
  6.7 10.6 %collective-permute-start.4 = (f32[4,128,128]{2,1,0:T(8,128)S(1)}, f32[4,128,128]{2,1,0:T(8,128)S(1)}, u32[]{:S(2)}, u32[]{:S(2)}) collective-permute-start(f32[4,128,128]{2,1,0:T(8,128)S(1)} %get-tuple-element.64), channel_id=1, source_target_pairs={{0,3},{1,0},{2,1},{3,2},{4,7},{5,4},{6,5},{7,6},{8,11},{9,8},{10,9... | collective-permute-start | bytes 786440 | tf_op jit(solution)/shard_map/ppermute | solution.py:310
  6.8 6.0 %collective-permute-start.1 = (f32[4,32,128]{2,1,0:T(8,128)S(1)}, f32[4,32,128]{2,1,0:T(8,128)S(1)}, u32[]{:S(2)}, u32[]{:S(2)}) collective-permute-start(f32[4,32,128]{2,1,0:T(8,128)S(1)} %get-tuple-element.61), channel_id=1, source_target_pairs={{0,4},{4,8},{8,12},{12,0},{1,5},{5,9},{9,13},{13,1},{2,6},{6,10},{... | collective-permute-start | bytes 196616 | tf_op jit(solution)/shard_map/ppermute | solution.py:310
  12.8 4.4 %collective-permute-start.2 = (f32[4,32,128]{2,1,0:T(8,128)S(1)}, f32[4,32,128]{2,1,0:T(8,128)S(1)}, u32[]{:S(2)}, u32[]{:S(2)}) collective-permute-start(f32[4,32,128]{2,1,0:T(8,128)S(1)} %get-tuple-element.62), channel_id=1, source_target_pairs={{0,12},{4,0},{8,4},{12,8},{1,13},{5,1},{9,5},{13,9},{2,14},{6,2},{... | collective-permute-start | bytes 196616 | tf_op jit(solution)/shard_map/ppermute | solution.py:310
  25.6 31.3 %collective-permute-start.7 = (f32[128,32,128]{2,1,0:T(8,128)S(1)}, f32[128,32,128]{2,1,0:T(8,128)S(1)}, u32[]{:S(2)}, u32[]{:S(2)}) collective-permute-start(f32[128,32,128]{2,1,0:T(8,128)S(1)} %get-tuple-element.71.x0), channel_id=1, source_target_pairs={{0,16},{16,0},{32,48},{48,32},{64,80},{80,64},{96,112},{112,96},{1... | collective-permute-start | bytes 6291464 | tf_op jit(solution)/shard_map/ppermute | solution.py:321
  26.1 14.2 %collective-permute-start.6 = (f32[64,32,128]{2,1,0:T(8,128)S(1)}, f32[64,32,128]{2,1,0:T(8,128)S(1)}, u32[]{:S(2)}, u32[]{:S(2)}) collective-permute-start(f32[64,32,128]{2,1,0:T(8,128)S(1)} %get-tuple-element.60.x3b), channel_id=1, source_target_pairs={{0,112},{16,32},{32,16},{48,64},{64,48},{80,96},{96,80},{112,0},{1... | collective-permute-start | bytes 3145736 | tf_op jit(solution)/shard_map/ppermute | solution.py:321
  27.6 24.0 %collective-permute-start.12 = (f32[64,32,128]{2,1,0:T(8,128)S(1)}, f32[64,32,128]{2,1,0:T(8,128)S(1)}, u32[]{:S(2)}, u32[]{:S(2)}) collective-permute-start(f32[64,32,128]{2,1,0:T(8,128)S(1)} %get-tuple-element.74.x3a), channel_id=1, source_target_pairs={{0,112},{16,32},{32,16},{48,64},{64,48},{80,96},{96,80},{112,0},{1... | collective-permute-start | bytes 3145736 | tf_op jit(solution)/shard_map/ppermute | solution.py:321
  41.0 15.3 %collective-permute-start.10 = (f32[4,128,128]{2,1,0:T(8,128)S(1)}, f32[4,128,128]{2,1,0:T(8,128)S(1)}, u32[]{:S(2)}, u32[]{:S(2)}) collective-permute-start(f32[4,128,128]{2,1,0:T(8,128)S(1)} %get-tuple-element.82), channel_id=1, source_target_pairs={{0,1},{1,2},{2,3},{3,0},{4,5},{5,6},{6,7},{7,4},{8,9},{9,10},{10,1... | collective-permute-start | bytes 786440 | tf_op jit(solution)/shard_map/ppermute | solution.py:310
  43.0 13.3 %collective-permute-start.11 = (f32[4,128,128]{2,1,0:T(8,128)S(1)}, f32[4,128,128]{2,1,0:T(8,128)S(1)}, u32[]{:S(2)}, u32[]{:S(2)}) collective-permute-start(f32[4,128,128]{2,1,0:T(8,128)S(1)} %get-tuple-element.83), channel_id=1, source_target_pairs={{0,3},{1,0},{2,1},{3,2},{4,7},{5,4},{6,5},{7,6},{8,11},{9,8},{10,9... | collective-permute-start | bytes 786440 | tf_op jit(solution)/shard_map/ppermute | solution.py:310
  43.1 11.3 %collective-permute-start.8 = (f32[4,32,128]{2,1,0:T(8,128)S(1)}, f32[4,32,128]{2,1,0:T(8,128)S(1)}, u32[]{:S(2)}, u32[]{:S(2)}) collective-permute-start(f32[4,32,128]{2,1,0:T(8,128)S(1)} %get-tuple-element.80), channel_id=1, source_target_pairs={{0,4},{4,8},{8,12},{12,0},{1,5},{5,9},{9,13},{13,1},{2,6},{6,10},{... | collective-permute-start | bytes 196616 | tf_op jit(solution)/shard_map/ppermute | solution.py:310
  51.6 4.7 %collective-permute-start.9 = (f32[4,32,128]{2,1,0:T(8,128)S(1)}, f32[4,32,128]{2,1,0:T(8,128)S(1)}, u32[]{:S(2)}, u32[]{:S(2)}) collective-permute-start(f32[4,32,128]{2,1,0:T(8,128)S(1)} %get-tuple-element.81), channel_id=1, source_target_pairs={{0,12},{4,0},{8,4},{12,8},{1,13},{5,1},{9,5},{13,9},{2,14},{6,2},{... | collective-permute-start | bytes 196616 | tf_op jit(solution)/shard_map/ppermute | solution.py:310
  60.4 35.9 %collective-permute-start.23 = (f32[128,32,128]{2,1,0:T(8,128)S(1)}, f32[128,32,128]{2,1,0:T(8,128)S(1)}, u32[]{:S(2)}, u32[]{:S(2)}) collective-permute-start(f32[128,32,128]{2,1,0:T(8,128)S(1)} %get-tuple-element.105.x0), channel_id=1, source_target_pairs={{0,16},{16,0},{32,48},{48,32},{64,80},{80,64},{96,112},{112,96},{1... | collective-permute-start | bytes 6291464 | tf_op jit(solution)/shard_map/ppermute | solution.py:321
  60.5 17.1 %collective-permute-start.13 = (f32[64,32,128]{2,1,0:T(8,128)S(1)}, f32[64,32,128]{2,1,0:T(8,128)S(1)}, u32[]{:S(2)}, u32[]{:S(2)}) collective-permute-start(f32[64,32,128]{2,1,0:T(8,128)S(1)} %get-tuple-element.79.x3b), channel_id=1, source_target_pairs={{16,32},{32,16},{48,64},{64,48},{80,96},{96,80},{17,33},{33,17},{4... | collective-permute-start | bytes 3145736 | tf_op jit(solution)/shard_map/ppermute | solution.py:321
  65.1 41.1 %collective-permute-start.14 = (f32[64,32,128]{2,1,0:T(8,128)S(1)}, f32[64,32,128]{2,1,0:T(8,128)S(1)}, u32[]{:S(2)}, u32[]{:S(2)}) collective-permute-start(f32[64,32,128]{2,1,0:T(8,128)S(1)} %get-tuple-element.91.x3a), channel_id=1, source_target_pairs={{0,112},{16,32},{32,16},{48,64},{64,48},{80,96},{96,80},{112,0},{1... | collective-permute-start | bytes 3145736 | tf_op jit(solution)/shard_map/ppermute | solution.py:321
  78.2 28.9 %collective-permute-start.19 = (f32[64,32,128]{2,1,0:T(8,128)S(1)}, f32[64,32,128]{2,1,0:T(8,128)S(1)}, u32[]{:S(2)}, u32[]{:S(2)}) collective-permute-start(f32[64,32,128]{2,1,0:T(8,128)S(1)} %get-tuple-element.96.x3b), channel_id=1, source_target_pairs={{16,32},{32,16},{48,64},{64,48},{80,96},{96,80},{17,33},{33,17},{4... | collective-permute-start | bytes 3145736 | tf_op jit(solution)/shard_map/ppermute | solution.py:321
  82.1 5.9 %collective-permute-start.15 = (f32[4,32,128]{2,1,0:T(8,128)S(1)}, f32[4,32,128]{2,1,0:T(8,128)S(1)}, u32[]{:S(2)}, u32[]{:S(2)}) collective-permute-start(f32[4,32,128]{2,1,0:T(8,128)S(1)} %get-tuple-element.97), channel_id=1, source_target_pairs={{0,4},{4,8},{8,12},{12,0},{1,5},{5,9},{9,13},{13,1},{2,6},{6,10},{... | collective-permute-start | bytes 196616 | tf_op jit(solution)/shard_map/ppermute | solution.py:310
  83.3 6.6 %collective-permute-start.16 = (f32[4,32,128]{2,1,0:T(8,128)S(1)}, f32[4,32,128]{2,1,0:T(8,128)S(1)}, u32[]{:S(2)}, u32[]{:S(2)}) collective-permute-start(f32[4,32,128]{2,1,0:T(8,128)S(1)} %get-tuple-element.98), channel_id=1, source_target_pairs={{0,12},{4,0},{8,4},{12,8},{1,13},{5,1},{9,5},{13,9},{2,14},{6,2},{... | collective-permute-start | bytes 196616 | tf_op jit(solution)/shard_map/ppermute | solution.py:310
  88.0 6.6 %collective-permute-start.17 = (f32[4,128,128]{2,1,0:T(8,128)S(1)}, f32[4,128,128]{2,1,0:T(8,128)S(1)}, u32[]{:S(2)}, u32[]{:S(2)}) collective-permute-start(f32[4,128,128]{2,1,0:T(8,128)S(1)} %get-tuple-element.99), channel_id=1, source_target_pairs={{0,1},{1,2},{2,3},{3,0},{4,5},{5,6},{6,7},{7,4},{8,9},{9,10},{10,1... | collective-permute-start | bytes 786440 | tf_op jit(solution)/shard_map/ppermute | solution.py:310
  89.9 6.4 %collective-permute-start.18 = (f32[4,128,128]{2,1,0:T(8,128)S(1)}, f32[4,128,128]{2,1,0:T(8,128)S(1)}, u32[]{:S(2)}, u32[]{:S(2)}) collective-permute-start(f32[4,128,128]{2,1,0:T(8,128)S(1)} %get-tuple-element.100), channel_id=1, source_target_pairs={{0,3},{1,0},{2,1},{3,2},{4,7},{5,4},{6,5},{7,6},{8,11},{9,8},{10,9... | collective-permute-start | bytes 786440 | tf_op jit(solution)/shard_map/ppermute | solution.py:310
  101.8 8.0 %collective-permute-start.26 = (f32[2,3,32,128]{3,2,1,0:T(8,128)S(1)}, f32[2,3,32,128]{3,2,1,0:T(8,128)S(1)}, u32[]{:S(2)}, u32[]{:S(2)}) collective-permute-start(f32[2,3,32,128]{3,2,1,0:T(8,128)S(1)} %get-tuple-element.110.rest_0_), channel_id=1, source_target_pairs={{0,4},{4,8},{8,12},{12,0},{1,5},{5,9},{9,13},{13,1},{2,6},{6,10},{... | collective-permute-start | bytes 294920 | tf_op jit(solution)/shard_map/ppermute | solution.py:310
  101.9 10.5 %collective-permute-start.25 = (f32[2,3,32,128]{3,2,1,0:T(8,128)S(1)}, f32[2,3,32,128]{3,2,1,0:T(8,128)S(1)}, u32[]{:S(2)}, u32[]{:S(2)}) collective-permute-start(f32[2,3,32,128]{3,2,1,0:T(8,128)S(1)} %get-tuple-element.110.rest_0_), channel_id=1, source_target_pairs={{0,8},{4,12},{8,0},{12,4},{1,9},{5,13},{9,1},{13,5},{2,10},{6,14},... | collective-permute-start | bytes 294920 | tf_op jit(solution)/shard_map/ppermute | solution.py:310
  105.4 7.0 %collective-permute-start.24 = (f32[2,3,32,128]{3,2,1,0:T(8,128)S(1)}, f32[2,3,32,128]{3,2,1,0:T(8,128)S(1)}, u32[]{:S(2)}, u32[]{:S(2)}) collective-permute-start(f32[2,3,32,128]{3,2,1,0:T(8,128)S(1)} %get-tuple-element.110.rest_0_), channel_id=1, source_target_pairs={{0,12},{4,0},{8,4},{12,8},{1,13},{5,1},{9,5},{13,9},{2,14},{6,2},{... | collective-permute-start | bytes 294920 | tf_op jit(solution)/shard_map/ppermute | solution.py:310
  107.9 7.9 %collective-permute-start.22 = (f32[2,1,32,128]{3,2,1,0:T(8,128)S(1)}, f32[2,1,32,128]{3,2,1,0:T(8,128)S(1)}, u32[]{:S(2)}, u32[]{:S(2)}) collective-permute-start(f32[2,1,32,128]{3,2,1,0:T(8,128)S(1)} %get-tuple-element.104.rest_0_), channel_id=1, source_target_pairs={{0,4},{4,8},{8,12},{12,0},{1,5},{5,9},{9,13},{13,1},{2,6},{6,10},{... | collective-permute-start | bytes 98312 | tf_op jit(solution)/shard_map/ppermute | solution.py:310
  109.1 6.7 %collective-permute-start.21 = (f32[2,1,32,128]{3,2,1,0:T(8,128)S(1)}, f32[2,1,32,128]{3,2,1,0:T(8,128)S(1)}, u32[]{:S(2)}, u32[]{:S(2)}) collective-permute-start(f32[2,1,32,128]{3,2,1,0:T(8,128)S(1)} %get-tuple-element.104.rest_0_), channel_id=1, source_target_pairs={{0,8},{4,12},{8,0},{12,4},{1,9},{5,13},{9,1},{13,5},{2,10},{6,14},... | collective-permute-start | bytes 98312 | tf_op jit(solution)/shard_map/ppermute | solution.py:310
  109.9 6.0 %collective-permute-start.20 = (f32[2,1,32,128]{3,2,1,0:T(8,128)S(1)}, f32[2,1,32,128]{3,2,1,0:T(8,128)S(1)}, u32[]{:S(2)}, u32[]{:S(2)}) collective-permute-start(f32[2,1,32,128]{3,2,1,0:T(8,128)S(1)} %get-tuple-element.104.rest_0_), channel_id=1, source_target_pairs={{0,12},{4,0},{8,4},{12,8},{1,13},{5,1},{9,5},{13,9},{2,14},{6,2},{... | collective-permute-start | bytes 98312 | tf_op jit(solution)/shard_map/ppermute | solution.py:310

commit v4 on v3

--- a/solution.py
+++ b/solution.py
@@ -11,9 +11,9 @@
 VMEM = pltpu.MemorySpace.VMEM
 HBM = pltpu.MemorySpace.HBM
 NJ, NI, NK, NM = 4, 128, 32, 128
-HALF = NI // 2
+CUTS = ((0, 80), (80, 48))
 PLANE = (NI, NK, NM)
-HALF_PLANE = (HALF, NK, NM)
+PARTS = tuple((rows, NK, NM) for _, rows in CUTS)
 FACES = ((NJ, NK, NM),) * 2 + ((NJ, NI, NM),) * 2
 UNROLL = 8
 PIECE = 16
@@ -55,7 +55,8 @@
 
 
 def first(tracer, x3a, sems):
-    rows = [pl.ds(n, HALF // 4) for n in range(0, HALF, HALF // 4)]
+    size = CUTS[0][1] // 4
+    rows = [pl.ds(n * size, size) for n in range(4)]
     copies = [start(tracer.at[row_of(3), r], x3a.at[r], sems.at[n]) for n, r in enumerate(rows)]
     for copy in copies:
         copy.wait()
@@ -63,7 +64,7 @@
 
 def messages(tracer, x3b, x0, lon_low, lon_high, lev_low, lev_high, sems):
     pairs = [
-        (tracer.at[row_of(3), pl.ds(HALF, HALF)], x3b),
+        (tracer.at[row_of(3), pl.ds(*CUTS[1])], x3b),
         (tracer.at[row_of(0)], x0),
     ]
     for p in range(NJ):
@@ -86,7 +87,7 @@
         copy.wait()
 
 
-def advance(x, before, after, below, above, lev_low, lev_high, c, s, out, lev_outs=None, sums=None, top=False):
+def advance(rows, x, before, after, below, above, lev_low, lev_high, c, s, out, lev_outs=None, sums=None, top=False):
     def at(view, i, size=None):
         ref, first = view
         return ref[first + i] if size is None else ref[pl.ds(pl.multiple_of(first + i, UNROLL), size), :]
@@ -101,7 +102,7 @@
             if r < UNROLL - 1:
                 nxt = at(x, i0 + r + 1)
             else:
-                nxt = jnp.where(b == HALF // UNROLL - 1, after, at(x, jnp.minimum(i0 + UNROLL, HALF - 1)))
+                nxt = jnp.where(b == rows // UNROLL - 1, after, at(x, jnp.minimum(i0 + UNROLL, rows - 1)))
             down = jnp.concatenate([low[r : r + 1], here[: NK - 1]], axis=0)
             up = jnp.concatenate([here[1:], high[r : r + 1]], axis=0)
             over = at(above, i0 + r) if top is False else unless(top, at(above, i0 + r))
@@ -123,7 +124,7 @@
         first = 0
     else:
         first = (jnp.zeros((NK, NM), F32) if sums[0] is None else sums[0], sums[1])
-    return lax.fori_loop(0, HALF // UNROLL, block, first)
+    return lax.fori_loop(0, rows // UNROLL, block, first)
 
 
 def moments(q, sums):
@@ -151,12 +152,13 @@
         x, out = xs[p], outs[p]
         sums = no_sums() if stats is not None else None
         for h in (0, 1):
-            first = h * HALF
+            first, rows = CUTS[h]
             below = (on, first) if p == 0 else (xs[p - 1], first)
             above = (xs[3 + h], 0) if p == 2 else (xs[p + 1], first)
-            before = x[HALF - 1] if h else unless(at_end("lon", False), lon_low[p])
-            after = unless(at_end("lon", True), lon_high[p]) if h else x[HALF]
+            before = x[first - 1] if h else unless(at_end("lon", False), lon_low[p])
+            after = unless(at_end("lon", True), lon_high[p]) if h else x[rows]
             sums = advance(
+                rows,
                 (x, first), before, after, below, above, (lev_low.at[p], first), (lev_high.at[p], first),
                 (cs[p][0], first), (cs[p][1], first), (out, first),
                 None if faces is None else ((faces[2].at[p], first), (faces[3].at[p], first)),
@@ -172,18 +174,18 @@
 
 def edge_half(h, x2, x3, cross, halo, c3, s3, out, faces=None, sums=None):
     lon_low, lon_high, lev_low, lev_high = halo
-    p, first = 3, h * HALF
-    before = x3[0][HALF - 1] if h else unless(at_end("lon", False), lon_low[p])
+    p, (first, rows) = 3, CUTS[h]
+    before = x3[0][first - 1] if h else unless(at_end("lon", False), lon_low[p])
     after = unless(at_end("lon", True), lon_high[p]) if h else x3[1][0]
     sums = advance(
-        (x3[h], 0), before, after,
+        rows, (x3[h], 0), before, after,
         (x2, first), (cross, 0), (lev_low.at[p], first), (lev_high.at[p], first), (c3, first), (s3, first), (out, 0),
         None if faces is None else ((faces[2].at[p], first), (faces[3].at[p], first)), sums,
         jnp.logical_or(at_end("lat", False), at_end("lat", True)),
     )
     if faces is not None:
         if h:
-            faces[1][p] = out[HALF - 1]
+            faces[1][p] = out[rows - 1]
         else:
             faces[0][p] = out[0]
     return sums
@@ -203,8 +205,9 @@
 
 def edge_b_last(x2, x3a, x3b, cross, ll, lh, vl, vh, c3, s3, raw, out, stats):
     mean, square = moments(out, edge_half(1, x2, (x3a, x3b), cross, (ll, lh, vl, vh), c3, s3, out, None, no_sums()))
-    stats[0, 0] = 0.5 * (raw[0] + mean)
-    stats[1, 0] = raw[1] + square + (0.5 * HALF) * ((raw[0] - mean) * (raw[0] - mean))
+    (_, a), (_, b) = CUTS
+    stats[0, 0] = (a / NI) * raw[0] + (b / NI) * mean
+    stats[1, 0] = raw[1] + square + (a * b / NI) * ((raw[0] - mean) * (raw[0] - mean))
 
 
 def inner_first(
@@ -236,7 +239,7 @@
     outs, copies = ((q0, q1, q2), [])
 
     def done(p, h):
-        rows = pl.ds(h * HALF, HALF)
+        rows = pl.ds(*CUTS[h])
         copies.append(start(outs[p].at[rows], end.at[row_of(p), rows], sems.at[2 * p + h]))
 
     inner_planes(
@@ -269,7 +272,7 @@
 def scale_inner(parts):
     def kernel(q0, q1, q2, q3a, q3b, *rest):
         stats, (_, out, end, buffers, sems) = rest[:parts], rest[parts:]
-        copies = [start(q, end.at[row_of(3), pl.ds(h * HALF, HALF)], sems.at[3 + h]) for h, q in enumerate((q3a, q3b))]
+        copies = [start(q, end.at[row_of(3), pl.ds(*CUTS[h])], sems.at[3 + h]) for h, q in enumerate((q3a, q3b))]
         for p, q in enumerate((q0, q1, q2)):
             scale_rows(q, *scaled(parts, p, stats), buffers.at[p])
             copies.append(start(buffers.at[p], out.at[row_of(p)], sems.at[p]))
@@ -285,8 +288,8 @@
         mean, scale = scaled(parts, 0, stats)
         copies = []
         for h, q in enumerate((q3a, q3b)):
-            for first in range(0, HALF, PIECE):
-                rows = pl.ds(h * HALF + first, PIECE)
+            for first in range(0, CUTS[h][1], PIECE):
+                rows = pl.ds(CUTS[h][0] + first, PIECE)
                 scale_rows(q.at[pl.ds(first, PIECE)], mean, scale, buffer.at[rows])
                 copies.append(start(buffer.at[rows], out.at[row_of(3), rows], sems.at[len(copies)]))
         for copy in copies:
@@ -322,11 +325,11 @@
 
     vm = lambda *arrays: [(a, VMEM) for a in arrays]
     dma = pltpu.SemaphoreType.DMA
-    half, plane, face_outs = ((HALF_PLANE, VMEM), (PLANE, VMEM), [(f, VMEM) for f in FACES])
+    half, plane, face_outs = ([(shape, VMEM) for shape in PARTS], (PLANE, VMEM), [(f, VMEM) for f in FACES])
     inner_fields = ((3, *PLANE), VMEM)
 
-    (x3a,) = call(first, [(tracer, HBM)], [half], scratch=[dma((4,))])
-    x3b, x0, *faces = call(messages, [(tracer, HBM)], [half, plane] + face_outs, scratch=[dma((2 + 4 * NJ,))])
+    (x3a,) = call(first, [(tracer, HBM)], [half[0]], scratch=[dma((4,))])
+    x3b, x0, *faces = call(messages, [(tracer, HBM)], [half[1], plane] + face_outs, scratch=[dma((2 + 4 * NJ,))])
     cross = [swapped(x3a, cross_pairs), swapped(x3b, cross_pairs)]
     on = swapped(x0, on_pairs)
     halo = exchanged(faces)
@@ -336,7 +339,7 @@
         edge = vm(x2, x3a, x3b)
         rest = vm(*halo, c3, s3)
         if step < STEPS - 1:
-            qa, *faces = call(edge_a, edge + vm(cross[0]) + rest, [half] + face_outs)
+            qa, *faces = call(edge_a, edge + vm(cross[0]) + rest, [half[0]] + face_outs)
             cross[0] = swapped(qa, cross_pairs)
             outs = [plane] * 3 + face_outs
             if step == 0:
@@ -353,7 +356,7 @@
                 )
             on = swapped(q0, on_pairs)
             qb, *faces = call(
-                edge_b, edge + vm(cross[1]) + rest + vm(*faces), [half] + face_outs,
+                edge_b, edge + vm(cross[1]) + rest + vm(*faces), [half[1]] + face_outs,
                 aliases={10 + n: 1 + n for n in range(4)},
             )
             cross[1] = swapped(qb, inside_pairs)
@@ -364,8 +367,8 @@
                 [plane] * 3 + [((2, 3, NK, NM), VMEM), ((NJ, *PLANE), HBM)], scratch=[dma((6,))],
             )
             inner_stats = of_everyone(stats)
-            qa, raw = call(edge_a_last, edge + vm(cross[0]) + rest, [half, ((2, NK, NM), VMEM)])
-            qb, stats = call(edge_b_last, edge + vm(cross[1]) + rest + vm(raw), [half, ((2, 1, NK, NM), VMEM)])
+            qa, raw = call(edge_a_last, edge + vm(cross[0]) + rest, [half[0], ((2, NK, NM), VMEM)])
+            qb, stats = call(edge_b_last, edge + vm(cross[1]) + rest + vm(raw), [half[1], ((2, 1, NK, NM), VMEM)])
             edge_stats = of_everyone(stats)
         x0, x1, x2, x3a, x3b = q0, q1, q2, qa, qb
 

time: 119 us -> 127 us (1.067)
  waiting for transfers between devices: 48 us -> 56.9 us
  starting transfers between devices: 37.8 us -> 36.4 us
    ppermute x18, waiting for transfers between devices: 14.9 us -> 19.5 us  [rotated(): return lax.ppermute(array, axis, [(i, (i + by) % n) for i in range(n)])]
    ppermute x9, waiting for transfers between devices: 33.1 us -> 37.3 us  [swapped(): return lax.ppermute(q, 'lat', pairs)]
    ppermute x18, starting transfers between devices: 26.1 us -> 24.6 us  [rotated(): return lax.ppermute(array, axis, [(i, (i + by) % n) for i in range(n)])]
where the time goes in v4:
time: 127 us; the launch traced here: 125 us
  waiting for transfers between devices  56.9 us (45%)
  starting transfers between devices  36.4 us (29%)
  Pallas kernels  30.6 us (24%)
    ppermute x9, waiting for transfers between devices, swapped(): return lax.ppermute(q, 'lat', pairs)  37.3 us
    pallas_call x14, Pallas kernels, call(): pl.pallas_call(kernel, out_shape=tuple((space(shape, F32) for shape, spac...  30.6 us
    ppermute x18, starting transfers between devices, rotated(): return lax.ppermute(array, axis, [(i, (i + by) % n) for i in range(n)])  24.6 us
    ppermute x18, waiting for transfers between devices, rotated(): return lax.ppermute(array, axis, [(i, (i + by) % n) for i in range(n)])  19.5 us
    ppermute x9, starting transfers between devices, swapped(): return lax.ppermute(q, 'lat', pairs)  11.8 us
  transfers between devices with their start and end apart: 27, of which 9 were waited for; matrix products, arithmetic and copies ran while one was open for 0% of the time, Pallas kernels for 14%

profile of v4, /device:TPU:40, one launch (start us, length us, event | category | flops | bytes accessed | tf_op | source)
XLA Modules:
  0.0 124.7 jit_solution(9318139480900518)
XLA Ops:
  0.6 2.1 %shard_map.50 = (f32[48,32,128]{2,1,0:T(8,128)S(1)}, f32[128,32,128]{2,1,0:T(8,128)S(1)}, f32[4,32,128]{2,1,0:T(8,128)S(1)}, f32[4,32,128]{2,1,0:T(8,128)S(1)}, ...) custom-call(f32[4,128,32,128]{3,2,1,0:T(8,128)} %tracer.7), custom_call_target="tpu_custom_call" | custom-call | tf_op jit(solution)/shard_map/pallas_call | solution.py:27
  2.9 1.3 %shard_map.52.x3a = f32[80,32,128]{2,1,0:T(8,128)S(1)} custom-call(f32[4,128,32,128]{3,2,1,0:T(8,128)} %tracer.7), custom_call_target="tpu_custom_call" | custom-call | tf_op jit(solution)/shard_map/pallas_call | solution.py:27
  4.2 0.6 collective-permute-start.5
  4.8 1.9 %collective-permute-start.3 = (f32[4,128,128]{2,1,0:T(8,128)S(1)}, f32[4,128,128]{2,1,0:T(8,128)S(1)}, u32[]{:S(2)}, u32[]{:S(2)}) collective-permute-start(f32[4,128,128]{2,1,0:T(8,128)S(1)} %get-tuple-element.63), channel_id=1, source_target_pairs={{0,1},{1,2},{2,3},{3,0},{4,5},{5,6},{6,7},{7,4},{8,9},{9,10},{10,1... | collective-permute-start | bytes 786440 | tf_op jit(solution)/shard_map/ppermute | solution.py:313
  6.7 0.1 collective-permute-start.4
  6.8 1.5 %collective-permute-start.1 = (f32[4,32,128]{2,1,0:T(8,128)S(1)}, f32[4,32,128]{2,1,0:T(8,128)S(1)}, u32[]{:S(2)}, u32[]{:S(2)}) collective-permute-start(f32[4,32,128]{2,1,0:T(8,128)S(1)} %get-tuple-element.61), channel_id=1, source_target_pairs={{0,4},{4,8},{8,12},{12,0},{1,5},{5,9},{9,13},{13,1},{2,6},{6,10},{... | collective-permute-start | bytes 196616 | tf_op jit(solution)/shard_map/ppermute | solution.py:313
  8.3 4.5 %collective-permute-done.1.ll = f32[4,32,128]{2,1,0:T(8,128)S(1)} collective-permute-done((f32[4,32,128]{2,1,0:T(8,128)S(1)}, f32[4,32,128]{2,1,0:T(8,128)S(1)}, u32[]{:S(2)}, u32[]{:S(2)}) %collective-permute-start.1) | collective-permute-done | bytes 65568 | tf_op jit(solution)/shard_map/ppermute | solution.py:313
  12.8 1.5 %collective-permute-start.2 = (f32[4,32,128]{2,1,0:T(8,128)S(1)}, f32[4,32,128]{2,1,0:T(8,128)S(1)}, u32[]{:S(2)}, u32[]{:S(2)}) collective-permute-start(f32[4,32,128]{2,1,0:T(8,128)S(1)} %get-tuple-element.62), channel_id=1, source_target_pairs={{0,12},{4,0},{8,4},{12,8},{1,13},{5,1},{9,5},{13,9},{2,14},{6,2},{... | collective-permute-start | bytes 196616 | tf_op jit(solution)/shard_map/ppermute | solution.py:313
  14.4 2.9 %shard_map.51 = (f32[128,32,128]{2,1,0:T(8,128)S(1)}, f32[128,32,128]{2,1,0:T(8,128)S(1)}, f32[128,32,128]{2,1,0:T(8,128)S(1)}) custom-call(f32[4,128,32,128]{3,2,1,0:T(8,128)} %tracer.7, f32[4,128,32,128]{3,2,1,0:T(8,128)} %c.3, f32[4,128,32,128]{3,2,1,0:T(8,128)} %s.3), custom_call_target="tpu_custom_call" | custom-call | tf_op jit(solution)/shard_map/pallas_call | solution.py:27
  17.3 4.0 %collective-permute-done.5.cross = f32[80,32,128]{2,1,0:T(8,128)S(1)} collective-permute-done((f32[80,32,128]{2,1,0:T(8,128)S(1)}, f32[80,32,128]{2,1,0:T(8,128)S(1)}, u32[]{:S(2)}, u32[]{:S(2)}) %collective-permute-start.5) | collective-permute-done | bytes 1310752 | tf_op jit(solution)/shard_map/ppermute | solution.py:324
  21.3 0.7 shard_map.53
  22.0 6.5 %shard_map.54 = (f32[128,32,128]{2,1,0:T(8,128)S(1)}, f32[128,32,128]{2,1,0:T(8,128)S(1)}, f32[128,32,128]{2,1,0:T(8,128)S(1)}, f32[4,32,128]{2,1,0:T(8,128)S(1)...) custom-call(f32[4,128,32,128]{3,2,1,0:T(8,128)} %tracer.7, ...), custom_call_target="tpu_custom_call", output_to_operand_aliasing={{3}: (12, {}), {4}: (13, {}), {5}: (14, {}), {6}: (15, {})} | custom-call | tf_op jit(solution)/shard_map/pallas_call | solution.py:27
  28.5 0.6 collective-permute-start.7
  29.1 1.4 %collective-permute-start.12 = (f32[80,32,128]{2,1,0:T(8,128)S(1)}, f32[80,32,128]{2,1,0:T(8,128)S(1)}, u32[]{:S(2)}, u32[]{:S(2)}) collective-permute-start(f32[80,32,128]{2,1,0:T(8,128)S(1)} %get-tuple-element.74.x3a), channel_id=1, source_target_pairs={{0,112},{16,32},{32,16},{48,64},{64,48},{80,96},{96,80},{112,0},{1... | collective-permute-start | bytes 3932168 | tf_op jit(solution)/shard_map/ppermute | solution.py:324
  30.5 0.3 collective-permute-start.6
  30.8 23.7 %collective-permute-done.6.cross = f32[48,32,128]{2,1,0:T(8,128)S(1)} collective-permute-done((f32[48,32,128]{2,1,0:T(8,128)S(1)}, f32[48,32,128]{2,1,0:T(8,128)S(1)}, u32[]{:S(2)}, u32[]{:S(2)}) %collective-permute-start.6) | collective-permute-done | bytes 786464 | tf_op jit(solution)/shard_map/ppermute | solution.py:324
  54.6 0.4 shard_map.55
  55.0 2.0 %collective-permute-start.10 = (f32[4,128,128]{2,1,0:T(8,128)S(1)}, f32[4,128,128]{2,1,0:T(8,128)S(1)}, u32[]{:S(2)}, u32[]{:S(2)}) collective-permute-start(f32[4,128,128]{2,1,0:T(8,128)S(1)} %get-tuple-element.82), channel_id=1, source_target_pairs={{0,1},{1,2},{2,3},{3,0},{4,5},{5,6},{6,7},{7,4},{8,9},{9,10},{10,1... | collective-permute-start | bytes 786440 | tf_op jit(solution)/shard_map/ppermute | solution.py:313
  57.0 0.1 collective-permute-start.11
  57.1 1.5 %collective-permute-start.8 = (f32[4,32,128]{2,1,0:T(8,128)S(1)}, f32[4,32,128]{2,1,0:T(8,128)S(1)}, u32[]{:S(2)}, u32[]{:S(2)}) collective-permute-start(f32[4,32,128]{2,1,0:T(8,128)S(1)} %get-tuple-element.80), channel_id=1, source_target_pairs={{0,4},{4,8},{8,12},{12,0},{1,5},{5,9},{9,13},{13,1},{2,6},{6,10},{... | collective-permute-start | bytes 196616 | tf_op jit(solution)/shard_map/ppermute | solution.py:313
  58.6 4.0 %collective-permute-done.8.ll = f32[4,32,128]{2,1,0:T(8,128)S(1)} collective-permute-done((f32[4,32,128]{2,1,0:T(8,128)S(1)}, f32[4,32,128]{2,1,0:T(8,128)S(1)}, u32[]{:S(2)}, u32[]{:S(2)}) %collective-permute-start.8) | collective-permute-done | bytes 65568 | tf_op jit(solution)/shard_map/ppermute | solution.py:313
  62.6 1.5 %collective-permute-start.9 = (f32[4,32,128]{2,1,0:T(8,128)S(1)}, f32[4,32,128]{2,1,0:T(8,128)S(1)}, u32[]{:S(2)}, u32[]{:S(2)}) collective-permute-start(f32[4,32,128]{2,1,0:T(8,128)S(1)} %get-tuple-element.81), channel_id=1, source_target_pairs={{0,12},{4,0},{8,4},{12,8},{1,13},{5,1},{9,5},{13,9},{2,14},{6,2},{... | collective-permute-start | bytes 196616 | tf_op jit(solution)/shard_map/ppermute | solution.py:313
  64.1 2.7 %collective-permute-done.9.lh = f32[4,32,128]{2,1,0:T(8,128)S(1)} collective-permute-done((f32[4,32,128]{2,1,0:T(8,128)S(1)}, f32[4,32,128]{2,1,0:T(8,128)S(1)}, u32[]{:S(2)}, u32[]{:S(2)}) %collective-permute-start.9) | collective-permute-done | bytes 65568 | tf_op jit(solution)/shard_map/ppermute | solution.py:313
  66.9 0.7 shard_map.56
  67.6 3.5 %shard_map.57 = (f32[128,32,128]{2,1,0:T(8,128)S(1)}, f32[128,32,128]{2,1,0:T(8,128)S(1)}, f32[128,32,128]{2,1,0:T(8,128)S(1)}, f32[4,32,128]{2,1,0:T(8,128)S(1)...) custom-call(f32[128,32,128]{2,1,0:T(8,128)S(1)} %get-tuple-element.7, ...), custom_call_target="tpu_custom_call", output_to_operand_aliasing={{3}: (12, {}), {4}: (13, {}), {5}: (14, {}), {6}: (15, {})} | custom-call | tf_op jit(solution)/shard_map/pallas_call | solution.py:27
  71.1 0.1 collective-permute-start.23
  71.2 4.6 %collective-permute-start.13 = (f32[48,32,128]{2,1,0:T(8,128)S(1)}, f32[48,32,128]{2,1,0:T(8,128)S(1)}, u32[]{:S(2)}, u32[]{:S(2)}) collective-permute-start(f32[48,32,128]{2,1,0:T(8,128)S(1)} %get-tuple-element.79.x3b), channel_id=1, source_target_pairs={{16,32},{32,16},{48,64},{64,48},{80,96},{96,80},{17,33},{33,17},{4... | collective-permute-start | bytes 2359304 | tf_op jit(solution)/shard_map/ppermute | solution.py:324
  75.9 0.1 collective-permute-start.14
  76.0 9.6 %collective-permute-done.13.cross = f32[48,32,128]{2,1,0:T(8,128)S(1)} collective-permute-done((f32[48,32,128]{2,1,0:T(8,128)S(1)}, f32[48,32,128]{2,1,0:T(8,128)S(1)}, u32[]{:S(2)}, u32[]{:S(2)}) %collective-permute-start.13) | collective-permute-done | bytes 786464 | tf_op jit(solution)/shard_map/ppermute | solution.py:324
  85.5 0.4 shard_map.58
  86.0 3.9 %collective-permute-start.19 = (f32[48,32,128]{2,1,0:T(8,128)S(1)}, f32[48,32,128]{2,1,0:T(8,128)S(1)}, u32[]{:S(2)}, u32[]{:S(2)}) collective-permute-start(f32[48,32,128]{2,1,0:T(8,128)S(1)} %get-tuple-element.96.x3b), channel_id=1, source_target_pairs={{16,32},{32,16},{48,64},{64,48},{80,96},{96,80},{17,33},{33,17},{4... | collective-permute-start | bytes 2359304 | tf_op jit(solution)/shard_map/ppermute | solution.py:324
  89.9 0.3 collective-permute-start.15
  90.3 3.0 %collective-permute-start.16 = (f32[4,32,128]{2,1,0:T(8,128)S(1)}, f32[4,32,128]{2,1,0:T(8,128)S(1)}, u32[]{:S(2)}, u32[]{:S(2)}) collective-permute-start(f32[4,32,128]{2,1,0:T(8,128)S(1)} %get-tuple-element.98), channel_id=1, source_target_pairs={{0,12},{4,0},{8,4},{12,8},{1,13},{5,1},{9,5},{13,9},{2,14},{6,2},{... | collective-permute-start | bytes 196616 | tf_op jit(solution)/shard_map/ppermute | solution.py:313
  93.2 2.2 %collective-permute-done.15.ll = f32[4,32,128]{2,1,0:T(8,128)S(1)} collective-permute-done((f32[4,32,128]{2,1,0:T(8,128)S(1)}, f32[4,32,128]{2,1,0:T(8,128)S(1)}, u32[]{:S(2)}, u32[]{:S(2)}) %collective-permute-start.15) | collective-permute-done | bytes 65568 | tf_op jit(solution)/shard_map/ppermute | solution.py:313
  95.5 1.9 %collective-permute-start.17 = (f32[4,128,128]{2,1,0:T(8,128)S(1)}, f32[4,128,128]{2,1,0:T(8,128)S(1)}, u32[]{:S(2)}, u32[]{:S(2)}) collective-permute-start(f32[4,128,128]{2,1,0:T(8,128)S(1)} %get-tuple-element.99), channel_id=1, source_target_pairs={{0,1},{1,2},{2,3},{3,0},{4,5},{5,6},{6,7},{7,4},{8,9},{9,10},{10,1... | collective-permute-start | bytes 786440 | tf_op jit(solution)/shard_map/ppermute | solution.py:313
  97.4 0.3 collective-permute-start.18
  97.7 4.3 %collective-permute-done.17.vl = f32[4,128,128]{2,1,0:T(8,128)S(1)} collective-permute-done((f32[4,128,128]{2,1,0:T(8,128)S(1)}, f32[4,128,128]{2,1,0:T(8,128)S(1)}, u32[]{:S(2)}, u32[]{:S(2)}) %collective-permute-start.17) | collective-permute-done | bytes 262176 | tf_op jit(solution)/shard_map/ppermute | solution.py:313
  102.0 1.7 %collective-permute-done.18.vh = f32[4,128,128]{2,1,0:T(8,128)S(1)} collective-permute-done((f32[4,128,128]{2,1,0:T(8,128)S(1)}, f32[4,128,128]{2,1,0:T(8,128)S(1)}, u32[]{:S(2)}, u32[]{:S(2)}) %collective-permute-start.18) | collective-permute-done | bytes 262176 | tf_op jit(solution)/shard_map/ppermute | solution.py:313
  103.8 5.4 %shard_map.61 = (f32[128,32,128]{2,1,0:T(8,128)S(1)}, f32[128,32,128]{2,1,0:T(8,128)S(1)}, f32[128,32,128]{2,1,0:T(8,128)S(1)}, f32[2,3,32,128]{3,2,1,0:T(8,128)S(1)}, f32[4,128,32,128]{3,2,1,0:T(8,128)}) custom-call(f32[128,32,128]{2,1,0:T(8,128)S(1)} %get-tuple-element.105.x0, f32[128,32,128]{2,1,0:T(8,128)S(1)} %get-tuple-element.106.x1, ...), custom_call_target="tpu_custom_call" | custom-call | tf_op jit(solution)/shard_map/pallas_call | solution.py:27
  109.3 3.0 %collective-permute-start.25 = (f32[2,3,32,128]{3,2,1,0:T(8,128)S(1)}, f32[2,3,32,128]{3,2,1,0:T(8,128)S(1)}, u32[]{:S(2)}, u32[]{:S(2)}) collective-permute-start(f32[2,3,32,128]{3,2,1,0:T(8,128)S(1)} %get-tuple-element.110.rest_0_), channel_id=1, source_target_pairs={{0,8},{4,12},{8,0},{12,4},{1,9},{5,13},{9,1},{13,5},{2,10},{6,14},... | collective-permute-start | bytes 294920 | tf_op jit(solution)/shard_map/ppermute | solution.py:313
  112.3 0.7 collective-permute-start.24
  113.0 1.0 shard_map.59
  114.0 0.6 shard_map.60
  114.6 1.4 %collective-permute-start.22 = (f32[2,1,32,128]{3,2,1,0:T(8,128)S(1)}, f32[2,1,32,128]{3,2,1,0:T(8,128)S(1)}, u32[]{:S(2)}, u32[]{:S(2)}) collective-permute-start(f32[2,1,32,128]{3,2,1,0:T(8,128)S(1)} %get-tuple-element.104.rest_0_), channel_id=1, source_target_pairs={{0,4},{4,8},{8,12},{12,0},{1,5},{5,9},{9,13},{13,1},{2,6},{6,10},{... | collective-permute-start | bytes 98312 | tf_op jit(solution)/shard_map/ppermute | solution.py:313
  116.0 1.2 collective-permute-start.21
  117.2 2.5 %collective-permute-start.20 = (f32[2,1,32,128]{3,2,1,0:T(8,128)S(1)}, f32[2,1,32,128]{3,2,1,0:T(8,128)S(1)}, u32[]{:S(2)}, u32[]{:S(2)}) collective-permute-start(f32[2,1,32,128]{3,2,1,0:T(8,128)S(1)} %get-tuple-element.104.rest_0_), channel_id=1, source_target_pairs={{0,12},{4,0},{8,4},{12,8},{1,13},{5,1},{9,5},{13,9},{2,14},{6,2},{... | collective-permute-start | bytes 98312 | tf_op jit(solution)/shard_map/ppermute | solution.py:313
  119.8 3.4 %shard_map.62 = (f32[4,128,32,128]{3,2,1,0:T(8,128)}, f32[4,128,32,128]{3,2,1,0:T(8,128)}) custom-call(f32[128,32,128]{2,1,0:T(8,128)S(1)} %get-tuple-element.107.q0, f32[128,32,128]{2,1,0:T(8,128)S(1)} %get-tuple-element.108.q1, f32[128,32,128]{2,1,0:T(8,128)S(1)} %get-tuple-element.109.q2, ...), custom_call_target="tpu_custom_call", output_to_operand_aliasing={{1}: (9, {})} | custom-call | tf_op jit(solution)/shard_map/pallas_call | solution.py:27
  123.2 1.4 %shard_map.63 = f32[4,128,32,128]{3,2,1,0:T(8,128)} custom-call(f32[80,32,128]{2,1,0:T(8,128)S(1)} %get-tuple-element.101.q3a, f32[48,32,128]{2,1,0:T(8,128)S(1)} %get-tuple-element.103.q3b, f32[2,1,32,128]{3,2,1,0:T(8,128)S(1)} %get-tuple-element.104.rest_0_, f32[2,1,32,128]{3,2,1,0:T(8,128)S(1)} %collective-permute-done.20.rest_1_, ...), custom_call_target="tpu_custom_call", output_to_operand_aliasing={{}: (6, {})} | custom-call | tf_op jit(solution)/shard_map/pallas_call | solution.py:27
  (20 shorter events, 0.2 us)
Async XLA Ops:
  2.8 19.3 %collective-permute-start = (f32[128,32,128]{2,1,0:T(8,128)S(1)}, f32[128,32,128]{2,1,0:T(8,128)S(1)}, u32[]{:S(2)}, u32[]{:S(2)}) collective-permute-start(f32[128,32,128]{2,1,0:T(8,128)S(1)} %get-tuple-element.58.x0), channel_id=1, source_target_pairs={{0,16},{16,0},{32,48},{48,32},{64,80},{80,64},{96,112},{112,96},{1... | collective-permute-start | bytes 6291464 | tf_op jit(solution)/shard_map/ppermute | solution.py:324
  4.2 17.1 %collective-permute-start.5 = (f32[80,32,128]{2,1,0:T(8,128)S(1)}, f32[80,32,128]{2,1,0:T(8,128)S(1)}, u32[]{:S(2)}, u32[]{:S(2)}) collective-permute-start(f32[80,32,128]{2,1,0:T(8,128)S(1)} %shard_map.52.x3a), channel_id=1, source_target_pairs={{0,112},{16,32},{32,16},{48,64},{64,48},{80,96},{96,80},{112,0},{1... | collective-permute-start | bytes 3932168 | tf_op jit(solution)/shard_map/ppermute | solution.py:324
  4.8 12.5 %collective-permute-start.3 = (f32[4,128,128]{2,1,0:T(8,128)S(1)}, f32[4,128,128]{2,1,0:T(8,128)S(1)}, u32[]{:S(2)}, u32[]{:S(2)}) collective-permute-start(f32[4,128,128]{2,1,0:T(8,128)S(1)} %get-tuple-element.63), channel_id=1, source_target_pairs={{0,1},{1,2},{2,3},{3,0},{4,5},{5,6},{6,7},{7,4},{8,9},{9,10},{10,1... | collective-permute-start | bytes 786440 | tf_op jit(solution)/shard_map/ppermute | solution.py:313
  6.7 10.6 %collective-permute-start.4 = (f32[4,128,128]{2,1,0:T(8,128)S(1)}, f32[4,128,128]{2,1,0:T(8,128)S(1)}, u32[]{:S(2)}, u32[]{:S(2)}) collective-permute-start(f32[4,128,128]{2,1,0:T(8,128)S(1)} %get-tuple-element.64), channel_id=1, source_target_pairs={{0,3},{1,0},{2,1},{3,2},{4,7},{5,4},{6,5},{7,6},{8,11},{9,8},{10,9... | collective-permute-start | bytes 786440 | tf_op jit(solution)/shard_map/ppermute | solution.py:313
  6.8 6.0 %collective-permute-start.1 = (f32[4,32,128]{2,1,0:T(8,128)S(1)}, f32[4,32,128]{2,1,0:T(8,128)S(1)}, u32[]{:S(2)}, u32[]{:S(2)}) collective-permute-start(f32[4,32,128]{2,1,0:T(8,128)S(1)} %get-tuple-element.61), channel_id=1, source_target_pairs={{0,4},{4,8},{8,12},{12,0},{1,5},{5,9},{9,13},{13,1},{2,6},{6,10},{... | collective-permute-start | bytes 196616 | tf_op jit(solution)/shard_map/ppermute | solution.py:313
  12.8 4.4 %collective-permute-start.2 = (f32[4,32,128]{2,1,0:T(8,128)S(1)}, f32[4,32,128]{2,1,0:T(8,128)S(1)}, u32[]{:S(2)}, u32[]{:S(2)}) collective-permute-start(f32[4,32,128]{2,1,0:T(8,128)S(1)} %get-tuple-element.62), channel_id=1, source_target_pairs={{0,12},{4,0},{8,4},{12,8},{1,13},{5,1},{9,5},{13,9},{2,14},{6,2},{... | collective-permute-start | bytes 196616 | tf_op jit(solution)/shard_map/ppermute | solution.py:313
  28.5 39.1 %collective-permute-start.7 = (f32[128,32,128]{2,1,0:T(8,128)S(1)}, f32[128,32,128]{2,1,0:T(8,128)S(1)}, u32[]{:S(2)}, u32[]{:S(2)}) collective-permute-start(f32[128,32,128]{2,1,0:T(8,128)S(1)} %get-tuple-element.71.x0), channel_id=1, source_target_pairs={{0,16},{16,0},{32,48},{48,32},{64,80},{80,64},{96,112},{112,96},{1... | collective-permute-start | bytes 6291464 | tf_op jit(solution)/shard_map/ppermute | solution.py:324
  29.1 37.8 %collective-permute-start.12 = (f32[80,32,128]{2,1,0:T(8,128)S(1)}, f32[80,32,128]{2,1,0:T(8,128)S(1)}, u32[]{:S(2)}, u32[]{:S(2)}) collective-permute-start(f32[80,32,128]{2,1,0:T(8,128)S(1)} %get-tuple-element.74.x3a), channel_id=1, source_target_pairs={{0,112},{16,32},{32,16},{48,64},{64,48},{80,96},{96,80},{112,0},{1... | collective-permute-start | bytes 3932168 | tf_op jit(solution)/shard_map/ppermute | solution.py:324
  30.5 24.0 %collective-permute-start.6 = (f32[48,32,128]{2,1,0:T(8,128)S(1)}, f32[48,32,128]{2,1,0:T(8,128)S(1)}, u32[]{:S(2)}, u32[]{:S(2)}) collective-permute-start(f32[48,32,128]{2,1,0:T(8,128)S(1)} %get-tuple-element.60.x3b), channel_id=1, source_target_pairs={{0,112},{16,32},{32,16},{48,64},{64,48},{80,96},{96,80},{112,0},{1... | collective-permute-start | bytes 2359304 | tf_op jit(solution)/shard_map/ppermute | solution.py:324
  55.0 11.8 %collective-permute-start.10 = (f32[4,128,128]{2,1,0:T(8,128)S(1)}, f32[4,128,128]{2,1,0:T(8,128)S(1)}, u32[]{:S(2)}, u32[]{:S(2)}) collective-permute-start(f32[4,128,128]{2,1,0:T(8,128)S(1)} %get-tuple-element.82), channel_id=1, source_target_pairs={{0,1},{1,2},{2,3},{3,0},{4,5},{5,6},{6,7},{7,4},{8,9},{9,10},{10,1... | collective-permute-start | bytes 786440 | tf_op jit(solution)/shard_map/ppermute | solution.py:313
  57.0 9.9 %collective-permute-start.11 = (f32[4,128,128]{2,1,0:T(8,128)S(1)}, f32[4,128,128]{2,1,0:T(8,128)S(1)}, u32[]{:S(2)}, u32[]{:S(2)}) collective-permute-start(f32[4,128,128]{2,1,0:T(8,128)S(1)} %get-tuple-element.83), channel_id=1, source_target_pairs={{0,3},{1,0},{2,1},{3,2},{4,7},{5,4},{6,5},{7,6},{8,11},{9,8},{10,9... | collective-permute-start | bytes 786440 | tf_op jit(solution)/shard_map/ppermute | solution.py:313
  57.1 5.5 %collective-permute-start.8 = (f32[4,32,128]{2,1,0:T(8,128)S(1)}, f32[4,32,128]{2,1,0:T(8,128)S(1)}, u32[]{:S(2)}, u32[]{:S(2)}) collective-permute-start(f32[4,32,128]{2,1,0:T(8,128)S(1)} %get-tuple-element.80), channel_id=1, source_target_pairs={{0,4},{4,8},{8,12},{12,0},{1,5},{5,9},{9,13},{13,1},{2,6},{6,10},{... | collective-permute-start | bytes 196616 | tf_op jit(solution)/shard_map/ppermute | solution.py:313
  62.6 4.3 %collective-permute-start.9 = (f32[4,32,128]{2,1,0:T(8,128)S(1)}, f32[4,32,128]{2,1,0:T(8,128)S(1)}, u32[]{:S(2)}, u32[]{:S(2)}) collective-permute-start(f32[4,32,128]{2,1,0:T(8,128)S(1)} %get-tuple-element.81), channel_id=1, source_target_pairs={{0,12},{4,0},{8,4},{12,8},{1,13},{5,1},{9,5},{13,9},{2,14},{6,2},{... | collective-permute-start | bytes 196616 | tf_op jit(solution)/shard_map/ppermute | solution.py:313
  71.1 32.6 %collective-permute-start.23 = (f32[128,32,128]{2,1,0:T(8,128)S(1)}, f32[128,32,128]{2,1,0:T(8,128)S(1)}, u32[]{:S(2)}, u32[]{:S(2)}) collective-permute-start(f32[128,32,128]{2,1,0:T(8,128)S(1)} %get-tuple-element.105.x0), channel_id=1, source_target_pairs={{0,16},{16,0},{32,48},{48,32},{64,80},{80,64},{96,112},{112,96},{1... | collective-permute-start | bytes 6291464 | tf_op jit(solution)/shard_map/ppermute | solution.py:324
  71.2 14.3 %collective-permute-start.13 = (f32[48,32,128]{2,1,0:T(8,128)S(1)}, f32[48,32,128]{2,1,0:T(8,128)S(1)}, u32[]{:S(2)}, u32[]{:S(2)}) collective-permute-start(f32[48,32,128]{2,1,0:T(8,128)S(1)} %get-tuple-element.79.x3b), channel_id=1, source_target_pairs={{16,32},{32,16},{48,64},{64,48},{80,96},{96,80},{17,33},{33,17},{4... | collective-permute-start | bytes 2359304 | tf_op jit(solution)/shard_map/ppermute | solution.py:324
  75.9 37.1 %collective-permute-start.14 = (f32[80,32,128]{2,1,0:T(8,128)S(1)}, f32[80,32,128]{2,1,0:T(8,128)S(1)}, u32[]{:S(2)}, u32[]{:S(2)}) collective-permute-start(f32[80,32,128]{2,1,0:T(8,128)S(1)} %get-tuple-element.91.x3a), channel_id=1, source_target_pairs={{0,112},{16,32},{32,16},{48,64},{64,48},{80,96},{96,80},{112,0},{1... | collective-permute-start | bytes 3932168 | tf_op jit(solution)/shard_map/ppermute | solution.py:324
  86.0 28.0 %collective-permute-start.19 = (f32[48,32,128]{2,1,0:T(8,128)S(1)}, f32[48,32,128]{2,1,0:T(8,128)S(1)}, u32[]{:S(2)}, u32[]{:S(2)}) collective-permute-start(f32[48,32,128]{2,1,0:T(8,128)S(1)} %get-tuple-element.96.x3b), channel_id=1, source_target_pairs={{16,32},{32,16},{48,64},{64,48},{80,96},{96,80},{17,33},{33,17},{4... | collective-permute-start | bytes 2359304 | tf_op jit(solution)/shard_map/ppermute | solution.py:324
  89.9 5.5 %collective-permute-start.15 = (f32[4,32,128]{2,1,0:T(8,128)S(1)}, f32[4,32,128]{2,1,0:T(8,128)S(1)}, u32[]{:S(2)}, u32[]{:S(2)}) collective-permute-start(f32[4,32,128]{2,1,0:T(8,128)S(1)} %get-tuple-element.97), channel_id=1, source_target_pairs={{0,4},{4,8},{8,12},{12,0},{1,5},{5,9},{9,13},{13,1},{2,6},{6,10},{... | collective-permute-start | bytes 196616 | tf_op jit(solution)/shard_map/ppermute | solution.py:313
  90.3 7.1 %collective-permute-start.16 = (f32[4,32,128]{2,1,0:T(8,128)S(1)}, f32[4,32,128]{2,1,0:T(8,128)S(1)}, u32[]{:S(2)}, u32[]{:S(2)}) collective-permute-start(f32[4,32,128]{2,1,0:T(8,128)S(1)} %get-tuple-element.98), channel_id=1, source_target_pairs={{0,12},{4,0},{8,4},{12,8},{1,13},{5,1},{9,5},{13,9},{2,14},{6,2},{... | collective-permute-start | bytes 196616 | tf_op jit(solution)/shard_map/ppermute | solution.py:313
  95.5 6.5 %collective-permute-start.17 = (f32[4,128,128]{2,1,0:T(8,128)S(1)}, f32[4,128,128]{2,1,0:T(8,128)S(1)}, u32[]{:S(2)}, u32[]{:S(2)}) collective-permute-start(f32[4,128,128]{2,1,0:T(8,128)S(1)} %get-tuple-element.99), channel_id=1, source_target_pairs={{0,1},{1,2},{2,3},{3,0},{4,5},{5,6},{6,7},{7,4},{8,9},{9,10},{10,1... | collective-permute-start | bytes 786440 | tf_op jit(solution)/shard_map/ppermute | solution.py:313
  97.4 6.4 %collective-permute-start.18 = (f32[4,128,128]{2,1,0:T(8,128)S(1)}, f32[4,128,128]{2,1,0:T(8,128)S(1)}, u32[]{:S(2)}, u32[]{:S(2)}) collective-permute-start(f32[4,128,128]{2,1,0:T(8,128)S(1)} %get-tuple-element.100), channel_id=1, source_target_pairs={{0,3},{1,0},{2,1},{3,2},{4,7},{5,4},{6,5},{7,6},{8,11},{9,8},{10,9... | collective-permute-start | bytes 786440 | tf_op jit(solution)/shard_map/ppermute | solution.py:313
  109.2 8.0 %collective-permute-start.26 = (f32[2,3,32,128]{3,2,1,0:T(8,128)S(1)}, f32[2,3,32,128]{3,2,1,0:T(8,128)S(1)}, u32[]{:S(2)}, u32[]{:S(2)}) collective-permute-start(f32[2,3,32,128]{3,2,1,0:T(8,128)S(1)} %get-tuple-element.110.rest_0_), channel_id=1, source_target_pairs={{0,4},{4,8},{8,12},{12,0},{1,5},{5,9},{9,13},{13,1},{2,6},{6,10},{... | collective-permute-start | bytes 294920 | tf_op jit(solution)/shard_map/ppermute | solution.py:313
  109.3 10.5 %collective-permute-start.25 = (f32[2,3,32,128]{3,2,1,0:T(8,128)S(1)}, f32[2,3,32,128]{3,2,1,0:T(8,128)S(1)}, u32[]{:S(2)}, u32[]{:S(2)}) collective-permute-start(f32[2,3,32,128]{3,2,1,0:T(8,128)S(1)} %get-tuple-element.110.rest_0_), channel_id=1, source_target_pairs={{0,8},{4,12},{8,0},{12,4},{1,9},{5,13},{9,1},{13,5},{2,10},{6,14},... | collective-permute-start | bytes 294920 | tf_op jit(solution)/shard_map/ppermute | solution.py:313
  112.3 7.5 %collective-permute-start.24 = (f32[2,3,32,128]{3,2,1,0:T(8,128)S(1)}, f32[2,3,32,128]{3,2,1,0:T(8,128)S(1)}, u32[]{:S(2)}, u32[]{:S(2)}) collective-permute-start(f32[2,3,32,128]{3,2,1,0:T(8,128)S(1)} %get-tuple-element.110.rest_0_), channel_id=1, source_target_pairs={{0,12},{4,0},{8,4},{12,8},{1,13},{5,1},{9,5},{13,9},{2,14},{6,2},{... | collective-permute-start | bytes 294920 | tf_op jit(solution)/shard_map/ppermute | solution.py:313
  114.6 8.6 %collective-permute-start.22 = (f32[2,1,32,128]{3,2,1,0:T(8,128)S(1)}, f32[2,1,32,128]{3,2,1,0:T(8,128)S(1)}, u32[]{:S(2)}, u32[]{:S(2)}) collective-permute-start(f32[2,1,32,128]{3,2,1,0:T(8,128)S(1)} %get-tuple-element.104.rest_0_), channel_id=1, source_target_pairs={{0,4},{4,8},{8,12},{12,0},{1,5},{5,9},{9,13},{13,1},{2,6},{6,10},{... | collective-permute-start | bytes 98312 | tf_op jit(solution)/shard_map/ppermute | solution.py:313
  116.0 7.2 %collective-permute-start.21 = (f32[2,1,32,128]{3,2,1,0:T(8,128)S(1)}, f32[2,1,32,128]{3,2,1,0:T(8,128)S(1)}, u32[]{:S(2)}, u32[]{:S(2)}) collective-permute-start(f32[2,1,32,128]{3,2,1,0:T(8,128)S(1)} %get-tuple-element.104.rest_0_), channel_id=1, source_target_pairs={{0,8},{4,12},{8,0},{12,4},{1,9},{5,13},{9,1},{13,5},{2,10},{6,14},... | collective-permute-start | bytes 98312 | tf_op jit(solution)/shard_map/ppermute | solution.py:313
  117.2 6.0 %collective-permute-start.20 = (f32[2,1,32,128]{3,2,1,0:T(8,128)S(1)}, f32[2,1,32,128]{3,2,1,0:T(8,128)S(1)}, u32[]{:S(2)}, u32[]{:S(2)}) collective-permute-start(f32[2,1,32,128]{3,2,1,0:T(8,128)S(1)} %get-tuple-element.104.rest_0_), channel_id=1, source_target_pairs={{0,12},{4,0},{8,4},{12,8},{1,13},{5,1},{9,5},{13,9},{2,14},{6,2},{... | collective-permute-start | bytes 98312 | tf_op jit(solution)/shard_map/ppermute | solution.py:313
